TPU v7x, 128 devices: a whole 4x4x4 slice. The times are simulated.
128 devices in a mesh: expert: 4 (over x), shard: 32 (over z, y, core).
Axes of the slice: x: 4, y: 4, z: 4, core: 2. Of those that a mesh axis runs over, the one named last changes fastest.
Arguments:
- hidden: bfloat16 [256, 4096], P('shard'), may hold values from -6 to 6
- queries: bfloat16 [256, 32, 128], P('shard', 'expert'), may hold values from -30 to 30
- key_cache: bfloat16 [256, 512, 8, 128], P('shard', None, 'expert'), may hold values from -16 to 16
- value_cache: bfloat16 [256, 512, 8, 128], P('shard', None, 'expert'), may hold values from -6 to 6
- out_weight: bfloat16 [4096, 4096], P('expert', 'shard'), may hold values from -0.09375 to 0.09375
- norm_gain: bfloat16 [4096], replicated, may hold values from 0.099609375 to 1.8984375
- router: bfloat16 [4096, 8], replicated, may hold values from -0.09375 to 0.09375
- expert_ids: int32 [256, 2], replicated, may hold values from 0 to 7, all different within a row; in each aligned block of 256 rows (0 to 255, 256 to 511, ...) at most 128 rows name the same one
- gate_weight: bfloat16 [8, 4096, 14336], P('expert', None, 'shard'), may hold values from -0.09375 to 0.09375
- up_weight: bfloat16 [8, 4096, 14336], P('expert', None, 'shard'), may hold values from -0.09375 to 0.09375
- down_weight: bfloat16 [8, 14336, 4096], P('expert', 'shard'), may hold values from -0.046875 to 0.046875
Outputs:
- layer_out: bfloat16 [256, 4096], P('shard')
Inputs may be any that keep to these rules, and one draw needn't show every extreme that they name: `expert_ids`: each token names two different experts; over all 256 tokens no expert is named by more than 128 tokens, a bound that some block reaches.
All inputs are finite; a program needn't handle non-finite values.
Results may differ from a plain program's by a relative error of at most 0.008.
Values may be sent and summed in bfloat16 or wider, within the bound.
No kernel may reach another device: no remote copies, remote signals or barrier semaphores. Data moves between devices by JAX's collectives and lax.ppermute only.
A program may use at most 128 MiB of HBM per device.

v0:
```python
import math

import jax
import jax.numpy as jnp
from jax import lax
from jax.sharding import Mesh
from jax.sharding import PartitionSpec as P

SHARD = ("shard_0", "shard_1", "shard_2")


def laid_out(pieces, dim):
    pieces = jnp.moveaxis(pieces, 0, dim)
    shape = pieces.shape
    return pieces.reshape(*shape[:dim], shape[dim] * shape[dim + 1], *shape[dim + 2 :])


def copy_for_each(shard, axis):
    size = lax.axis_size(axis)
    return lax.all_to_all(
        jnp.broadcast_to(shard[None], (size, *shard.shape)), axis, 0, 0, tiled=True
    )


def gathered_copies(shard, axis, dim):
    return laid_out(copy_for_each(shard, axis), dim)


def taken_together(shard, axis):
    everything = copy_for_each(shard, axis)
    return jnp.sum(everything, axis=0)


def whole_of(shard, axes, dim):
    far, near = axes
    pieces = copy_for_each(copy_for_each(shard, far), near)
    return laid_out(pieces.swapaxes(0, 1).reshape(-1, *shard.shape), dim)


def cut_along(shard, dim, size):
    shape = shard.shape
    pieces = shard.reshape(*shape[:dim], size, shape[dim] // size, *shape[dim + 1 :])
    return jnp.moveaxis(pieces, dim, 0)


def summed_on_arrival(shard, axis, dim):
    pieces = cut_along(shard, dim, lax.axis_size(axis))
    arrived = lax.all_to_all(pieces, axis, split_axis=0, concat_axis=0, tiled=True)
    return arrived.sum(axis=0)


def sum_in_two_steps(shard, axes, dim):
    far, near = axes
    own = summed_on_arrival(cut_along(shard, dim, lax.axis_size(far)), near, dim + 1)
    return jnp.sum(lax.all_to_all(own, far, 0, 0, tiled=True), axis=0)


def on_device(
    hidden,
    queries,
    key_cache,
    value_cache,
    out_weight,
    norm_gain,
    router,
    expert_ids,
    gate_weight,
    up_weight,
    down_weight,
):
    count_local, heads_local, head_size = queries.shape
    kv_local = key_cache.shape[2]
    per_kv = heads_local // kv_local
    query_blocks = queries.reshape(count_local, kv_local, per_kv, head_size)
    scores = jnp.einsum(
        "tkgd,tpkd->tkgp", query_blocks, key_cache, preferred_element_type=jnp.float32
    ) / math.sqrt(head_size)
    attn_weights = jax.nn.softmax(scores, axis=-1).astype(jnp.bfloat16)
    attended = jnp.einsum(
        "tkgp,tpkd->tkgd", attn_weights, value_cache, preferred_element_type=jnp.float32
    )
    attended = attended.astype(jnp.bfloat16).reshape(count_local, heads_local * head_size)
    all_attended = gathered_copies(attended, SHARD, 0)
    partial_cols = jnp.dot(all_attended, out_weight, preferred_element_type=jnp.float32)
    partial_heads = lax.all_to_all(partial_cols, SHARD, split_axis=0, concat_axis=1, tiled=True)
    attn_out = taken_together(partial_heads, "expert")
    stream = hidden.astype(jnp.float32) + attn_out
    scaled = stream * lax.rsqrt(jnp.mean(stream * stream, axis=-1, keepdims=True) + 1e-05)
    normed = (scaled * norm_gain.astype(jnp.float32)).astype(jnp.bfloat16)
    everyone = whole_of(normed, (("shard_0", "shard_1"), "shard_2"), 0)
    token_count = everyone.shape[0]
    logits = jnp.dot(everyone, router, preferred_element_type=jnp.float32)
    top_first = jnp.take_along_axis(logits, expert_ids[:, 0:1], axis=1)[:, 0]
    top_second = jnp.take_along_axis(logits, expert_ids[:, 1:2], axis=1)[:, 0]
    weight_first = 1.0 / (1.0 + jnp.exp(top_second - top_first))
    weight_second = 1.0 / (1.0 + jnp.exp(top_first - top_second))
    local_experts = gate_weight.shape[0]
    group_index = lax.axis_index("expert")
    summed = jnp.zeros((token_count, everyone.shape[1]), jnp.float32)
    for member in range(local_experts):
        expert = group_index * local_experts + member
        in_first = expert_ids[:, 0] == expert
        in_second = expert_ids[:, 1] == expert
        routed_weight = jnp.where(in_first, weight_first, 0.0) + jnp.where(
            in_second, weight_second, 0.0
        )
        gated = jnp.dot(everyone, gate_weight[member], preferred_element_type=jnp.float32)
        upward = jnp.dot(everyone, up_weight[member], preferred_element_type=jnp.float32)
        activated = (jax.nn.silu(gated) * upward).astype(jnp.bfloat16)
        expert_out = jnp.dot(activated, down_weight[member], preferred_element_type=jnp.float32)
        summed = summed + routed_weight[:, None] * expert_out
    reduced = sum_in_two_steps(summed, (("shard_0", "shard_1"), "shard_2"), 0)
    expert_mix = taken_together(reduced, "expert")
    return (stream + expert_mix).astype(jnp.bfloat16)


def solution(mesh):
    split = Mesh(
        mesh.devices.reshape(mesh.shape["expert"], 4, 4, 2),
        ("expert", "shard_0", "shard_1", "shard_2"),
    )
    in_specs = (
        P(SHARD, None),
        P(SHARD, "expert", None),
        P(SHARD, None, "expert", None),
        P(SHARD, None, "expert", None),
        P("expert", SHARD),
        P(),
        P(),
        P(),
        P("expert", None, SHARD),
        P("expert", None, SHARD),
        P("expert", SHARD, None),
    )
    out_specs = P(SHARD, None)
    return jax.shard_map(
        on_device, mesh=split, in_specs=in_specs, out_specs=out_specs, check_vma=False
    )
```

profile of v0, /device:TPU:0, one launch (start us, length us, event | category | flops | bytes accessed | tf_op | source)
XLA Modules:
  0.0 172.5 jit_solution(3267594386998008416)
XLA Ops:
  0.0 1.6 copy-done
  1.6 1.4 fusion.36
  3.0 0.2 fusion.75
  3.2 2.1 %fusion.39 = bf16[8,2,4,128]{3,2,1,0:T(4,128)(2,1)S(1)} fusion(bf16[8,512,2,128]{3,2,1,0:T(2,128)(2,1)} %param.16, f32[8,2,4]{2,1,0:T(2,128)S(1)} %fusion.75, f32[8,2,4,512]{3,2,1,0:T(4,128)S(1)} %fusion.36), kind=kOutput, calls=%fused_computation.34 | convolution fusion | flops 8495679 | bytes 2244864 | tf_op jit(solution)/shard_map/tkgp,tpkd->tkgd/dot_general | solution.py:79
  5.4 19.8 %all_to_all.48 = bf16[32,8,1024]{2,1,0:T(8,128)(2,1)S(1)} all-to-all(bf16[32,8,1024]{2,1,0:T(8,128)(2,1)S(1)} %broadcast_in_dim.25), channel_id=1, replica_groups=mesh['expert'=4,'shard_0'=4,'shard_1'=4,'shard_2'=2] {'shard_0','shard_1..., dimensions={0} | all-to-all | bytes 1048576 | tf_op jit(solution)/shard_map/all_to_all | solution.py:20
  25.3 0.3 fusion.56
  25.6 11.2 %all_to_all.49 = f32[32,8,128]{2,1,0:T(8,128)S(1)} all-to-all(f32[32,8,128]{2,1,0:T(8,128)S(1)} %fusion.56), channel_id=1, replica_groups=mesh['expert'=4,'shard_0'=4,'shard_1'=4,'shard_2'=2] {'shard_0','shard_1..., dimensions={0} | all-to-all | bytes 262144 | tf_op jit(solution)/shard_map/all_to_all | solution.py:85
  36.8 0.8 broadcast_in_dim.27
  37.6 4.3 %all-to-all-start.2 = ((f32[4,8,4096]{2,1,0:T(8,128)}), f32[4,8,4096]{2,1,0:T(8,128)S(1)}, u32[]{:S(2)}, u32[]{:S(2)}) async-start(f32[4,8,4096]{2,1,0:T(8,128)} %broadcast_in_dim.27), calls=%async_computation.2 | async-start | bytes 1048576 | tf_op jit(solution)/shard_map/all_to_all | solution.py:20
  41.9 9.7 %all-to-all-done.2 = f32[4,8,4096]{2,1,0:T(8,128)S(1)} async-done(((f32[4,8,4096]{2,1,0:T(8,128)}), f32[4,8,4096]{2,1,0:T(8,128)S(1)}, u32[]{:S(2)}, u32[]{:S(2)}) %all-to-all-start.2) | async-done | bytes 524320 | tf_op jit(solution)/shard_map/all_to_all | solution.py:20
  51.7 0.1 multiply_reduce_fusion
  51.9 0.1 multiply_convert_fusion
  52.0 1.1 broadcast_in_dim.28
  53.1 3.7 %all-to-all-start.3 = ((bf16[16,8,4096]{2,1,0:T(8,128)(2,1)}), bf16[16,8,4096]{2,1,0:T(8,128)(2,1)S(1)}, u32[]{:S(2)}, u32[]{:S(2)}) async-start(bf16[16,8,4096]{2,1,0:T(8,128)(2,1)} %broadcast_in_dim.28), calls=%async_computation.3 | async-start | bytes 2097152 | tf_op jit(solution)/shard_map/all_to_all | solution.py:20
  56.8 16.8 %all-to-all-done.3 = bf16[16,8,4096]{2,1,0:T(8,128)(2,1)S(1)} async-done(((bf16[16,8,4096]{2,1,0:T(8,128)(2,1)}), bf16[16,8,4096]{2,1,0:T(8,128)(2,1)S(1)}, u32[]{:S(2)}, u32[]{:S(2)}) %all-to-all-start.3) | async-done | bytes 1048608 | tf_op jit(solution)/shard_map/all_to_all | solution.py:20
  73.6 0.3 broadcast_in_dim.54
  73.9 5.7 %all_to_all.50 = bf16[2,16,8,4096]{3,2,1,0:T(8,128)(2,1)S(1)} all-to-all(bf16[2,16,8,4096]{3,2,1,0:T(8,128)(2,1)S(1)} %broadcast_in_dim.54), channel_id=1, replica_groups=mesh['expert'=4,'shard_0'=4,'shard_1'=4,'shard_2'=2] {'shard_2'}, dimensions={0} | all-to-all | bytes 4194304 | tf_op jit(solution)/shard_map/all_to_all | solution.py:20
  79.6 0.2 copy.22
  79.8 4.1 %fusion.5 = f32[256,448]{0,1:T(8,128)S(1)} fusion(bf16[256,4096]{1,0:T(8,128)(2,1)S(1)} %bitcast.71, bf16[2,4096,448]{1,2,0:T(8,128)(2,1)} %param.21), kind=kOutput, calls=%fused_computation.10 | convolution fusion | flops 939524096 | bytes 6225920 | tf_op jit(solution)/shard_map/dot_general | solution.py:107
  83.9 1.1 fusion.10
  85.1 0.6 fusion.76
  85.7 1.8 %gather_fusion.1 = f32[256]{0:T(256)S(1)} fusion(f32[256,8]{0,1:T(8,128)S(1)} %fusion.76, s32[256]{0:T(256)S(1)} %bitcast.69), kind=kCustom, calls=%fused_computation.1.clone | custom fusion | bytes 4096 | tf_op jit(solution)/shard_map/jit(take_along_axis)/gather | solution.py:93
  87.6 1.8 %gather_fusion = f32[256]{0:T(256)S(1)} fusion(f32[256,8]{0,1:T(8,128)S(1)} %fusion.76, s32[256]{0:T(256)S(1)} %bitcast.68), kind=kCustom, calls=%fused_computation.clone | custom fusion | bytes 4096 | tf_op jit(solution)/shard_map/jit(take_along_axis)/gather | solution.py:94
  89.5 10.0 %convolution_multiply_fusion.1 = f32[256,4096]{1,0:T(8,128)} fusion(bf16[2,448,4096]{2,1,0:T(8,128)(2,1)} %param.23, f32[256]{0:T(256)S(1)} %bitcast.82, bf16[256,4096]{1,0:T(8,128)(2,1)} %bitcast.74, bf16[2,4096,448]{1,2,0:T(8,128)(2,1)} %param.22, f32[256,448]{0,1:T(8,128)S(1)} %fusion.10), kind=kOutput, calls=%fused_computation.5 | convolution fusion | flops 1880784896 | bytes 14091264 | tf_op jit(solution)/shard_map/dot_general | solution.py:110
  99.4 11.2 %fusion.1 = f32[256,4096]{1,0:T(8,128)} fusion(f32[256,4096]{1,0:T(8,128)} %convolution_multiply_fusion.1, bf16[2,448,4096]{2,1,0:T(8,128)(2,1)} %param.23, f32[256]{0:T(256)S(1)} %bitcast.81, bf16[256,4096]{1,0:T(8,128)(2,1)} %bitcast.75, bf16[2,4096,448]{1,2,0:T(8,128)(2,1)} %param.22, f32[256,448]{0,1:T(8,128)S(1)} %fusion.5), kind=kOutput, calls=%fused_computation.4 | convolution fusion | flops 1881833472 | bytes 18285568 | tf_op jit(solution)/shard_map/dot_general | solution.py:110
  110.6 2.5 %copy.33 = f32[16,2,8,4096]{3,2,0,1:T(8,128)S(1)} copy(f32[16,2,8,4096]{3,2,1,0:T(8,128)} %bitcast.76) | data formatting | bytes 8388608 | tf_op jit(solution)/shard_map/reshape;reshape | solution.py:42
  113.1 8.2 %all_to_all.51 = f32[2,16,8,4096]{3,2,1,0:T(8,128)} all-to-all(f32[2,16,8,4096]{3,2,1,0:T(8,128)S(1)} %bitcast.70), channel_id=1, replica_groups=mesh['expert'=4,'shard_0'=4,'shard_1'=4,'shard_2'=2] {'shard_2'}, dimensions={0} | all-to-all | bytes 8388608 | tf_op jit(solution)/shard_map/all_to_all | solution.py:48
  121.3 4.0 %reduce_sum.57 = f32[16,8,4096]{2,1,0:T(8,128)} reduce(f32[2,16,8,4096]{3,2,1,0:T(8,128)} %all_to_all.51, f32[]{:T(128)} %constant.8.clone.1), dimensions={0}, to_apply=%region_4.6 | reduce | flops 524288 | bytes 6291460 | tf_op jit(solution)/shard_map/reduce_sum | solution.py:49
  125.3 33.5 %all_to_all.52 = f32[16,8,4096]{2,1,0:T(8,128)} all-to-all(f32[16,8,4096]{2,1,0:T(8,128)} %reduce_sum.57), channel_id=1, replica_groups=mesh['expert'=4,'shard_0'=4,'shard_1'=4,'shard_2'=2] {'shard_0','shard_1'}, dimensions={0} | all-to-all | bytes 4194304 | tf_op jit(solution)/shard_map/all_to_all | solution.py:55
  158.8 1.7 reduce_sum.58
  160.5 11.3 %all_to_all.53 = f32[4,8,4096]{2,1,0:T(8,128)S(1)} all-to-all(f32[4,8,4096]{2,1,0:T(8,128)S(1)} %broadcast_in_dim.56), channel_id=1, replica_groups=mesh['expert'=4,'shard_0'=4,'shard_1'=4,'shard_2'=2] {'expert'}, dimensions={0} | all-to-all | bytes 1048576 | tf_op jit(solution)/shard_map/all_to_all | solution.py:20
  171.9 0.7 add_convert_fusion
  (32 shorter events, 0.3 us)
Async XLA Ops:
  0.0 1.6 copy-start
  1.6 23.7 %copy-start.3 = (bf16[1024,128]{1,0:T(8,128)(2,1)S(1)}, bf16[1024,128]{1,0:T(8,128)(2,1)}, u32[]{:S(2)}) copy-start(bf16[1024,128]{1,0:T(8,128)(2,1)} %param.17) | copy-start | bytes 786436
  3.2 38.7 %copy-start.6 = (bf16[4096]{0:T(1024)(128)(2,1)S(1)}, bf16[4096]{0:T(1024)(128)(2,1)}, u32[]{:S(2)}) copy-start(bf16[4096]{0:T(1024)(128)(2,1)} %param.18) | copy-start | bytes 24580
  3.2 48.5 %copy-start.2 = (bf16[8,4096]{1,0:T(8,128)(2,1)S(1)}, bf16[8,4096]{1,0:T(8,128)(2,1)}, u32[]{:S(2)}) copy-start(bf16[8,4096]{1,0:T(8,128)(2,1)} %param.13) | copy-start | bytes 196612
  25.2 31.5 %copy-start.5 = (s32[256,2]{0,1:T(2,128)S(1)}, s32[256,2]{0,1:T(2,128)}, u32[]{:S(2)}) copy-start(s32[256,2]{0,1:T(2,128)} %param.20) | copy-start | bytes 6148
  37.6 14.0 %all-to-all-start.2 = ((f32[4,8,4096]{2,1,0:T(8,128)}), f32[4,8,4096]{2,1,0:T(8,128)S(1)}, u32[]{:S(2)}, u32[]{:S(2)}) async-start(f32[4,8,4096]{2,1,0:T(8,128)} %broadcast_in_dim.27), calls=%async_computation.2 | async-start | bytes 1048576 | tf_op jit(solution)/shard_map/all_to_all | solution.py:20
  53.1 20.6 %all-to-all-start.3 = ((bf16[16,8,4096]{2,1,0:T(8,128)(2,1)}), bf16[16,8,4096]{2,1,0:T(8,128)(2,1)S(1)}, u32[]{:S(2)}, u32[]{:S(2)}) async-start(bf16[16,8,4096]{2,1,0:T(8,128)(2,1)} %broadcast_in_dim.28), calls=%async_computation.3 | async-start | bytes 2097152 | tf_op jit(solution)/shard_map/all_to_all | solution.py:20
  73.9 10.0 %slice-start = ((s8[7340032]{0:T(1024)(128)(4,1)}), s8[4194304]{0:T(1024)(128)(4,1)S(1)}, s32[]{:S(2)}) async-start(s8[7340032]{0:T(1024)(128)(4,1)} %bitcast.83), calls=%async_computation.8 | async-start | bytes 8388608
  79.6 4.3 %slice-start.1 = ((s8[7340032]{0:T(1024)(128)(4,1)}), s8[3145728]{0:T(1024)(128)(4,1)S(1)}, s32[]{:S(2)}) async-start(s8[7340032]{0:T(1024)(128)(4,1)} %bitcast.83), calls=%async_computation.9 | async-start | bytes 6291456
  79.8 5.3 %copy-start.1 = (bf16[2,16,8,4096]{3,2,0,1:T(8,128)(2,1)}, bf16[2,16,8,4096]{3,2,0,1:T(8,128)(2,1)S(1)}, u32[]{:S(2)}) copy-start(bf16[2,16,8,4096]{3,2,0,1:T(8,128)(2,1)S(1)} %copy.22) | copy-start | bytes 6291460
  83.9 1.2 copy-start.4
where the time goes:
time: 173 us
  blocking collectives  89.8 us (52%)
  matrix products  30.8 us (18%)
  waiting for transfers between devices  26.6 us (15%)
  local copies, waits for them, and re-layouts  10.3 us (6%)
  starting transfers between devices  7.95 us (5%)
  other arithmetic  6.97 us (4%)
    all_to_all x3, blocking collectives, copy_for_each(): lax.all_to_all(jnp.broadcast_to(shard[None], (size, *shard.shape)), axis,...  36.8 us
    all_to_all x1, blocking collectives, sum_in_two_steps(): return jnp.sum(lax.all_to_all(own, far, 0, 0, tiled=True), axis=0)  33.5 us
    all_to_all x2, waiting for transfers between devices, copy_for_each(): lax.all_to_all(jnp.broadcast_to(shard[None], (size, *shard.shape)), axis,...  26.6 us
    dot_general x2, matrix products, on_device(): jnp.dot(activated, down_weight[member], preferred_element_type=jnp.float32)  21.1 us
    all_to_all x1, blocking collectives, on_device(): lax.all_to_all(partial_cols, SHARD, split_axis=0, concat_axis=1, tiled=True)  11.2 us
    all_to_all x1, blocking collectives, summed_on_arrival(): lax.all_to_all(pieces, axis, split_axis=0, concat_axis=0, tiled=True)  8.17 us
    all_to_all x2, starting transfers between devices, copy_for_each(): lax.all_to_all(jnp.broadcast_to(shard[None], (size, *shard.shape)), axis,...  7.95 us
    dot_general x2, matrix products, on_device(): jnp.dot(everyone, gate_weight[member], preferred_element_type=jnp.float32)  5.2 us
  transfers between devices with their start and end apart: 2, of which 2 were waited for; matrix products, arithmetic and copies ran while one was open for 0% of the time, Pallas kernels for 0%

commit v1 on v0

v1 whole, which is shorter than its diff:
```python
import functools
import math

import jax
import jax.numpy as jnp
from jax import lax
from jax.experimental import pallas as pl
from jax.experimental.pallas import tpu as pltpu
from jax.sharding import Mesh
from jax.sharding import PartitionSpec as P

SHARD = ("shard_0", "shard_1", "shard_2")
PLANE = ("shard_0", "shard_1")
CORE_MAJOR = ("shard_2", "shard_0", "shard_1")
F32 = jnp.float32
BF16 = jnp.bfloat16


def shifted(x, axis, by):
    size = lax.axis_size(axis)
    return lax.ppermute(x, axis, [(i, (i + by) % size) for i in range(size)])


def sum_over_groups(part):
    one, two, three = (shifted(part, "expert", by) for by in (1, 2, 3))
    return (part.astype(F32) + two.astype(F32)) + (one.astype(F32) + three.astype(F32))


def expert_kernel(
    place, own, partner, ids, gain, router, attn, gate, up, down,
    send, keep, weights, down_v, mixed, hidden_t, act, sems,
):
    core, shard, first_expert, adds = place[0], place[1], place[2], place[3]
    units = gate.shape[0]
    half_units = units // 2
    tokens = own.shape[2]
    half = tokens // 2
    width = down.shape[1]
    block = own.shape[1]
    copies = [
        pltpu.make_async_copy(
            source.at[pl.ds(m * half_units, half_units)],
            weights.at[pl.ds(at + m * half_units, half_units)],
            sems.at[number * 2 + m],
        )
        for number, (source, at) in enumerate(((gate, 0), (up, units)))
        for m in range(2)
    ]
    copies = [copies[0], copies[2], copies[1], copies[3]]
    last = pltpu.make_async_copy(down, down_v, sems.at[4])
    for copy in copies:
        copy.start()
    last.start()

    def norm_block(j, squares):
        for mine, part in ((core, own), (1 - core, partner)):
            x = part[j]
            rows = pl.ds(pl.multiple_of((2 * j + mine) * block, block), block)
            g = gain[rows, :]
            mixed[rows, :] = (
                x.astype(F32) * jnp.concatenate([g, g], axis=1).astype(F32)
            ).astype(BF16)
            y = x.astype(F32)
            squares = squares + (y * y).reshape(block // 8, 8, tokens).sum(axis=0)
        return squares

    squares = lax.fori_loop(0, own.shape[0], norm_block, jnp.zeros((8, tokens), F32))
    scale = lax.rsqrt(squares.sum(axis=0, keepdims=True) / width + 1e-05)
    logits = jnp.dot(router[...], mixed[...], preferred_element_type=F32) * scale
    numbers = lax.broadcasted_iota(jnp.int32, logits.shape, 0)
    first, second = ids[0:1, :], ids[1:2, :]
    a = jnp.where(numbers == first, logits, 0.0).sum(axis=0, keepdims=True)
    b = jnp.where(numbers == second, logits, 0.0).sum(axis=0, keepdims=True)
    weight_first = 1.0 / (1.0 + jnp.exp(b - a))
    weight_second = 1.0 / (1.0 + jnp.exp(a - b))

    for at, copy in zip((0, units, half_units, units + half_units), copies):
        copy.wait()
        hidden_t[pl.ds(at, half_units), :] = jnp.dot(
            weights[pl.ds(at, half_units), :], mixed[...], preferred_element_type=F32
        )

    for m in range(2):
        expert = first_expert + m
        routed = jnp.where(first == expert, weight_first, 0.0) + jnp.where(
            second == expert, weight_second, 0.0
        )
        gated = hidden_t[pl.ds(m * half_units, half_units), :] * scale
        upward = hidden_t[pl.ds(units + m * half_units, half_units), :] * scale
        value = gated / (1.0 + jnp.exp(-gated)) * upward * routed
        turned = value.T.astype(BF16)
        for h in range(2):
            rows = pl.ds(pl.multiple_of(jnp.where(core == h, half, 0), half), half)
            act[m, rows, :] = turned[h * half : (h + 1) * half, :]

    last.wait()
    step = 512

    def down_block(n, carry):
        columns = pl.ds(pl.multiple_of(n * step, step), step)
        total = jnp.dot(
            act[0], down_v[pl.ds(0, half_units), columns], preferred_element_type=F32
        ) + jnp.dot(
            act[1], down_v[pl.ds(half_units, half_units), columns], preferred_element_type=F32
        )
        send[:, columns] = total[:half].astype(BF16)
        keep[:, columns] = total[half:]
        return carry

    lax.fori_loop(0, width // step, down_block, 0)
    rows = attn[...].T * adds.astype(F32)
    columns = pl.ds(pl.multiple_of(shard * block, block), block)
    theirs = jnp.where(core == 0, rows[half:], rows[:half])
    mine = jnp.where(core == 0, rows[:half], rows[half:])
    keep[:, columns] += mine
    send[:, columns] = (send[:, columns].astype(F32) + theirs).astype(BF16)


def experts(place, own, partner, ids, gain, router, attn, gate, up, down):
    units, width = down.shape
    tokens = own.shape[2]
    vmem = pl.BlockSpec(memory_space=pltpu.VMEM)
    hbm = pl.BlockSpec(memory_space=pl.ANY)
    return pl.pallas_call(
        expert_kernel,
        out_shape=(
            jax.ShapeDtypeStruct((tokens // 2, width), BF16),
            jax.ShapeDtypeStruct((tokens // 2, width), F32),
        ),
        in_specs=[pl.BlockSpec(memory_space=pltpu.SMEM)] + [vmem] * 6 + [hbm] * 3,
        out_specs=(vmem, vmem),
        scratch_shapes=[
            pltpu.VMEM((2 * units, width), BF16),
            pltpu.VMEM((units, width), BF16),
            pltpu.VMEM((width, tokens), BF16),
            pltpu.VMEM((2 * units, tokens), F32),
            pltpu.VMEM((2, tokens, units // 2), BF16),
            pltpu.SemaphoreType.DMA((5,)),
        ],
        compiler_params=pltpu.CompilerParams(vmem_limit_bytes=60 * 1024 * 1024),
        cost_estimate=pl.CostEstimate(
            flops=6 * tokens * units * width,
            bytes_accessed=6 * units * width,
            transcendentals=2 * units * tokens,
        ),
        name="experts",
    )(place, own, partner, ids, gain, router, attn, gate, up, down)


def on_device(
    hidden, queries, key_cache, value_cache, out_weight, norm_gain, router,
    expert_ids, gate_weight, up_weight, down_weight,
):
    count_local, heads_local, head_size = queries.shape
    kv_local = key_cache.shape[2]
    width = hidden.shape[1]
    block = out_weight.shape[1]
    chips, cores = lax.axis_size(PLANE), lax.axis_size("shard_2")
    shards = chips * cores
    tokens = shards * count_local
    query_blocks = queries.reshape(count_local, kv_local, heads_local // kv_local, head_size)
    scores = jnp.einsum(
        "tkgd,tpkd->tkgp", query_blocks, key_cache, preferred_element_type=F32
    ) / math.sqrt(head_size)
    attn_weights = jax.nn.softmax(scores, axis=-1).astype(BF16)
    attended = jnp.einsum(
        "tkgp,tpkd->tkgd", attn_weights, value_cache, preferred_element_type=F32
    )
    attended = attended.astype(BF16).reshape(count_local, heads_local * head_size)
    own_cols = hidden.reshape(count_local, chips, cores, block).transpose(2, 1, 0, 3)
    pieces = jnp.concatenate(
        [
            jnp.broadcast_to(attended[None], (shards, *attended.shape)),
            own_cols.reshape(shards, count_local, block),
        ],
        axis=-1,
    )
    arrived = lax.all_to_all(pieces, CORE_MAJOR, 0, 0, tiled=True).reshape(tokens, -1)
    heads = attended.shape[1]
    part = lax.dot_general(
        out_weight, arrived[:, :heads], (((0,), (1,)), ((), ())), preferred_element_type=F32
    ).astype(BF16)
    hidden_t = arrived[:, heads:].T.astype(F32)
    attn_out = sum_over_groups(part)
    stream = (attn_out + hidden_t).astype(BF16)
    own = lax.all_to_all(
        jnp.broadcast_to(stream[None], (chips, block, tokens)), PLANE, 0, 0, tiled=True
    )
    partner = shifted(own, "shard_2", 1)
    core = lax.axis_index("shard_2")
    shard = lax.axis_index(PLANE) * cores + core
    group = lax.axis_index("expert")
    local = gate_weight.shape[0]
    place = jnp.stack([core, shard, group * local, (group == 0).astype(jnp.int32)]).astype(jnp.int32)
    ids = expert_ids.reshape(chips, cores, count_local, 2).transpose(3, 1, 0, 2).reshape(2, tokens)
    units = local * gate_weight.shape[2]
    send, keep = experts(
        place,
        own,
        partner,
        ids,
        jnp.broadcast_to(norm_gain[:, None], (width, 128)),
        router.T,
        attn_out,
        gate_weight.transpose(0, 2, 1).reshape(units, width),
        up_weight.transpose(0, 2, 1).reshape(units, width),
        down_weight.reshape(units, width),
    )
    pair = (keep + shifted(send, "shard_2", 1).astype(F32)).astype(BF16)
    parts = lax.all_to_all(pair.reshape(chips, count_local, width), PLANE, 0, 0, tiled=True)
    reduced = parts.astype(F32).sum(axis=0).astype(BF16)
    return (hidden.astype(F32) + sum_over_groups(reduced)).astype(BF16)


def solution(mesh):
    split = Mesh(
        mesh.devices.reshape(mesh.shape["expert"], 4, 4, 2),
        ("expert", "shard_0", "shard_1", "shard_2"),
    )
    in_specs = (
        P(SHARD, None),
        P(SHARD, "expert", None),
        P(SHARD, None, "expert", None),
        P(SHARD, None, "expert", None),
        P("expert", SHARD),
        P(),
        P(),
        P(),
        P("expert", None, SHARD),
        P("expert", None, SHARD),
        P("expert", SHARD, None),
    )
    return jax.shard_map(
        on_device, mesh=split, in_specs=in_specs, out_specs=P(SHARD, None), check_vma=False
    )
```

time: 173 us -> 113 us (0.65)
  blocking collectives: 89.8 us -> 61.5 us
  matrix products: 30.8 us -> 3.72 us
  Pallas kernels: 0 us -> 17.3 us
  waiting for transfers between devices: 26.6 us -> 12.4 us
  local copies, waits for them, and re-layouts: 10.3 us -> 4.41 us
  other arithmetic: 6.97 us -> 4.24 us
    all_to_all x6 -> x3, blocking collectives: 89.8 us -> 61.5 us  [the longest x1 20.9 us: on_device(): lax.all_to_all(pieces, CORE_MAJOR, 0, 0, tiled=True).reshape(tokens, -1)]
    dot_general x6 -> x1, matrix products: 27.3 us -> 0.31 us  [on_device(): lax.dot_general(out_weight, arrived[:, :heads], (((0,), (1,)), ((), ())),...]
    all_to_all x2 -> x0, waiting for transfers between devices: 26.6 us -> none  [copy_for_each(): lax.all_to_all(jnp.broadcast_to(shard[None], (size, *shard.shape)), axis,...]
    pallas_call x0 -> x1, Pallas kernels: none -> 17.3 us  [experts(): pl.pallas_call(expert_kernel, out_shape=(jax.ShapeDtypeStruct((tokens //...]
    ppermute x0 -> x8, waiting for transfers between devices: none -> 12.4 us  [shifted(): return lax.ppermute(x, axis, [(i, (i + by) % size) for i in range(size)])]
    ppermute x0 -> x8, starting transfers between devices: none -> 8.68 us  [shifted(): return lax.ppermute(x, axis, [(i, (i + by) % size) for i in range(size)])]
    all_to_all x2 -> x0, starting transfers between devices: 7.95 us -> none  [copy_for_each(): lax.all_to_all(jnp.broadcast_to(shard[None], (size, *shard.shape)), axis,...]
    reduce_sum x5 -> x1, other arithmetic: 5.92 us -> 0.14 us  [on_device(): reduced = parts.astype(F32).sum(axis=0).astype(BF16)]
  transfers between devices with their start and end apart: 2 -> 8, of which waited for: 2 -> 5; matrix products, arithmetic and copies ran while one was open for 0% -> 1% of each run, Pallas kernels for 0% -> 0%
where the time goes in v1:
time: 113 us; the launch traced here: 112 us
  blocking collectives  61.5 us (54%)
  Pallas kernels  17.3 us (15%)
  waiting for transfers between devices  12.4 us (11%)
  starting transfers between devices  8.68 us (8%)
  local copies, waits for them, and re-layouts  4.41 us (4%)
  other arithmetic  4.24 us (4%)
  matrix products  3.72 us (3%)
    all_to_all x1, blocking collectives, on_device(): lax.all_to_all(pieces, CORE_MAJOR, 0, 0, tiled=True).reshape(tokens, -1)  20.9 us
    all_to_all x1, blocking collectives, on_device(): lax.all_to_all(pair.reshape(chips, count_local, width), PLANE, 0, 0, tile...  20.5 us
    all_to_all x1, blocking collectives, on_device(): lax.all_to_all(jnp.broadcast_to(stream[None], (chips, block, tokens)), PL...  20.1 us
    pallas_call x1, Pallas kernels, experts(): pl.pallas_call(expert_kernel, out_shape=(jax.ShapeDtypeStruct((tokens //...  17.3 us
    ppermute x8, waiting for transfers between devices, shifted(): return lax.ppermute(x, axis, [(i, (i + by) % size) for i in range(size)])  12.4 us
    ppermute x8, starting transfers between devices, shifted(): return lax.ppermute(x, axis, [(i, (i + by) % size) for i in range(size)])  8.68 us
  transfers between devices with their start and end apart: 8, of which 5 were waited for; matrix products, arithmetic and copies ran while one was open for 1% of the time, Pallas kernels for 0%

profile of v1, /device:TPU:0, one launch (start us, length us, event | category | flops | bytes accessed | tf_op | source)
XLA Modules:
  0.0 112.3 jit_solution(10082928278059167109)
XLA Ops:
  0.0 1.0 copy.20
  1.0 0.6 copy-done
  1.6 1.4 %fusion.7 = f32[8,2,4,512]{3,2,1,0:T(4,128)S(1)} fusion(bf16[8,2,4,128]{3,2,1,0:T(4,128)(2,1)} %bitcast.44, bf16[8,512,2,128]{3,2,1,0:T(2,128)(2,1)S(1)} %copy-done), kind=kOutput, calls=%fused_computation.8 | convolution fusion | flops 8421376 | bytes 2244608 | tf_op jit(solution)/shard_map/tkgd,tpkd->tkgp/dot_general | solution.py:162
  3.0 0.2 fusion.18
  3.2 2.1 %fusion.11 = bf16[8,2,4,128]{3,2,1,0:T(4,128)(2,1)S(1)} fusion(bf16[8,512,2,128]{3,2,1,0:T(2,128)(2,1)} %param.14, f32[8,2,4]{2,1,0:T(2,128)S(1)} %fusion.18, f32[8,2,4,512]{3,2,1,0:T(4,128)S(1)} %fusion.7), kind=kOutput, calls=%fused_computation.11 | convolution fusion | flops 8495679 | bytes 2244864 | tf_op jit(solution)/shard_map/tkgp,tpkd->tkgd/dot_general | solution.py:166
  5.3 0.1 broadcast_in_dim.9
  5.4 20.9 %all_to_all.15 = bf16[32,8,1152]{2,1,0:T(8,128)(2,1)S(1)} all-to-all(bf16[32,8,1152]{2,1,0:T(8,128)(2,1)S(1)} %pad_maximum_fusion), channel_id=1, replica_groups=mesh['expert'=4,'shard_0'=4,'shard_1'=4,'shard_2'=2] {'shard_2','shard_0..., dimensions={0} | all-to-all | bytes 1179648 | tf_op jit(solution)/shard_map/all_to_all | solution.py:178
  26.3 0.3 fusion.10
  26.6 2.8 %collective-permute-start.2 = (bf16[128,256]{1,0:T(8,128)(2,1)S(1)}, bf16[128,256]{1,0:T(8,128)(2,1)S(1)}, u32[]{:S(2)}, u32[]{:S(2)}) collective-permute-start(bf16[128,256]{1,0:T(8,128)(2,1)S(1)} %fusion.10), channel_id=1, source_target_pairs={{0,96},{32,0},{64,32},{96,64},{1,97},{33,1},{65,33},{97,65},{2,98}... | collective-permute-start | bytes 196616 | tf_op jit(solution)/shard_map/ppermute | solution.py:21
  29.5 2.3 %collective-permute-start = (bf16[128,256]{1,0:T(8,128)(2,1)S(1)}, bf16[128,256]{1,0:T(8,128)(2,1)S(1)}, u32[]{:S(2)}, u32[]{:S(2)}) collective-permute-start(bf16[128,256]{1,0:T(8,128)(2,1)S(1)} %fusion.10), channel_id=1, source_target_pairs={{0,64},{32,96},{64,0},{96,32},{1,65},{33,97},{65,1},{97,33},{2,66}... | collective-permute-start | bytes 196616 | tf_op jit(solution)/shard_map/ppermute | solution.py:21
  31.8 0.1 copy.25
  31.9 3.8 %collective-permute-done.1 = bf16[128,256]{1,0:T(8,128)(2,1)S(1)} collective-permute-done((bf16[128,256]{1,0:T(8,128)(2,1)S(1)}, bf16[128,256]{1,0:T(8,128)(2,1)S(1)}, u32[]{:S(2)}, u32[]{:S(2)}) %collective-permute-start.1) | collective-permute-done | bytes 65568 | tf_op jit(solution)/shard_map/ppermute | solution.py:21
  35.7 0.7 fusion.16
  36.4 0.1 broadcast_in_dim.10
  36.5 20.1 %all_to_all.16.own = bf16[16,128,256]{2,1,0:T(8,128)(2,1)S(1)} all-to-all(bf16[16,128,256]{2,1,0:T(8,128)(2,1)S(1)} %broadcast_in_dim.10), channel_id=1, replica_groups=mesh['expert'=4,'shard_0'=4,'shard_1'=4,'shard_2'=2] {'shard_0','shard_1'}, dimensions={0} | all-to-all | bytes 2097152 | tf_op jit(solution)/shard_map/all_to_all | solution.py:186
  56.5 0.1 reshape.39
  56.7 0.8 reshape.40.ids
  57.5 0.7 pad_add_fusion.place
  58.1 1.2 %collective-permute-done.3.partner = bf16[16,128,256]{2,1,0:T(8,128)(2,1)} collective-permute-done((bf16[16,128,256]{2,1,0:T(8,128)(2,1)S(1)}, bf16[16,128,256]{2,1,0:T(8,128)(2,1)}, u32[]{:S(2)}, u32[]{:S(2)}) %collective-permute-start.3) | collective-permute-done | bytes 1048608 | tf_op jit(solution)/shard_map/ppermute | solution.py:21
  59.3 1.6 %broadcast_in_dim.11.gain = bf16[4096,128]{1,0:T(8,128)(2,1)} broadcast(bf16[4096]{0:T(1024)(128)(2,1)S(1)} %copy-done.3), dimensions={0} | broadcast | bytes 1056768 | tf_op jit(solution)/shard_map/broadcast_in_dim | solution.py:202
  60.9 17.3 %experts.1 = (bf16[128,4096]{1,0:T(8,128)(2,1)}, f32[128,4096]{1,0:T(8,128)}) custom-call(s32[4]{0:T(128)} %pad_add_fusion.place, bf16[16,128,256]{2,1,0:T(8,128)(2,1)} %copy-done.1, bf16[16,128,256]{2,1,0:T(8,128)(2,1)} %collective-permute-done.3.partner, s32[2,256]{1,0:T(2,128)} %reshape.40.ids, bf16[4096,128]{1,0:T(8,128)(2,1)} %broadcast_in_dim.11.gain, ...), custom_call_target="tpu_custom_call" | custom-call | flops 5637144576 | bytes 22020096 | tf_op jit(solution)/shard_map/experts/pallas_call | solution.py:124
  78.2 0.2 collective-permute-start.4
  78.4 2.7 %collective-permute-done.4 = bf16[128,4096]{1,0:T(8,128)(2,1)S(1)} collective-permute-done((bf16[128,4096]{1,0:T(8,128)(2,1)}, bf16[128,4096]{1,0:T(8,128)(2,1)S(1)}, u32[]{:S(2)}, u32[]{:S(2)}) %collective-permute-start.4) | collective-permute-done | bytes 1048608 | tf_op jit(solution)/shard_map/ppermute | solution.py:21
  81.2 1.8 %fusion.14 = bf16[16,8,4096]{2,1,0:T(8,128)(2,1)S(1)} fusion(f32[128,4096]{1,0:T(8,128)} %get-tuple-element.7, bf16[128,4096]{1,0:T(8,128)(2,1)S(1)} %collective-permute-done.4), kind=kLoop, calls=%fused_computation.12 | loop fusion | flops 1572864 | bytes 4194304 | tf_op jit(solution)/shard_map/reshape | solution.py:210
  83.0 20.5 %all_to_all.17 = bf16[16,8,4096]{2,1,0:T(8,128)(2,1)S(1)} all-to-all(bf16[16,8,4096]{2,1,0:T(8,128)(2,1)S(1)} %fusion.14), channel_id=1, replica_groups=mesh['expert'=4,'shard_0'=4,'shard_1'=4,'shard_2'=2] {'shard_0','shard_1'}, dimensions={0} | all-to-all | bytes 2097152 | tf_op jit(solution)/shard_map/all_to_all | solution.py:210
  103.5 0.1 reduce_sum.22
  103.7 1.8 %collective-permute-start.7 = (bf16[8,4096]{1,0:T(8,128)(2,1)S(1)}, bf16[8,4096]{1,0:T(8,128)(2,1)S(1)}, u32[]{:S(2)}, u32[]{:S(2)}) collective-permute-start(bf16[8,4096]{1,0:T(8,128)(2,1)S(1)} %reduce_sum.22), channel_id=1, source_target_pairs={{0,96},{32,0},{64,32},{96,64},{1,97},{33,1},{65,33},{97,65},{2,98}... | collective-permute-start | bytes 196616 | tf_op jit(solution)/shard_map/ppermute | solution.py:21
  105.5 0.3 collective-permute-start.6
  105.8 1.3 %collective-permute-start.5 = (bf16[8,4096]{1,0:T(8,128)(2,1)S(1)}, bf16[8,4096]{1,0:T(8,128)(2,1)S(1)}, u32[]{:S(2)}, u32[]{:S(2)}) collective-permute-start(bf16[8,4096]{1,0:T(8,128)(2,1)S(1)} %reduce_sum.22), channel_id=1, source_target_pairs={{0,64},{32,96},{64,0},{96,32},{1,65},{33,97},{65,1},{97,33},{2,66}... | collective-permute-start | bytes 196616 | tf_op jit(solution)/shard_map/ppermute | solution.py:21
  107.0 1.0 collective-permute-done.7
  108.0 3.6 %collective-permute-done.6 = bf16[8,4096]{1,0:T(8,128)(2,1)S(1)} collective-permute-done((bf16[8,4096]{1,0:T(8,128)(2,1)S(1)}, bf16[8,4096]{1,0:T(8,128)(2,1)S(1)}, u32[]{:S(2)}, u32[]{:S(2)}) %collective-permute-start.6) | collective-permute-done | bytes 65568 | tf_op jit(solution)/shard_map/ppermute | solution.py:21
  111.7 0.7 add_convert_fusion.1
  (20 shorter events, 0.1 us)
Async XLA Ops:
  0.0 1.6 %copy-start = (bf16[8,512,2,128]{3,2,1,0:T(2,128)(2,1)S(1)}, bf16[8,512,2,128]{3,2,1,0:T(2,128)(2,1)}, u32[]{:S(2)}) copy-start(bf16[8,512,2,128]{3,2,1,0:T(2,128)(2,1)} %param.13) | copy-start | bytes 6291460
  5.3 21.0 %copy-start.5 = (bf16[1024,128]{1,0:T(8,128)(2,1)S(1)}, bf16[1024,128]{1,0:T(8,128)(2,1)}, u32[]{:S(2)}) copy-start(bf16[1024,128]{1,0:T(8,128)(2,1)} %param.15) | copy-start | bytes 786436
  26.6 29.9 %copy-start.4 = (s32[256,2]{0,1:T(2,128)S(1)}, s32[256,2]{0,1:T(2,128)}, u32[]{:S(2)}) copy-start(s32[256,2]{0,1:T(2,128)} %param.18) | copy-start | bytes 6148
  26.6 32.7 %copy-start.3 = (bf16[4096]{0:T(1024)(128)(2,1)S(1)}, bf16[4096]{0:T(1024)(128)(2,1)}, u32[]{:S(2)}) copy-start(bf16[4096]{0:T(1024)(128)(2,1)} %param.16) | copy-start | bytes 24580
  26.6 5.2 %collective-permute-start.2 = (bf16[128,256]{1,0:T(8,128)(2,1)S(1)}, bf16[128,256]{1,0:T(8,128)(2,1)S(1)}, u32[]{:S(2)}, u32[]{:S(2)}) collective-permute-start(bf16[128,256]{1,0:T(8,128)(2,1)S(1)} %fusion.10), channel_id=1, source_target_pairs={{0,96},{32,0},{64,32},{96,64},{1,97},{33,1},{65,33},{97,65},{2,98}... | collective-permute-start | bytes 196616 | tf_op jit(solution)/shard_map/ppermute | solution.py:21
  29.5 6.2 %collective-permute-start.1 = (bf16[128,256]{1,0:T(8,128)(2,1)S(1)}, bf16[128,256]{1,0:T(8,128)(2,1)S(1)}, u32[]{:S(2)}, u32[]{:S(2)}) collective-permute-start(bf16[128,256]{1,0:T(8,128)(2,1)S(1)} %fusion.10), channel_id=1, source_target_pairs={{0,32},{32,64},{64,96},{96,0},{1,33},{33,65},{65,97},{97,1},{2,34}... | collective-permute-start | bytes 196616 | tf_op jit(solution)/shard_map/ppermute | solution.py:21
  29.5 6.2 %collective-permute-start = (bf16[128,256]{1,0:T(8,128)(2,1)S(1)}, bf16[128,256]{1,0:T(8,128)(2,1)S(1)}, u32[]{:S(2)}, u32[]{:S(2)}) collective-permute-start(bf16[128,256]{1,0:T(8,128)(2,1)S(1)} %fusion.10), channel_id=1, source_target_pairs={{0,64},{32,96},{64,0},{96,32},{1,65},{33,97},{65,1},{97,33},{2,66}... | collective-permute-start | bytes 196616 | tf_op jit(solution)/shard_map/ppermute | solution.py:21
  56.5 4.4 %copy-start.1 = (bf16[16,128,256]{2,1,0:T(8,128)(2,1)}, bf16[16,128,256]{2,1,0:T(8,128)(2,1)S(1)}, u32[]{:S(2)}) copy-start(bf16[16,128,256]{2,1,0:T(8,128)(2,1)S(1)} %all_to_all.16.own) | copy-start | bytes 3145732
  56.5 2.8 %collective-permute-start.3 = (bf16[16,128,256]{2,1,0:T(8,128)(2,1)S(1)}, bf16[16,128,256]{2,1,0:T(8,128)(2,1)}, u32[]{:S(2)}, u32[]{:S(2)}) collective-permute-start(bf16[16,128,256]{2,1,0:T(8,128)(2,1)S(1)} %all_to_all.16.own), channel_id=1, source_target_pairs={{0,1},{1,0},{2,3},{3,2},{4,5},{5,4},{6,7},{7,6},{8,9},{9,8},{10,11... | collective-permute-start | bytes 3145736 | tf_op jit(solution)/shard_map/ppermute | solution.py:21
  78.2 3.0 %collective-permute-start.4 = (bf16[128,4096]{1,0:T(8,128)(2,1)}, bf16[128,4096]{1,0:T(8,128)(2,1)S(1)}, u32[]{:S(2)}, u32[]{:S(2)}) collective-permute-start(bf16[128,4096]{1,0:T(8,128)(2,1)} %get-tuple-element.8), channel_id=1, source_target_pairs={{0,1},{1,0},{2,3},{3,2},{4,5},{5,4},{6,7},{7,6},{8,9},{9,8},{10,11... | collective-permute-start | bytes 3145736 | tf_op jit(solution)/shard_map/ppermute | solution.py:21
  83.0 28.7 %copy-start.2 = (bf16[8,4096]{1,0:T(8,128)(2,1)S(1)}, bf16[8,4096]{1,0:T(8,128)(2,1)}, u32[]{:S(2)}) copy-start(bf16[8,4096]{1,0:T(8,128)(2,1)} %param.11) | copy-start | bytes 196612
  103.7 4.3 %collective-permute-start.7 = (bf16[8,4096]{1,0:T(8,128)(2,1)S(1)}, bf16[8,4096]{1,0:T(8,128)(2,1)S(1)}, u32[]{:S(2)}, u32[]{:S(2)}) collective-permute-start(bf16[8,4096]{1,0:T(8,128)(2,1)S(1)} %reduce_sum.22), channel_id=1, source_target_pairs={{0,96},{32,0},{64,32},{96,64},{1,97},{33,1},{65,33},{97,65},{2,98}... | collective-permute-start | bytes 196616 | tf_op jit(solution)/shard_map/ppermute | solution.py:21
  105.5 6.2 %collective-permute-start.6 = (bf16[8,4096]{1,0:T(8,128)(2,1)S(1)}, bf16[8,4096]{1,0:T(8,128)(2,1)S(1)}, u32[]{:S(2)}, u32[]{:S(2)}) collective-permute-start(bf16[8,4096]{1,0:T(8,128)(2,1)S(1)} %reduce_sum.22), channel_id=1, source_target_pairs={{0,32},{32,64},{64,96},{96,0},{1,33},{33,65},{65,97},{97,1},{2,34}... | collective-permute-start | bytes 196616 | tf_op jit(solution)/shard_map/ppermute | solution.py:21
  105.8 5.9 %collective-permute-start.5 = (bf16[8,4096]{1,0:T(8,128)(2,1)S(1)}, bf16[8,4096]{1,0:T(8,128)(2,1)S(1)}, u32[]{:S(2)}, u32[]{:S(2)}) collective-permute-start(bf16[8,4096]{1,0:T(8,128)(2,1)S(1)} %reduce_sum.22), channel_id=1, source_target_pairs={{0,64},{32,96},{64,0},{96,32},{1,65},{33,97},{65,1},{97,33},{2,66}... | collective-permute-start | bytes 196616 | tf_op jit(solution)/shard_map/ppermute | solution.py:21

commit v2 on v1

v2 whole, which is shorter than its diff:
```python
import math

import jax
import jax.numpy as jnp
from jax import lax
from jax.experimental import pallas as pl
from jax.experimental.pallas import tpu as pltpu
from jax.sharding import Mesh
from jax.sharding import PartitionSpec as P

SHARD = ("shard_0", "shard_1", "shard_2")
PLANE = ("shard_0", "shard_1")
F32 = jnp.float32
BF16 = jnp.bfloat16


def shifted(x, axis, by):
    size = lax.axis_size(axis)
    return lax.ppermute(x, axis, [(i, (i + by) % size) for i in range(size)])


def sum_over_groups(part, ready=()):
    others = tuple(shifted(part, "expert", by) for by in (1, 2, 3))
    (one, two, three), ready = lax.optimization_barrier((others, ready))
    total = (part.astype(F32) + two.astype(F32)) + (one.astype(F32) + three.astype(F32))
    return (total, ready) if ready else total


def expert_kernel(
    place, own, partner, ids, gain, router, attn, gate_hbm, up_hbm, down_hbm,
    send, keep, mixed, hidden_t, act, gate_up, down, sems,
):
    core, shard, first_expert, adds = place[0], place[1], place[2], place[3]
    units, width = down.shape
    half_units = units // 2
    block, tokens = own.shape[1:]
    half = tokens // 2
    parts = sems.shape[0] - 4
    step = width // parts

    def gate_up_copy(k, source, at):
        return pltpu.make_async_copy(
            source.at[pl.ds(at, half_units)], gate_up.at[k], sems.at[k]
        )

    def down_copy(n):
        columns = pl.ds(pl.multiple_of(n * step, step), step)
        return pltpu.make_async_copy(
            down_hbm.at[:, columns], down.at[:, columns], sems.at[4 + n]
        )

    for m in range(2):
        gate_up_copy(2 * m, gate_hbm, m * half_units).start()
        gate_up_copy(2 * m + 1, up_hbm, m * half_units).start()
    for n in range(parts):
        down_copy(n).start()

    def norm_block(j, squares):
        for mine, part in ((core, own), (1 - core, partner)):
            x = part[j]
            if part is partner:
                x = jnp.concatenate([x[:, half:], x[:, :half]], axis=1)
            rows = pl.ds(pl.multiple_of((2 * j + mine) * block, block), block)
            g = gain[rows, :]
            y = x.astype(F32)
            mixed[rows, :] = (y * jnp.concatenate([g, g], axis=1).astype(F32)).astype(BF16)
            squares = squares + (y * y).reshape(block // 8, 8, tokens).sum(axis=0)
        return squares

    squares = lax.fori_loop(0, own.shape[0], norm_block, jnp.zeros((8, tokens), F32))
    scale = lax.rsqrt(squares.sum(axis=0, keepdims=True) / width + 1e-05)
    logits = jnp.dot(router[...], mixed[...], preferred_element_type=F32) * scale
    numbers = lax.broadcasted_iota(jnp.int32, logits.shape, 0)
    named = ids[...]
    named = jnp.where(
        core == 0, named, jnp.concatenate([named[:, half:], named[:, :half]], axis=1)
    )
    first, second = named[0:1, :], named[1:2, :]
    a = jnp.where(numbers == first, logits, 0.0).sum(axis=0, keepdims=True)
    b = jnp.where(numbers == second, logits, 0.0).sum(axis=0, keepdims=True)
    weight_first = 1.0 / (1.0 + jnp.exp(b - a))
    weight_second = 1.0 / (1.0 + jnp.exp(a - b))

    def gate_up_part(k, carry):
        gate_up_copy(k, gate_hbm, 0).wait()
        hidden_t[k] = jnp.dot(gate_up[k], mixed[...], preferred_element_type=F32)
        return carry

    lax.fori_loop(0, 4, gate_up_part, 0)
    for m in range(2):
        expert = first_expert + m
        routed = jnp.where(first == expert, weight_first, 0.0) + jnp.where(
            second == expert, weight_second, 0.0
        )
        gated = hidden_t[2 * m] * scale
        upward = hidden_t[2 * m + 1] * scale
        value = gated / (1.0 + jnp.exp(-gated)) * upward * routed
        act[m] = value.T.astype(BF16)

    def down_part(n, carry):
        down_copy(n).wait()
        columns = pl.ds(pl.multiple_of(n * step, step), step)
        total = jnp.dot(
            act[0], down[pl.ds(0, half_units), columns], preferred_element_type=F32
        ) + jnp.dot(
            act[1], down[pl.ds(half_units, half_units), columns], preferred_element_type=F32
        )
        keep[:, columns] = total[:half].astype(BF16)
        send[:, columns] = total[half:].astype(BF16)
        return carry

    lax.fori_loop(0, parts, down_part, 0)
    rows = attn[...].astype(F32).T * adds.astype(F32)
    columns = pl.ds(pl.multiple_of(shard * block, block), block)
    keep[:, columns] = (keep[:, columns].astype(F32) + rows[:half]).astype(BF16)
    send[:, columns] = (send[:, columns].astype(F32) + rows[half:]).astype(BF16)


def experts(place, own, partner, ids, gain, router, attn, gate, up, down):
    units, width = down.shape
    tokens = own.shape[2]
    vmem = pl.BlockSpec(memory_space=pltpu.VMEM)
    hbm = pl.BlockSpec(memory_space=pl.ANY)
    half = jax.ShapeDtypeStruct((tokens // 2, width), BF16)
    return pl.pallas_call(
        expert_kernel,
        out_shape=(half, half),
        in_specs=[pl.BlockSpec(memory_space=pltpu.SMEM)] + [vmem] * 6 + [hbm] * 3,
        out_specs=(vmem, vmem),
        scratch_shapes=[
            pltpu.VMEM((width, tokens), BF16),
            pltpu.VMEM((4, units // 2, tokens), F32),
            pltpu.VMEM((2, tokens, units // 2), BF16),
            pltpu.VMEM((4, units // 2, width), BF16),
            pltpu.VMEM((units, width), BF16),
            pltpu.SemaphoreType.DMA((8,)),
        ],
        compiler_params=pltpu.CompilerParams(vmem_limit_bytes=48 * 1024 * 1024),
        cost_estimate=pl.CostEstimate(
            flops=6 * tokens * units * width,
            bytes_accessed=6 * units * width,
            transcendentals=2 * units * tokens,
        ),
        name="experts",
    )(place, own, partner, ids, gain, router, attn, gate, up, down)


def on_device(
    hidden, queries, key_cache, value_cache, out_weight, norm_gain, router,
    expert_ids, gate_weight, up_weight, down_weight,
):
    count_local, heads_local, head_size = queries.shape
    kv_local = key_cache.shape[2]
    width = hidden.shape[1]
    block = out_weight.shape[1]
    chips, cores = lax.axis_size(PLANE), lax.axis_size("shard_2")
    tokens = chips * cores * count_local
    core = lax.axis_index("shard_2")
    shard = lax.axis_index(PLANE) * cores + core
    group = lax.axis_index("expert")
    query_blocks = queries.reshape(count_local, kv_local, heads_local // kv_local, head_size)
    scores = jnp.einsum(
        "tkgd,tpkd->tkgp", query_blocks, key_cache, preferred_element_type=F32
    ) / math.sqrt(head_size)
    attn_weights = jax.nn.softmax(scores, axis=-1).astype(BF16)
    attended = jnp.einsum(
        "tkgp,tpkd->tkgd", attn_weights, value_cache, preferred_element_type=F32
    )
    heads = heads_local * head_size
    attended = attended.astype(BF16).reshape(count_local, heads)
    pieces = jnp.concatenate(
        [
            jnp.broadcast_to(attended[None], (chips, count_local, heads)),
            hidden.reshape(count_local, chips, cores * block).transpose(1, 0, 2),
        ],
        axis=-1,
    )
    arrived = lax.all_to_all(pieces, PLANE, 0, 0, tiled=True).reshape(tokens // 2, -1)
    passed = shifted(arrived, "shard_2", 1)

    def project(rows):
        return lax.dot_general(
            out_weight, rows[:, :heads], (((0,), (1,)), ((), ())), preferred_element_type=F32
        ).astype(BF16)

    def my_columns(rows):
        return jnp.where(core == 0, rows[:, heads : heads + block], rows[:, heads + block :])

    part = jnp.concatenate([project(arrived), project(passed)], axis=1)
    hidden_t = jnp.concatenate([my_columns(arrived), my_columns(passed)], axis=0).T
    local = gate_weight.shape[0]
    place = jnp.stack([core, shard, group * local, (group == 0).astype(jnp.int32)]).astype(jnp.int32)
    ids = expert_ids.reshape(chips, cores, count_local, 2).transpose(3, 1, 0, 2).reshape(2, tokens)
    gain = jnp.broadcast_to(norm_gain[:, None], (width, 128))
    attn_out, (place, ids, gain, hidden_t) = sum_over_groups(part, (place, ids, gain, hidden_t))
    stream = (attn_out + hidden_t.astype(F32)).astype(BF16)
    own = lax.all_to_all(
        jnp.broadcast_to(stream[None], (chips, block, tokens)), PLANE, 0, 0, tiled=True
    )
    units = local * gate_weight.shape[2]
    partner = shifted(own, "shard_2", 1)
    send, keep = experts(
        place,
        own,
        partner,
        ids,
        gain,
        router.T,
        attn_out.astype(BF16),
        gate_weight.transpose(0, 2, 1).reshape(units, width),
        up_weight.transpose(0, 2, 1).reshape(units, width),
        down_weight.reshape(units, width),
    )
    pair = (keep.astype(F32) + shifted(send, "shard_2", 1).astype(F32)).astype(BF16)
    parts = lax.all_to_all(pair.reshape(chips, count_local, width), PLANE, 0, 0, tiled=True)
    reduced = parts.astype(F32).sum(axis=0).astype(BF16)
    return (hidden.astype(F32) + sum_over_groups(reduced)).astype(BF16)


def solution(mesh):
    split = Mesh(
        mesh.devices.reshape(mesh.shape["expert"], 4, 4, 2),
        ("expert", "shard_0", "shard_1", "shard_2"),
    )
    in_specs = (
        P(SHARD, None),
        P(SHARD, "expert", None),
        P(SHARD, None, "expert", None),
        P(SHARD, None, "expert", None),
        P("expert", SHARD),
        P(),
        P(),
        P(),
        P("expert", None, SHARD),
        P("expert", None, SHARD),
        P("expert", SHARD, None),
    )
    return jax.shard_map(
        on_device, mesh=split, in_specs=in_specs, out_specs=P(SHARD, None), check_vma=False
    )
```

time: 113 us -> 101 us (0.89)
  blocking collectives: 61.5 us -> 40.1 us
  waiting for transfers between devices: 12.4 us -> 25.2 us
  starting transfers between devices: 8.68 us -> 15.5 us
  Pallas kernels: 17.3 us -> 10.6 us
  other arithmetic: 4.24 us -> 2.21 us
  local copies, waits for them, and re-layouts: 4.41 us -> 2.75 us
    all_to_all x1 -> x0, blocking collectives: 20.9 us -> none  [on_device(): lax.all_to_all(pieces, CORE_MAJOR, 0, 0, tiled=True).reshape(tokens, -1)]
    all_to_all x0 -> x1, waiting for transfers between devices: none -> 9.06 us  [on_device(): lax.all_to_all(pieces, PLANE, 0, 0, tiled=True).reshape(tokens // 2, -1)]
    all_to_all x0 -> x1, starting transfers between devices: none -> 8.16 us  [on_device(): lax.all_to_all(pieces, PLANE, 0, 0, tiled=True).reshape(tokens // 2, -1)]
    pallas_call x1, Pallas kernels: 17.3 us -> 10.6 us  [experts(): pl.pallas_call(expert_kernel, out_shape=(half, half), in_specs=[pl.BlockS...]
    ppermute x8 -> x9, waiting for transfers between devices: 12.4 us -> 16.1 us  [shifted(): return lax.ppermute(x, axis, [(i, (i + by) % size) for i in range(size)])]
    reshape x1, other arithmetic: 1.79 us -> 0.25 us  [on_device(): pair.reshape(chips, count_local, width)]
    ppermute x8 -> x9, starting transfers between devices: 8.68 us -> 7.32 us  [shifted(): return lax.ppermute(x, axis, [(i, (i + by) % size) for i in range(size)])]
  transfers between devices with their start and end apart: 8 -> 10, of which waited for: 5 -> 10; matrix products, arithmetic and copies ran while one was open for 1% -> 1% of each run, Pallas kernels for 0% -> 0%
where the time goes in v2:
time: 101 us; the launch traced here: 100 us
  blocking collectives  40.1 us (40%)
  waiting for transfers between devices  25.2 us (25%)
  starting transfers between devices  15.5 us (15%)
  Pallas kernels  10.6 us (10%)
  matrix products  3.97 us (4%)
  local copies, waits for them, and re-layouts  2.75 us (3%)
  other arithmetic  2.21 us (2%)
    all_to_all x1, blocking collectives, on_device(): lax.all_to_all(pair.reshape(chips, count_local, width), PLANE, 0, 0, tile...  20.4 us
    all_to_all x1, blocking collectives, on_device(): lax.all_to_all(jnp.broadcast_to(stream[None], (chips, block, tokens)), PL...  19.7 us
    ppermute x9, waiting for transfers between devices, shifted(): return lax.ppermute(x, axis, [(i, (i + by) % size) for i in range(size)])  16.1 us
    pallas_call x1, Pallas kernels, experts(): pl.pallas_call(expert_kernel, out_shape=(half, half), in_specs=[pl.BlockS...  10.6 us
    all_to_all x1, waiting for transfers between devices, on_device(): lax.all_to_all(pieces, PLANE, 0, 0, tiled=True).reshape(tokens // 2, -1)  9.06 us
    all_to_all x1, starting transfers between devices, on_device(): lax.all_to_all(pieces, PLANE, 0, 0, tiled=True).reshape(tokens // 2, -1)  8.16 us
    ppermute x9, starting transfers between devices, shifted(): return lax.ppermute(x, axis, [(i, (i + by) % size) for i in range(size)])  7.32 us
    dot_general x1, matrix products, on_device(): jnp.einsum('tkgp,tpkd->tkgd', attn_weights, value_cache, preferred_elemen...  2.06 us
  transfers between devices with their start and end apart: 10, of which 10 were waited for; matrix products, arithmetic and copies ran while one was open for 1% of the time, Pallas kernels for 0%

profile of v2, /device:TPU:0, one launch (start us, length us, event | category | flops | bytes accessed | tf_op | source)
XLA Modules:
  0.0 100.5 jit_solution(12356156125400513693)
XLA Ops:
  0.0 1.6 %copy-done = bf16[8,512,2,128]{3,2,1,0:T(2,128)(2,1)S(1)} copy-done((bf16[8,512,2,128]{3,2,1,0:T(2,128)(2,1)S(1)}, bf16[8,512,2,128]{3,2,1,0:T(2,128)(2,1)}, u32[]{:S(2)}) %copy-start) | copy-done | bytes 2097176
  1.6 1.4 %fusion.7 = f32[8,2,4,512]{3,2,1,0:T(4,128)S(1)} fusion(bf16[8,2,4,128]{3,2,1,0:T(4,128)(2,1)} %bitcast.43, bf16[8,512,2,128]{3,2,1,0:T(2,128)(2,1)S(1)} %copy-done), kind=kOutput, calls=%fused_computation.8 | convolution fusion | flops 8421376 | bytes 2244608 | tf_op jit(solution)/shard_map/tkgd,tpkd->tkgp/dot_general | solution.py:162
  3.0 0.2 fusion.20
  3.2 2.1 %fusion.12 = bf16[8,2,4,128]{3,2,1,0:T(4,128)(2,1)S(1)} fusion(bf16[8,512,2,128]{3,2,1,0:T(2,128)(2,1)} %param.14, f32[8,2,4]{2,1,0:T(2,128)S(1)} %fusion.20, f32[8,2,4,512]{3,2,1,0:T(4,128)S(1)} %fusion.7), kind=kOutput, calls=%fused_computation.13 | convolution fusion | flops 8495679 | bytes 2244864 | tf_op jit(solution)/shard_map/tkgp,tpkd->tkgd/dot_general | solution.py:166
  5.3 0.7 pad_maximum_fusion
  6.1 8.2 %all-to-all-start = ((bf16[16,8,1280]{2,1,0:T(8,128)(2,1)}), bf16[16,8,1280]{2,1,0:T(8,128)(2,1)S(1)}, u32[]{:S(2)}, u32[]{:S(2)}) async-start(bf16[16,8,1280]{2,1,0:T(8,128)(2,1)} %pad_maximum_fusion), calls=%async_computation | async-start | bytes 655360 | tf_op jit(solution)/shard_map/all_to_all | solution.py:178
  14.6 9.1 %all-to-all-done = bf16[16,8,1280]{2,1,0:T(8,128)(2,1)S(1)} async-done(((bf16[16,8,1280]{2,1,0:T(8,128)(2,1)}), bf16[16,8,1280]{2,1,0:T(8,128)(2,1)S(1)}, u32[]{:S(2)}, u32[]{:S(2)}) %all-to-all-start) | async-done | bytes 327712 | tf_op jit(solution)/shard_map/all_to_all | solution.py:178
  23.6 0.2 copy.22
  23.9 0.3 fusion.10
  24.2 1.3 %collective-permute-done = bf16[128,1280]{0,1:T(8,128)(2,1)S(1)} collective-permute-done((bf16[128,1280]{0,1:T(8,128)(2,1)S(1)}, bf16[128,1280]{0,1:T(8,128)(2,1)S(1)}, u32[]{:S(2)}, u32[]{:S(2)}) %collective-permute-start) | collective-permute-done | bytes 327712 | tf_op jit(solution)/shard_map/ppermute | solution.py:19
  25.5 0.3 fusion.11
  25.8 2.8 %collective-permute-start.3 = (bf16[128,256]{1,0:T(8,128)(2,1)S(1)}, bf16[128,256]{1,0:T(8,128)(2,1)S(1)}, u32[]{:S(2)}, u32[]{:S(2)}) collective-permute-start(bf16[128,256]{1,0:T(8,128)(2,1)S(1)} %pad_maximum_fusion.1), channel_id=1, source_target_pairs={{0,96},{32,0},{64,32},{96,64},{1,97},{33,1},{65,33},{97,65},{2,98}... | collective-permute-start | bytes 196616 | tf_op jit(solution)/shard_map/ppermute | solution.py:19
  28.7 0.8 collective-permute-start.2
  29.5 0.9 collective-permute-start.1
  30.4 1.5 %collective-permute-done.3 = bf16[128,256]{1,0:T(8,128)(2,1)S(1)} collective-permute-done((bf16[128,256]{1,0:T(8,128)(2,1)S(1)}, bf16[128,256]{1,0:T(8,128)(2,1)S(1)}, u32[]{:S(2)}, u32[]{:S(2)}) %collective-permute-start.3) | collective-permute-done | bytes 65568 | tf_op jit(solution)/shard_map/ppermute | solution.py:19
  31.9 2.8 %collective-permute-done.2 = bf16[128,256]{1,0:T(8,128)(2,1)S(1)} collective-permute-done((bf16[128,256]{1,0:T(8,128)(2,1)S(1)}, bf16[128,256]{1,0:T(8,128)(2,1)S(1)}, u32[]{:S(2)}, u32[]{:S(2)}) %collective-permute-start.2) | collective-permute-done | bytes 65568 | tf_op jit(solution)/shard_map/ppermute | solution.py:19
  34.7 0.7 collective-permute-done.1
  35.4 0.6 broadcast_in_dim.10.gain
  36.2 19.7 %all_to_all.15.own = bf16[16,128,256]{2,1,0:T(8,128)(2,1)S(1)} all-to-all(bf16[16,128,256]{2,1,0:T(8,128)(2,1)S(1)} %broadcast_in_dim.11), channel_id=1, replica_groups=mesh['expert'=4,'shard_0'=4,'shard_1'=4,'shard_2'=2] {'shard_0','shard_1'}, dimensions={0} | all-to-all | bytes 2097152 | tf_op jit(solution)/shard_map/all_to_all | solution.py:197
  55.9 2.7 %collective-permute-done.4.partner = bf16[16,128,256]{2,1,0:T(8,128)(2,1)S(1)} collective-permute-done((bf16[16,128,256]{2,1,0:T(8,128)(2,1)S(1)}, bf16[16,128,256]{2,1,0:T(8,128)(2,1)S(1)}, u32[]{:S(2)}, u32[]{:S(2)}) %collective-permute-start.4) | collective-permute-done | bytes 1048608 | tf_op jit(solution)/shard_map/ppermute | solution.py:19
  58.6 10.6 %experts.1 = (bf16[128,4096]{1,0:T(8,128)(2,1)S(1)}, bf16[128,4096]{1,0:T(8,128)(2,1)S(1)}) custom-call(s32[4]{0:T(128)S(1)} %pad_add_fusion.place, bf16[16,128,256]{2,1,0:T(8,128)(2,1)S(1)} %all_to_all.15.own, bf16[16,128,256]{2,1,0:T(8,128)(2,1)S(1)} %collective-permute-done.4.partner, s32[2,256]{1,0:T(2,128)S(1)} %reshape.36.ids, ...), custom_call_target="tpu_custom_call" | custom-call | flops 5637144576 | bytes 22020096 | tf_op jit(solution)/shard_map/experts/pallas_call | solution.py:125
  69.2 0.2 collective-permute-start.5
  69.4 2.5 %collective-permute-done.5 = bf16[128,4096]{1,0:T(8,128)(2,1)S(1)} collective-permute-done((bf16[128,4096]{1,0:T(8,128)(2,1)S(1)}, bf16[128,4096]{1,0:T(8,128)(2,1)S(1)}, u32[]{:S(2)}, u32[]{:S(2)}) %collective-permute-start.5) | collective-permute-done | bytes 1048608 | tf_op jit(solution)/shard_map/ppermute | solution.py:19
  71.9 0.2 fusion.15
  72.2 20.4 %all_to_all.16 = bf16[16,8,4096]{2,1,0:T(8,128)(2,1)S(1)} all-to-all(bf16[16,8,4096]{2,1,0:T(8,128)(2,1)S(1)} %fusion.15), channel_id=1, replica_groups=mesh['expert'=4,'shard_0'=4,'shard_1'=4,'shard_2'=2] {'shard_0','shard_1'}, dimensions={0} | all-to-all | bytes 2097152 | tf_op jit(solution)/shard_map/all_to_all | solution.py:215
  92.7 0.2 collective-permute-start.8
  92.9 1.0 collective-permute-start.7
  93.9 1.3 %collective-permute-start.6 = (bf16[8,4096]{1,0:T(8,128)(2,1)S(1)}, bf16[8,4096]{1,0:T(8,128)(2,1)S(1)}, u32[]{:S(2)}, u32[]{:S(2)}) collective-permute-start(bf16[8,4096]{1,0:T(8,128)(2,1)S(1)} %reduce_sum.22), channel_id=1, source_target_pairs={{0,32},{32,64},{64,96},{96,0},{1,33},{33,65},{65,97},{97,1},{2,34}... | collective-permute-start | bytes 196616 | tf_op jit(solution)/shard_map/ppermute | solution.py:19
  95.2 1.8 %collective-permute-done.8 = bf16[8,4096]{1,0:T(8,128)(2,1)S(1)} collective-permute-done((bf16[8,4096]{1,0:T(8,128)(2,1)S(1)}, bf16[8,4096]{1,0:T(8,128)(2,1)S(1)}, u32[]{:S(2)}, u32[]{:S(2)}) %collective-permute-start.8) | collective-permute-done | bytes 65568 | tf_op jit(solution)/shard_map/ppermute | solution.py:19
  97.1 2.1 %collective-permute-done.7 = bf16[8,4096]{1,0:T(8,128)(2,1)S(1)} collective-permute-done((bf16[8,4096]{1,0:T(8,128)(2,1)S(1)}, bf16[8,4096]{1,0:T(8,128)(2,1)S(1)}, u32[]{:S(2)}, u32[]{:S(2)}) %collective-permute-start.7) | collective-permute-done | bytes 65568 | tf_op jit(solution)/shard_map/ppermute | solution.py:19
  99.1 0.7 collective-permute-done.6
  99.8 0.7 add_convert_fusion.1
  (26 shorter events, 0.8 us)
Async XLA Ops:
  0.0 1.6 %copy-start = (bf16[8,512,2,128]{3,2,1,0:T(2,128)(2,1)S(1)}, bf16[8,512,2,128]{3,2,1,0:T(2,128)(2,1)}, u32[]{:S(2)}) copy-start(bf16[8,512,2,128]{3,2,1,0:T(2,128)(2,1)} %param.13) | copy-start | bytes 6291460
  3.0 2.4 %copy-start.3 = (bf16[8,4096]{1,0:T(8,128)(2,1)S(1)}, bf16[8,4096]{1,0:T(8,128)(2,1)}, u32[]{:S(2)}) copy-start(bf16[8,4096]{1,0:T(8,128)(2,1)} %param.11) | copy-start | bytes 196612
  3.2 11.1 %copy-start.5 = (s32[256,2]{0,1:T(2,128)S(1)}, s32[256,2]{0,1:T(2,128)}, u32[]{:S(2)}) copy-start(s32[256,2]{0,1:T(2,128)} %param.18) | copy-start | bytes 6148
  5.2 18.7 %copy-start.2 = (bf16[1024,128]{1,0:T(8,128)(2,1)S(1)}, bf16[1024,128]{1,0:T(8,128)(2,1)}, u32[]{:S(2)}) copy-start(bf16[1024,128]{1,0:T(8,128)(2,1)} %param.15) | copy-start | bytes 786436
  5.3 30.2 %copy-start.4 = (bf16[4096]{0:T(1024)(128)(2,1)S(1)}, bf16[4096]{0:T(1024)(128)(2,1)}, u32[]{:S(2)}) copy-start(bf16[4096]{0:T(1024)(128)(2,1)} %param.16) | copy-start | bytes 24580
  6.1 17.6 %all-to-all-start = ((bf16[16,8,1280]{2,1,0:T(8,128)(2,1)}), bf16[16,8,1280]{2,1,0:T(8,128)(2,1)S(1)}, u32[]{:S(2)}, u32[]{:S(2)}) async-start(bf16[16,8,1280]{2,1,0:T(8,128)(2,1)} %pad_maximum_fusion), calls=%async_computation | async-start | bytes 655360 | tf_op jit(solution)/shard_map/all_to_all | solution.py:178
  23.8 1.7 %collective-permute-start = (bf16[128,1280]{0,1:T(8,128)(2,1)S(1)}, bf16[128,1280]{0,1:T(8,128)(2,1)S(1)}, u32[]{:S(2)}, u32[]{:S(2)}) collective-permute-start(bf16[128,1280]{0,1:T(8,128)(2,1)S(1)} %copy.22), channel_id=1, source_target_pairs={{0,1},{1,0},{2,3},{3,2},{4,5},{5,4},{6,7},{7,6},{8,9},{9,8},{10,11... | collective-permute-start | bytes 983048 | tf_op jit(solution)/shard_map/ppermute | solution.py:19
  25.8 6.0 %collective-permute-start.3 = (bf16[128,256]{1,0:T(8,128)(2,1)S(1)}, bf16[128,256]{1,0:T(8,128)(2,1)S(1)}, u32[]{:S(2)}, u32[]{:S(2)}) collective-permute-start(bf16[128,256]{1,0:T(8,128)(2,1)S(1)} %pad_maximum_fusion.1), channel_id=1, source_target_pairs={{0,96},{32,0},{64,32},{96,64},{1,97},{33,1},{65,33},{97,65},{2,98}... | collective-permute-start | bytes 196616 | tf_op jit(solution)/shard_map/ppermute | solution.py:19
  28.7 6.1 %collective-permute-start.2 = (bf16[128,256]{1,0:T(8,128)(2,1)S(1)}, bf16[128,256]{1,0:T(8,128)(2,1)S(1)}, u32[]{:S(2)}, u32[]{:S(2)}) collective-permute-start(bf16[128,256]{1,0:T(8,128)(2,1)S(1)} %pad_maximum_fusion.1), channel_id=1, source_target_pairs={{0,64},{32,96},{64,0},{96,32},{1,65},{33,97},{65,1},{97,33},{2,66}... | collective-permute-start | bytes 196616 | tf_op jit(solution)/shard_map/ppermute | solution.py:19
  29.5 6.0 %collective-permute-start.1 = (bf16[128,256]{1,0:T(8,128)(2,1)S(1)}, bf16[128,256]{1,0:T(8,128)(2,1)S(1)}, u32[]{:S(2)}, u32[]{:S(2)}) collective-permute-start(bf16[128,256]{1,0:T(8,128)(2,1)S(1)} %pad_maximum_fusion.1), channel_id=1, source_target_pairs={{0,32},{32,64},{64,96},{96,0},{1,33},{33,65},{65,97},{97,1},{2,34}... | collective-permute-start | bytes 196616 | tf_op jit(solution)/shard_map/ppermute | solution.py:19
  36.1 22.5 %copy-start.1 = (bf16[4096,8]{0,1:T(8,128)(2,1)S(1)}, bf16[4096,8]{0,1:T(8,128)(2,1)}, u32[]{:S(2)}) copy-start(bf16[4096,8]{0,1:T(8,128)(2,1)} %param.17) | copy-start | bytes 196612
  55.9 2.7 %collective-permute-start.4 = (bf16[16,128,256]{2,1,0:T(8,128)(2,1)S(1)}, bf16[16,128,256]{2,1,0:T(8,128)(2,1)S(1)}, u32[]{:S(2)}, u32[]{:S(2)}) collective-permute-start(bf16[16,128,256]{2,1,0:T(8,128)(2,1)S(1)} %all_to_all.15.own), channel_id=1, source_target_pairs={{0,1},{1,0},{2,3},{3,2},{4,5},{5,4},{6,7},{7,6},{8,9},{9,8},{10,11... | collective-permute-start | bytes 3145736 | tf_op jit(solution)/shard_map/ppermute | solution.py:19
  69.2 2.7 %collective-permute-start.5 = (bf16[128,4096]{1,0:T(8,128)(2,1)S(1)}, bf16[128,4096]{1,0:T(8,128)(2,1)S(1)}, u32[]{:S(2)}, u32[]{:S(2)}) collective-permute-start(bf16[128,4096]{1,0:T(8,128)(2,1)S(1)} %get-tuple-element.25), channel_id=1, source_target_pairs={{0,1},{1,0},{2,3},{3,2},{4,5},{5,4},{6,7},{7,6},{8,9},{9,8},{10,11... | collective-permute-start | bytes 3145736 | tf_op jit(solution)/shard_map/ppermute | solution.py:19
  92.7 4.3 %collective-permute-start.8 = (bf16[8,4096]{1,0:T(8,128)(2,1)S(1)}, bf16[8,4096]{1,0:T(8,128)(2,1)S(1)}, u32[]{:S(2)}, u32[]{:S(2)}) collective-permute-start(bf16[8,4096]{1,0:T(8,128)(2,1)S(1)} %reduce_sum.22), channel_id=1, source_target_pairs={{0,96},{32,0},{64,32},{96,64},{1,97},{33,1},{65,33},{97,65},{2,98}... | collective-permute-start | bytes 196616 | tf_op jit(solution)/shard_map/ppermute | solution.py:19
  92.9 6.2 %collective-permute-start.7 = (bf16[8,4096]{1,0:T(8,128)(2,1)S(1)}, bf16[8,4096]{1,0:T(8,128)(2,1)S(1)}, u32[]{:S(2)}, u32[]{:S(2)}) collective-permute-start(bf16[8,4096]{1,0:T(8,128)(2,1)S(1)} %reduce_sum.22), channel_id=1, source_target_pairs={{0,64},{32,96},{64,0},{96,32},{1,65},{33,97},{65,1},{97,33},{2,66}... | collective-permute-start | bytes 196616 | tf_op jit(solution)/shard_map/ppermute | solution.py:19
  93.9 5.9 %collective-permute-start.6 = (bf16[8,4096]{1,0:T(8,128)(2,1)S(1)}, bf16[8,4096]{1,0:T(8,128)(2,1)S(1)}, u32[]{:S(2)}, u32[]{:S(2)}) collective-permute-start(bf16[8,4096]{1,0:T(8,128)(2,1)S(1)} %reduce_sum.22), channel_id=1, source_target_pairs={{0,32},{32,64},{64,96},{96,0},{1,33},{33,65},{65,97},{97,1},{2,34}... | collective-permute-start | bytes 196616 | tf_op jit(solution)/shard_map/ppermute | solution.py:19

commit v3 on v2

v3 whole, which is shorter than its diff:
```python
import math

import jax
import jax.numpy as jnp
from jax import lax
from jax.experimental import pallas as pl
from jax.experimental.pallas import tpu as pltpu
from jax.sharding import Mesh
from jax.sharding import PartitionSpec as P

SHARD = ("shard_0", "shard_1", "shard_2")
PLANE = ("shard_0", "shard_1")
F32 = jnp.float32
BF16 = jnp.bfloat16


def shifted(x, axis, by):
    size = lax.axis_size(axis)
    return lax.ppermute(x, axis, [(i, (i + by) % size) for i in range(size)])


def sum_over_groups(part, ready=()):
    others = tuple(shifted(part, "expert", by) for by in (1, 2, 3))
    (one, two, three), ready = lax.optimization_barrier((others, ready))
    total = (part.astype(F32) + two.astype(F32)) + (one.astype(F32) + three.astype(F32))
    return (total, ready) if ready else total


def bring_kernel(_, gate, up, down, held, sems):
    units = gate.shape[0]
    copies = [
        pltpu.make_async_copy(source, held.at[pl.ds(n * units, units)], sems.at[n])
        for n, source in enumerate((gate, up, down))
    ]
    for copy in copies:
        copy.start()
    for copy in copies:
        copy.wait()


def brought_in(after, *weights):
    size = sum(w.size for w in weights)
    rows, width = weights[0].shape
    return pl.pallas_call(
        bring_kernel,
        out_shape=pltpu.VMEM((3 * rows, width), BF16),
        in_specs=[pl.BlockSpec(memory_space=pl.ANY)] * 4,
        out_specs=pl.BlockSpec(memory_space=pltpu.VMEM),
        scratch_shapes=[pltpu.SemaphoreType.DMA((3,))],
        compiler_params=pltpu.CompilerParams(vmem_limit_bytes=36 * 1024 * 1024),
        cost_estimate=pl.CostEstimate(flops=80 * size, bytes_accessed=4 * size, transcendentals=0),
        name="bring",
    )(after, *weights)


def expert_kernel(place, ids, gain, router, attn, held, *refs):
    streams, (send, keep, mixed, hidden_t, act) = refs[:-5], refs[-5:]
    core, far, near, first_expert, adds = (place[n] for n in range(5))
    units, width = held.shape[0] // 3, held.shape[1]
    half_units = units // 2
    spread, block, tokens = streams[0].shape
    half = tokens // 2
    step = width // 4

    squares = jnp.zeros((8, tokens), F32)
    for n, part in enumerate(streams):
        by, is_partner = n // 2, n % 2
        here = (far - by) & (spread - 1)

        def norm_block(r, squares):
            x = part[r]
            if is_partner:
                x = jnp.concatenate([x[:, half:], x[:, :half]], axis=1)
            chip = here * spread + ((near - r) & (spread - 1))
            shard = 2 * chip + (1 - core if is_partner else core)
            rows = pl.ds(pl.multiple_of(shard * block, block), block)
            g = gain[rows, :]
            y = x.astype(F32)
            mixed[rows, :] = (y * jnp.concatenate([g, g], axis=1).astype(F32)).astype(BF16)
            return squares + (y * y).reshape(block // 8, 8, tokens).sum(axis=0)

        squares = lax.fori_loop(0, spread, norm_block, squares)
    scale = lax.rsqrt(squares.sum(axis=0, keepdims=True) / width + 1e-05)
    logits = jnp.dot(router[...], mixed[...], preferred_element_type=F32) * scale
    numbers = lax.broadcasted_iota(jnp.int32, logits.shape, 0)
    named = ids[...]
    named = jnp.where(
        core == 0, named, jnp.concatenate([named[:, half:], named[:, :half]], axis=1)
    )
    first, second = named[0:1, :], named[1:2, :]
    a = jnp.where(numbers == first, logits, 0.0).sum(axis=0, keepdims=True)
    b = jnp.where(numbers == second, logits, 0.0).sum(axis=0, keepdims=True)
    weight_first = 1.0 / (1.0 + jnp.exp(b - a))
    weight_second = 1.0 / (1.0 + jnp.exp(a - b))

    def expert_part(m, carry):
        for n in range(2):
            rows = pl.ds(pl.multiple_of((2 * n + m) * half_units, half_units), half_units)
            hidden_t[n] = jnp.dot(held[rows, :], mixed[...], preferred_element_type=F32)
        expert = first_expert + m
        routed = jnp.where(first == expert, weight_first, 0.0) + jnp.where(
            second == expert, weight_second, 0.0
        )
        gated = hidden_t[0] * scale
        upward = hidden_t[1] * scale
        value = gated / (1.0 + jnp.exp(-gated)) * upward * routed
        act[m] = value.T.astype(BF16)
        return carry

    lax.fori_loop(0, 2, expert_part, 0)

    def down_part(n, carry):
        columns = pl.ds(pl.multiple_of(n * step, step), step)
        total = jnp.dot(
            act[0], held[pl.ds(2 * units, half_units), columns], preferred_element_type=F32
        ) + jnp.dot(
            act[1], held[pl.ds(2 * units + half_units, half_units), columns], preferred_element_type=F32
        )
        keep[:, columns] = total[:half].astype(BF16)
        send[:, columns] = total[half:].astype(BF16)
        return carry

    lax.fori_loop(0, width // step, down_part, 0)
    rows = attn[...].astype(F32).T * adds.astype(F32)
    shard = 2 * (far * spread + near) + core
    columns = pl.ds(pl.multiple_of(shard * block, block), block)
    keep[:, columns] = (keep[:, columns].astype(F32) + rows[:half]).astype(BF16)
    send[:, columns] = (send[:, columns].astype(F32) + rows[half:]).astype(BF16)


def experts(place, ids, gain, router, attn, held, *streams):
    units, width = held.shape[0] // 3, held.shape[1]
    tokens = attn.shape[1]
    vmem = pl.BlockSpec(memory_space=pltpu.VMEM)
    half = jax.ShapeDtypeStruct((tokens // 2, width), BF16)
    return pl.pallas_call(
        expert_kernel,
        out_shape=(half, half),
        in_specs=[pl.BlockSpec(memory_space=pltpu.SMEM)] + [vmem] * (5 + len(streams)),
        out_specs=(vmem, vmem),
        scratch_shapes=[
            pltpu.VMEM((width, tokens), BF16),
            pltpu.VMEM((2, units // 2, tokens), F32),
            pltpu.VMEM((2, tokens, units // 2), BF16),
        ],
        compiler_params=pltpu.CompilerParams(vmem_limit_bytes=12 * 1024 * 1024),
        cost_estimate=pl.CostEstimate(
            flops=6 * tokens * units * width,
            bytes_accessed=6 * units * width,
            transcendentals=2 * units * tokens,
        ),
        name="experts",
    )(place, ids, gain, router, attn, held, *streams)


def on_device(
    hidden, queries, key_cache, value_cache, out_weight, norm_gain, router,
    expert_ids, gate_weight, up_weight, down_weight,
):
    count_local, heads_local, head_size = queries.shape
    kv_local = key_cache.shape[2]
    width = hidden.shape[1]
    block = out_weight.shape[1]
    chips, cores = lax.axis_size(PLANE), lax.axis_size("shard_2")
    tokens = chips * cores * count_local
    core = lax.axis_index("shard_2")
    group = lax.axis_index("expert")
    query_blocks = queries.reshape(count_local, kv_local, heads_local // kv_local, head_size)
    scores = jnp.einsum(
        "tkgd,tpkd->tkgp", query_blocks, key_cache, preferred_element_type=F32
    ) / math.sqrt(head_size)
    attn_weights = jax.nn.softmax(scores, axis=-1).astype(BF16)
    attended = jnp.einsum(
        "tkgp,tpkd->tkgd", attn_weights, value_cache, preferred_element_type=F32
    )
    heads = heads_local * head_size
    attended = attended.astype(BF16).reshape(count_local, heads)
    pieces = jnp.concatenate(
        [
            jnp.broadcast_to(attended[None], (chips, count_local, heads)),
            hidden.reshape(count_local, chips, cores * block).transpose(1, 0, 2),
        ],
        axis=-1,
    )
    arrived = lax.all_to_all(pieces, PLANE, 0, 0, tiled=True).reshape(tokens // 2, -1)
    passed = shifted(arrived, "shard_2", 1)

    def project(rows):
        return lax.dot_general(
            out_weight, rows[:, :heads], (((0,), (1,)), ((), ())), preferred_element_type=F32
        ).astype(BF16)

    def my_columns(rows):
        return jnp.where(core == 0, rows[:, heads : heads + block], rows[:, heads + block :])

    part = jnp.concatenate([project(arrived), project(passed)], axis=1)
    hidden_t = jnp.concatenate([my_columns(arrived), my_columns(passed)], axis=0).T
    local = gate_weight.shape[0]
    place = jnp.stack(
        [
            core,
            lax.axis_index("shard_0"),
            lax.axis_index("shard_1"),
            group * local,
            (group == 0).astype(jnp.int32),
        ]
    ).astype(jnp.int32)
    ids = expert_ids.reshape(chips, cores, count_local, 2).transpose(3, 1, 0, 2).reshape(2, tokens)
    gain = jnp.broadcast_to(norm_gain[:, None], (width, 128))
    attn_out, (place, ids, gain, hidden_t) = sum_over_groups(part, (place, ids, gain, hidden_t))
    stream = (attn_out + hidden_t.astype(F32)).astype(BF16)
    row = [stream] + [shifted(stream, "shard_1", by) for by in (1, 2, 3)]
    line = jnp.stack(row)
    plane = [line] + [shifted(line, "shard_0", by) for by in (1, 2, 3)]
    units = local * gate_weight.shape[2]
    held = brought_in(
        row[-1],
        gate_weight.transpose(0, 2, 1).reshape(units, width),
        up_weight.transpose(0, 2, 1).reshape(units, width),
        down_weight.reshape(units, width),
    )
    plane, held = lax.optimization_barrier((plane, held))
    streams = [x for part in plane for x in (part, shifted(part, "shard_2", 1))]
    send, keep = experts(
        place, ids, gain, router.T, attn_out.astype(BF16), held, *streams
    )
    pair = (keep.astype(F32) + shifted(send, "shard_2", 1).astype(F32)).astype(BF16)
    parts = lax.all_to_all(pair.reshape(chips, count_local, width), PLANE, 0, 0, tiled=True)
    reduced = parts.astype(F32).sum(axis=0).astype(BF16)
    return (hidden.astype(F32) + sum_over_groups(reduced)).astype(BF16)


def solution(mesh):
    split = Mesh(
        mesh.devices.reshape(mesh.shape["expert"], 4, 4, 2),
        ("expert", "shard_0", "shard_1", "shard_2"),
    )
    in_specs = (
        P(SHARD, None),
        P(SHARD, "expert", None),
        P(SHARD, None, "expert", None),
        P(SHARD, None, "expert", None),
        P("expert", SHARD),
        P(),
        P(),
        P(),
        P("expert", None, SHARD),
        P("expert", None, SHARD),
        P("expert", SHARD, None),
    )
    return jax.shard_map(
        on_device, mesh=split, in_specs=in_specs, out_specs=P(SHARD, None), check_vma=False
    )
```

time: 101 us -> 102 us (level)
  blocking collectives: 40.1 us -> 20.4 us
  waiting for transfers between devices: 25.2 us -> 34.2 us
  starting transfers between devices: 15.5 us -> 21.5 us
  Pallas kernels: 10.6 us -> 16.3 us
    all_to_all x1 -> x0, blocking collectives: 19.7 us -> none  [on_device(): lax.all_to_all(jnp.broadcast_to(stream[None], (chips, block, tokens)), PL...]
    ppermute x9 -> x18, waiting for transfers between devices: 16.1 us -> 25.1 us  [shifted(): return lax.ppermute(x, axis, [(i, (i + by) % size) for i in range(size)])]
    pallas_call x0 -> x1, Pallas kernels: none -> 7.32 us  [brought_in(): pl.pallas_call(bring_kernel, out_shape=pltpu.VMEM((3 * rows, width), BF16...]
    ppermute x9 -> x18, starting transfers between devices: 7.32 us -> 13.3 us  [shifted(): return lax.ppermute(x, axis, [(i, (i + by) % size) for i in range(size)])]
    pallas_call x1, Pallas kernels: 10.6 us -> 9.02 us  [experts(): pl.pallas_call(expert_kernel, out_shape=(half, half), in_specs=[pl.BlockS...]
  transfers between devices with their start and end apart: 10 -> 19, of which waited for: 10 -> 18; matrix products, arithmetic and copies ran while one was open for 1% -> 1% of each run, Pallas kernels for 0% -> 7%
where the time goes in v3:
time: 102 us
  waiting for transfers between devices  34.2 us (34%)
  starting transfers between devices  21.5 us (21%)
  blocking collectives  20.4 us (20%)
  Pallas kernels  16.3 us (16%)
  matrix products  4 us (4%)
  local copies, waits for them, and re-layouts  2.75 us (3%)
  other arithmetic  2.16 us (2%)
    ppermute x18, waiting for transfers between devices, shifted(): return lax.ppermute(x, axis, [(i, (i + by) % size) for i in range(size)])  25.1 us
    all_to_all x1, blocking collectives, on_device(): lax.all_to_all(pair.reshape(chips, count_local, width), PLANE, 0, 0, tile...  20.4 us
    ppermute x18, starting transfers between devices, shifted(): return lax.ppermute(x, axis, [(i, (i + by) % size) for i in range(size)])  13.3 us
    all_to_all x1, waiting for transfers between devices, on_device(): lax.all_to_all(pieces, PLANE, 0, 0, tiled=True).reshape(tokens // 2, -1)  9.06 us
    pallas_call x1, Pallas kernels, experts(): pl.pallas_call(expert_kernel, out_shape=(half, half), in_specs=[pl.BlockS...  9.02 us
    all_to_all x1, starting transfers between devices, on_device(): lax.all_to_all(pieces, PLANE, 0, 0, tiled=True).reshape(tokens // 2, -1)  8.16 us
    pallas_call x1, Pallas kernels, brought_in(): pl.pallas_call(bring_kernel, out_shape=pltpu.VMEM((3 * rows, width), BF16...  7.32 us
    dot_general x1, matrix products, on_device(): jnp.einsum('tkgp,tpkd->tkgd', attn_weights, value_cache, preferred_elemen...  2.09 us
  transfers between devices with their start and end apart: 19, of which 18 were waited for; matrix products, arithmetic and copies ran while one was open for 1% of the time, Pallas kernels for 7%

profile of v3, /device:TPU:0, one launch (start us, length us, event | category | flops | bytes accessed | tf_op | source)
XLA Modules:
  0.0 101.5 jit_solution(1543993191879669909)
XLA Ops:
  0.0 1.6 %copy-done = bf16[8,512,2,128]{3,2,1,0:T(2,128)(2,1)S(1)} copy-done((bf16[8,512,2,128]{3,2,1,0:T(2,128)(2,1)S(1)}, bf16[8,512,2,128]{3,2,1,0:T(2,128)(2,1)}, u32[]{:S(2)}) %copy-start) | copy-done | bytes 2097176
  1.6 1.4 %fusion.7 = f32[8,2,4,512]{3,2,1,0:T(4,128)S(1)} fusion(bf16[8,2,4,128]{3,2,1,0:T(4,128)(2,1)} %bitcast.52, bf16[8,512,2,128]{3,2,1,0:T(2,128)(2,1)S(1)} %copy-done), kind=kOutput, calls=%fused_computation.8 | convolution fusion | flops 8421376 | bytes 2244608 | tf_op jit(solution)/shard_map/tkgd,tpkd->tkgp/dot_general | solution.py:169
  3.2 2.1 %fusion.12 = bf16[8,2,4,128]{3,2,1,0:T(4,128)(2,1)S(1)} fusion(bf16[8,512,2,128]{3,2,1,0:T(2,128)(2,1)} %param.14, f32[8,2,4]{2,1,0:T(2,128)S(1)} %fusion.20, f32[8,2,4,512]{3,2,1,0:T(4,128)S(1)} %fusion.7), kind=kOutput, calls=%fused_computation.13 | convolution fusion | flops 8495679 | bytes 2244864 | tf_op jit(solution)/shard_map/tkgp,tpkd->tkgd/dot_general | solution.py:173
  5.4 0.7 pad_maximum_fusion
  6.1 8.2 %all-to-all-start = ((bf16[16,8,1280]{2,1,0:T(8,128)(2,1)}), bf16[16,8,1280]{2,1,0:T(8,128)(2,1)S(1)}, u32[]{:S(2)}, u32[]{:S(2)}) async-start(bf16[16,8,1280]{2,1,0:T(8,128)(2,1)} %pad_maximum_fusion), calls=%async_computation | async-start | bytes 655360 | tf_op jit(solution)/shard_map/all_to_all | solution.py:185
  14.6 9.1 %all-to-all-done = bf16[16,8,1280]{2,1,0:T(8,128)(2,1)S(1)} async-done(((bf16[16,8,1280]{2,1,0:T(8,128)(2,1)}), bf16[16,8,1280]{2,1,0:T(8,128)(2,1)S(1)}, u32[]{:S(2)}, u32[]{:S(2)}) %all-to-all-start) | async-done | bytes 327712 | tf_op jit(solution)/shard_map/all_to_all | solution.py:185
  24.3 1.3 %collective-permute-done = bf16[128,1280]{0,1:T(8,128)(2,1)S(1)} collective-permute-done((bf16[128,1280]{0,1:T(8,128)(2,1)S(1)}, bf16[128,1280]{0,1:T(8,128)(2,1)S(1)}, u32[]{:S(2)}, u32[]{:S(2)}) %collective-permute-start) | collective-permute-done | bytes 327712 | tf_op jit(solution)/shard_map/ppermute | solution.py:19
  25.9 2.8 %collective-permute-start.3 = (bf16[128,256]{1,0:T(8,128)(2,1)S(1)}, bf16[128,256]{1,0:T(8,128)(2,1)S(1)}, u32[]{:S(2)}, u32[]{:S(2)}) collective-permute-start(bf16[128,256]{1,0:T(8,128)(2,1)S(1)} %pad_maximum_fusion.2), channel_id=1, source_target_pairs={{0,96},{32,0},{64,32},{96,64},{1,97},{33,1},{65,33},{97,65},{2,98}... | collective-permute-start | bytes 196616 | tf_op jit(solution)/shard_map/ppermute | solution.py:19
  28.7 0.8 collective-permute-start.2
  29.5 0.9 collective-permute-start.1
  30.4 1.5 %collective-permute-done.3 = bf16[128,256]{1,0:T(8,128)(2,1)S(1)} collective-permute-done((bf16[128,256]{1,0:T(8,128)(2,1)S(1)}, bf16[128,256]{1,0:T(8,128)(2,1)S(1)}, u32[]{:S(2)}, u32[]{:S(2)}) %collective-permute-start.3) | collective-permute-done | bytes 65568 | tf_op jit(solution)/shard_map/ppermute | solution.py:19
  31.9 2.8 %collective-permute-done.2 = bf16[128,256]{1,0:T(8,128)(2,1)S(1)} collective-permute-done((bf16[128,256]{1,0:T(8,128)(2,1)S(1)}, bf16[128,256]{1,0:T(8,128)(2,1)S(1)}, u32[]{:S(2)}, u32[]{:S(2)}) %collective-permute-start.2) | collective-permute-done | bytes 65568 | tf_op jit(solution)/shard_map/ppermute | solution.py:19
  34.8 0.7 collective-permute-done.1
  35.5 0.6 broadcast_in_dim.8.gain
  36.1 0.7 collective-permute-start.6
  36.8 2.0 %collective-permute-start.5 = (bf16[128,256]{1,0:T(8,128)(2,1)S(1)}, bf16[128,256]{1,0:T(8,128)(2,1)S(1)}, u32[]{:S(2)}, u32[]{:S(2)}) collective-permute-start(bf16[128,256]{1,0:T(8,128)(2,1)S(1)} %get-tuple-element.39), channel_id=1, source_target_pairs={{0,4},{2,6},{4,0},{6,2},{1,5},{3,7},{5,1},{7,3},{8,12},{10,14},{12... | collective-permute-start | bytes 196616 | tf_op jit(solution)/shard_map/ppermute | solution.py:19
  38.8 1.6 %collective-permute-done.6._ = bf16[128,256]{1,0:T(8,128)(2,1)S(1)} collective-permute-done((bf16[128,256]{1,0:T(8,128)(2,1)S(1)}, bf16[128,256]{1,0:T(8,128)(2,1)S(1)}, u32[]{:S(2)}, u32[]{:S(2)}) %collective-permute-start.6) | collective-permute-done | bytes 65568 | tf_op jit(solution)/shard_map/ppermute | solution.py:19
  40.5 2.8 %collective-permute-done.5 = bf16[128,256]{1,0:T(8,128)(2,1)S(1)} collective-permute-done((bf16[128,256]{1,0:T(8,128)(2,1)S(1)}, bf16[128,256]{1,0:T(8,128)(2,1)S(1)}, u32[]{:S(2)}, u32[]{:S(2)}) %collective-permute-start.5) | collective-permute-done | bytes 65568 | tf_op jit(solution)/shard_map/ppermute | solution.py:19
  43.2 1.1 %collective-permute-done.4 = bf16[128,256]{1,0:T(8,128)(2,1)S(1)} collective-permute-done((bf16[128,256]{1,0:T(8,128)(2,1)S(1)}, bf16[128,256]{1,0:T(8,128)(2,1)S(1)}, u32[]{:S(2)}, u32[]{:S(2)}) %collective-permute-start.4) | collective-permute-done | bytes 65568 | tf_op jit(solution)/shard_map/ppermute | solution.py:19
  44.4 0.9 collective-permute-start.9
  45.3 0.8 collective-permute-start.8
  46.7 7.3 %bring.1.held = bf16[2688,4096]{1,0:T(8,128)(2,1)S(1)} custom-call(bf16[128,256]{1,0:T(8,128)(2,1)} %copy-done.2, bf16[896,4096]{1,0:T(8,128)(2,1)} %bitcast.41, bf16[896,4096]{1,0:T(8,128)(2,1)} %bitcast.42, bf16[896,4096]{1,0:T(8,128)(2,1)} %bitcast.43), custom_call_target="tpu_custom_call" | custom-call | flops 880803840 | bytes 44040192 | tf_op jit(solution)/shard_map/bring/pallas_call | solution.py:44
  54.0 1.6 %collective-permute-done.8.refs_4_ = bf16[4,128,256]{2,1,0:T(8,128)(2,1)S(1)} collective-permute-done((bf16[4,128,256]{2,1,0:T(8,128)(2,1)S(1)}, bf16[4,128,256]{2,1,0:T(8,128)(2,1)S(1)}, u32[]{:S(2)}, u32[]{:S(2)}) %collective-permute-start.8) | collective-permute-done | bytes 262176 | tf_op jit(solution)/shard_map/ppermute | solution.py:19
  55.6 2.8 %collective-permute-done.7.refs_2_ = bf16[4,128,256]{2,1,0:T(8,128)(2,1)S(1)} collective-permute-done((bf16[4,128,256]{2,1,0:T(8,128)(2,1)S(1)}, bf16[4,128,256]{2,1,0:T(8,128)(2,1)S(1)}, u32[]{:S(2)}, u32[]{:S(2)}) %collective-permute-start.7) | collective-permute-done | bytes 262176 | tf_op jit(solution)/shard_map/ppermute | solution.py:19
  61.1 9.0 %experts.1 = (bf16[128,4096]{1,0:T(8,128)(2,1)S(1)}, bf16[128,4096]{1,0:T(8,128)(2,1)S(1)}) custom-call(s32[5]{0:T(128)S(1)} %stack.42.place, s32[2,256]{1,0:T(2,128)S(1)} %reshape.35.ids, bf16[4096,128]{1,0:T(8,128)(2,1)S(1)} %broadcast_in_dim.8.gain, bf16[8,4096]{1,0:T(8,128)(2,1)S(1)} %bitcast.40, bf16[128,256]{1,0:T(8,128)(2,1)S(1)} %get-tuple-element.40.attn, ...), custom_call_target="tpu_custom_call" | custom-call | flops 5637144576 | bytes 22020096 | tf_op jit(solution)/shard_map/experts/pallas_call | solution.py:136
  70.3 2.5 %collective-permute-done.14 = bf16[128,4096]{1,0:T(8,128)(2,1)S(1)} collective-permute-done((bf16[128,4096]{1,0:T(8,128)(2,1)S(1)}, bf16[128,4096]{1,0:T(8,128)(2,1)S(1)}, u32[]{:S(2)}, u32[]{:S(2)}) %collective-permute-start.14) | collective-permute-done | bytes 1048608 | tf_op jit(solution)/shard_map/ppermute | solution.py:19
  73.1 20.4 %all_to_all.10 = bf16[16,8,4096]{2,1,0:T(8,128)(2,1)S(1)} all-to-all(bf16[16,8,4096]{2,1,0:T(8,128)(2,1)S(1)} %fusion.15), channel_id=1, replica_groups=mesh['expert'=4,'shard_0'=4,'shard_1'=4,'shard_2'=2] {'shard_0','shard_1'}, dimensions={0} | all-to-all | bytes 2097152 | tf_op jit(solution)/shard_map/all_to_all | solution.py:228
  93.7 1.0 %collective-permute-start.16 = (bf16[8,4096]{1,0:T(8,128)(2,1)S(1)}, bf16[8,4096]{1,0:T(8,128)(2,1)S(1)}, u32[]{:S(2)}, u32[]{:S(2)}) collective-permute-start(bf16[8,4096]{1,0:T(8,128)(2,1)S(1)} %reduce_sum.22), channel_id=1, source_target_pairs={{0,64},{32,96},{64,0},{96,32},{1,65},{33,97},{65,1},{97,33},{2,66}... | collective-permute-start | bytes 196616 | tf_op jit(solution)/shard_map/ppermute | solution.py:19
  94.8 1.3 %collective-permute-start.15 = (bf16[8,4096]{1,0:T(8,128)(2,1)S(1)}, bf16[8,4096]{1,0:T(8,128)(2,1)S(1)}, u32[]{:S(2)}, u32[]{:S(2)}) collective-permute-start(bf16[8,4096]{1,0:T(8,128)(2,1)S(1)} %reduce_sum.22), channel_id=1, source_target_pairs={{0,32},{32,64},{64,96},{96,0},{1,33},{33,65},{65,97},{97,1},{2,34}... | collective-permute-start | bytes 196616 | tf_op jit(solution)/shard_map/ppermute | solution.py:19
  96.1 1.9 %collective-permute-done.17 = bf16[8,4096]{1,0:T(8,128)(2,1)S(1)} collective-permute-done((bf16[8,4096]{1,0:T(8,128)(2,1)S(1)}, bf16[8,4096]{1,0:T(8,128)(2,1)S(1)}, u32[]{:S(2)}, u32[]{:S(2)}) %collective-permute-start.17) | collective-permute-done | bytes 65568 | tf_op jit(solution)/shard_map/ppermute | solution.py:19
  98.0 2.4 %collective-permute-done.16 = bf16[8,4096]{1,0:T(8,128)(2,1)S(1)} collective-permute-done((bf16[8,4096]{1,0:T(8,128)(2,1)S(1)}, bf16[8,4096]{1,0:T(8,128)(2,1)S(1)}, u32[]{:S(2)}, u32[]{:S(2)}) %collective-permute-start.16) | collective-permute-done | bytes 65568 | tf_op jit(solution)/shard_map/ppermute | solution.py:19
  100.8 0.7 add_convert_fusion.1
  (46 shorter events, 6.0 us)
Async XLA Ops:
  0.0 1.6 %copy-start = (bf16[8,512,2,128]{3,2,1,0:T(2,128)(2,1)S(1)}, bf16[8,512,2,128]{3,2,1,0:T(2,128)(2,1)}, u32[]{:S(2)}) copy-start(bf16[8,512,2,128]{3,2,1,0:T(2,128)(2,1)} %param.13) | copy-start | bytes 6291460
  3.0 2.4 %copy-start.4 = (bf16[8,4096]{1,0:T(8,128)(2,1)S(1)}, bf16[8,4096]{1,0:T(8,128)(2,1)}, u32[]{:S(2)}) copy-start(bf16[8,4096]{1,0:T(8,128)(2,1)} %param.11) | copy-start | bytes 196612
  3.2 11.1 %copy-start.6 = (s32[256,2]{0,1:T(2,128)S(1)}, s32[256,2]{0,1:T(2,128)}, u32[]{:S(2)}) copy-start(s32[256,2]{0,1:T(2,128)} %param.18) | copy-start | bytes 6148
  3.2 20.8 %copy-start.3 = (bf16[1024,128]{1,0:T(8,128)(2,1)S(1)}, bf16[1024,128]{1,0:T(8,128)(2,1)}, u32[]{:S(2)}) copy-start(bf16[1024,128]{1,0:T(8,128)(2,1)} %param.15) | copy-start | bytes 786436
  5.3 30.2 %copy-start.5 = (bf16[4096]{0:T(1024)(128)(2,1)S(1)}, bf16[4096]{0:T(1024)(128)(2,1)}, u32[]{:S(2)}) copy-start(bf16[4096]{0:T(1024)(128)(2,1)} %param.16) | copy-start | bytes 24580
  6.1 17.6 %all-to-all-start = ((bf16[16,8,1280]{2,1,0:T(8,128)(2,1)}), bf16[16,8,1280]{2,1,0:T(8,128)(2,1)S(1)}, u32[]{:S(2)}, u32[]{:S(2)}) async-start(bf16[16,8,1280]{2,1,0:T(8,128)(2,1)} %pad_maximum_fusion), calls=%async_computation | async-start | bytes 655360 | tf_op jit(solution)/shard_map/all_to_all | solution.py:185
  23.9 1.7 %collective-permute-start = (bf16[128,1280]{0,1:T(8,128)(2,1)S(1)}, bf16[128,1280]{0,1:T(8,128)(2,1)S(1)}, u32[]{:S(2)}, u32[]{:S(2)}) collective-permute-start(bf16[128,1280]{0,1:T(8,128)(2,1)S(1)} %copy.22), channel_id=1, source_target_pairs={{0,1},{1,0},{2,3},{3,2},{4,5},{5,4},{6,7},{7,6},{8,9},{9,8},{10,11... | collective-permute-start | bytes 983048 | tf_op jit(solution)/shard_map/ppermute | solution.py:19
  25.9 6.0 %collective-permute-start.3 = (bf16[128,256]{1,0:T(8,128)(2,1)S(1)}, bf16[128,256]{1,0:T(8,128)(2,1)S(1)}, u32[]{:S(2)}, u32[]{:S(2)}) collective-permute-start(bf16[128,256]{1,0:T(8,128)(2,1)S(1)} %pad_maximum_fusion.2), channel_id=1, source_target_pairs={{0,96},{32,0},{64,32},{96,64},{1,97},{33,1},{65,33},{97,65},{2,98}... | collective-permute-start | bytes 196616 | tf_op jit(solution)/shard_map/ppermute | solution.py:19
  28.7 6.1 %collective-permute-start.2 = (bf16[128,256]{1,0:T(8,128)(2,1)S(1)}, bf16[128,256]{1,0:T(8,128)(2,1)S(1)}, u32[]{:S(2)}, u32[]{:S(2)}) collective-permute-start(bf16[128,256]{1,0:T(8,128)(2,1)S(1)} %pad_maximum_fusion.2), channel_id=1, source_target_pairs={{0,64},{32,96},{64,0},{96,32},{1,65},{33,97},{65,1},{97,33},{2,66}... | collective-permute-start | bytes 196616 | tf_op jit(solution)/shard_map/ppermute | solution.py:19
  29.5 6.0 %collective-permute-start.1 = (bf16[128,256]{1,0:T(8,128)(2,1)S(1)}, bf16[128,256]{1,0:T(8,128)(2,1)S(1)}, u32[]{:S(2)}, u32[]{:S(2)}) collective-permute-start(bf16[128,256]{1,0:T(8,128)(2,1)S(1)} %pad_maximum_fusion.2), channel_id=1, source_target_pairs={{0,32},{32,64},{64,96},{96,0},{1,33},{33,65},{65,97},{97,1},{2,34}... | collective-permute-start | bytes 196616 | tf_op jit(solution)/shard_map/ppermute | solution.py:19
  36.1 4.3 %collective-permute-start.6 = (bf16[128,256]{1,0:T(8,128)(2,1)S(1)}, bf16[128,256]{1,0:T(8,128)(2,1)S(1)}, u32[]{:S(2)}, u32[]{:S(2)}) collective-permute-start(bf16[128,256]{1,0:T(8,128)(2,1)S(1)} %get-tuple-element.39), channel_id=1, source_target_pairs={{0,6},{2,0},{4,2},{6,4},{1,7},{3,1},{5,3},{7,5},{8,14},{10,8},{12,... | collective-permute-start | bytes 196616 | tf_op jit(solution)/shard_map/ppermute | solution.py:19
  36.8 6.4 %collective-permute-start.5 = (bf16[128,256]{1,0:T(8,128)(2,1)S(1)}, bf16[128,256]{1,0:T(8,128)(2,1)S(1)}, u32[]{:S(2)}, u32[]{:S(2)}) collective-permute-start(bf16[128,256]{1,0:T(8,128)(2,1)S(1)} %get-tuple-element.39), channel_id=1, source_target_pairs={{0,4},{2,6},{4,0},{6,2},{1,5},{3,7},{5,1},{7,3},{8,12},{10,14},{12... | collective-permute-start | bytes 196616 | tf_op jit(solution)/shard_map/ppermute | solution.py:19
  38.8 5.5 %collective-permute-start.4 = (bf16[128,256]{1,0:T(8,128)(2,1)S(1)}, bf16[128,256]{1,0:T(8,128)(2,1)S(1)}, u32[]{:S(2)}, u32[]{:S(2)}) collective-permute-start(bf16[128,256]{1,0:T(8,128)(2,1)S(1)} %get-tuple-element.39), channel_id=1, source_target_pairs={{0,2},{2,4},{4,6},{6,0},{1,3},{3,5},{5,7},{7,1},{8,10},{10,12},{12... | collective-permute-start | bytes 196616 | tf_op jit(solution)/shard_map/ppermute | solution.py:19
  40.5 6.2 %copy-start.2 = (bf16[128,256]{1,0:T(8,128)(2,1)}, bf16[128,256]{1,0:T(8,128)(2,1)S(1)}, u32[]{:S(2)}) copy-start(bf16[128,256]{1,0:T(8,128)(2,1)S(1)} %collective-permute-done.6._) | copy-start | bytes 196612
  44.4 9.7 %collective-permute-start.9 = (bf16[4,128,256]{2,1,0:T(8,128)(2,1)S(1)}, bf16[4,128,256]{2,1,0:T(8,128)(2,1)S(1)}, u32[]{:S(2)}, u32[]{:S(2)}) collective-permute-start(bf16[4,128,256]{2,1,0:T(8,128)(2,1)S(1)} %pad_maximum_fusion.1.refs_0_), channel_id=1, source_target_pairs={{0,24},{8,0},{16,8},{24,16},{1,25},{9,1},{17,9},{25,17},{2,26},{10... | collective-permute-start | bytes 786440 | tf_op jit(solution)/shard_map/ppermute | solution.py:19
  45.3 10.4 %collective-permute-start.8 = (bf16[4,128,256]{2,1,0:T(8,128)(2,1)S(1)}, bf16[4,128,256]{2,1,0:T(8,128)(2,1)S(1)}, u32[]{:S(2)}, u32[]{:S(2)}) collective-permute-start(bf16[4,128,256]{2,1,0:T(8,128)(2,1)S(1)} %pad_maximum_fusion.1.refs_0_), channel_id=1, source_target_pairs={{0,16},{8,24},{16,0},{24,8},{1,17},{9,25},{17,1},{25,9},{2,18},{10... | collective-permute-start | bytes 786440 | tf_op jit(solution)/shard_map/ppermute | solution.py:19
  46.1 12.3 %collective-permute-start.7 = (bf16[4,128,256]{2,1,0:T(8,128)(2,1)S(1)}, bf16[4,128,256]{2,1,0:T(8,128)(2,1)S(1)}, u32[]{:S(2)}, u32[]{:S(2)}) collective-permute-start(bf16[4,128,256]{2,1,0:T(8,128)(2,1)S(1)} %pad_maximum_fusion.1.refs_0_), channel_id=1, source_target_pairs={{0,8},{8,16},{16,24},{24,0},{1,9},{9,17},{17,25},{25,1},{2,10},{10... | collective-permute-start | bytes 786440 | tf_op jit(solution)/shard_map/ppermute | solution.py:19
  46.7 14.4 %copy-start.1 = (bf16[4096,8]{0,1:T(8,128)(2,1)S(1)}, bf16[4096,8]{0,1:T(8,128)(2,1)}, u32[]{:S(2)}) copy-start(bf16[4096,8]{0,1:T(8,128)(2,1)} %param.17) | copy-start | bytes 196612
  58.4 1.5 %collective-permute-start.10 = (bf16[4,128,256]{2,1,0:T(8,128)(2,1)S(1)}, bf16[4,128,256]{2,1,0:T(8,128)(2,1)S(1)}, u32[]{:S(2)}, u32[]{:S(2)}) collective-permute-start(bf16[4,128,256]{2,1,0:T(8,128)(2,1)S(1)} %pad_maximum_fusion.1.refs_0_), channel_id=1, source_target_pairs={{0,1},{1,0},{2,3},{3,2},{4,5},{5,4},{6,7},{7,6},{8,9},{9,8},{10,11... | collective-permute-start | bytes 786440 | tf_op jit(solution)/shard_map/ppermute | solution.py:19
  58.4 1.9 %collective-permute-start.11 = (bf16[4,128,256]{2,1,0:T(8,128)(2,1)S(1)}, bf16[4,128,256]{2,1,0:T(8,128)(2,1)S(1)}, u32[]{:S(2)}, u32[]{:S(2)}) collective-permute-start(bf16[4,128,256]{2,1,0:T(8,128)(2,1)S(1)} %collective-permute-done.7.refs_2_), channel_id=1, source_target_pairs={{0,1},{1,0},{2,3},{3,2},{4,5},{5,4},{6,7},{7,6},{8,9},{9,8},{10,11... | collective-permute-start | bytes 786440 | tf_op jit(solution)/shard_map/ppermute | solution.py:19
  58.9 1.8 %collective-permute-start.12 = (bf16[4,128,256]{2,1,0:T(8,128)(2,1)S(1)}, bf16[4,128,256]{2,1,0:T(8,128)(2,1)S(1)}, u32[]{:S(2)}, u32[]{:S(2)}) collective-permute-start(bf16[4,128,256]{2,1,0:T(8,128)(2,1)S(1)} %collective-permute-done.8.refs_4_), channel_id=1, source_target_pairs={{0,1},{1,0},{2,3},{3,2},{4,5},{5,4},{6,7},{7,6},{8,9},{9,8},{10,11... | collective-permute-start | bytes 786440 | tf_op jit(solution)/shard_map/ppermute | solution.py:19
  58.9 2.1 %collective-permute-start.13 = (bf16[4,128,256]{2,1,0:T(8,128)(2,1)S(1)}, bf16[4,128,256]{2,1,0:T(8,128)(2,1)S(1)}, u32[]{:S(2)}, u32[]{:S(2)}) collective-permute-start(bf16[4,128,256]{2,1,0:T(8,128)(2,1)S(1)} %collective-permute-done.9.refs_6_), channel_id=1, source_target_pairs={{0,1},{1,0},{2,3},{3,2},{4,5},{5,4},{6,7},{7,6},{8,9},{9,8},{10,11... | collective-permute-start | bytes 786440 | tf_op jit(solution)/shard_map/ppermute | solution.py:19
  70.1 2.7 %collective-permute-start.14 = (bf16[128,4096]{1,0:T(8,128)(2,1)S(1)}, bf16[128,4096]{1,0:T(8,128)(2,1)S(1)}, u32[]{:S(2)}, u32[]{:S(2)}) collective-permute-start(bf16[128,4096]{1,0:T(8,128)(2,1)S(1)} %get-tuple-element.35), channel_id=1, source_target_pairs={{0,1},{1,0},{2,3},{3,2},{4,5},{5,4},{6,7},{7,6},{8,9},{9,8},{10,11... | collective-permute-start | bytes 3145736 | tf_op jit(solution)/shard_map/ppermute | solution.py:19
  93.6 4.3 %collective-permute-start.17 = (bf16[8,4096]{1,0:T(8,128)(2,1)S(1)}, bf16[8,4096]{1,0:T(8,128)(2,1)S(1)}, u32[]{:S(2)}, u32[]{:S(2)}) collective-permute-start(bf16[8,4096]{1,0:T(8,128)(2,1)S(1)} %reduce_sum.22), channel_id=1, source_target_pairs={{0,96},{32,0},{64,32},{96,64},{1,97},{33,1},{65,33},{97,65},{2,98}... | collective-permute-start | bytes 196616 | tf_op jit(solution)/shard_map/ppermute | solution.py:19
  93.7 6.6 %collective-permute-start.16 = (bf16[8,4096]{1,0:T(8,128)(2,1)S(1)}, bf16[8,4096]{1,0:T(8,128)(2,1)S(1)}, u32[]{:S(2)}, u32[]{:S(2)}) collective-permute-start(bf16[8,4096]{1,0:T(8,128)(2,1)S(1)} %reduce_sum.22), channel_id=1, source_target_pairs={{0,64},{32,96},{64,0},{96,32},{1,65},{33,97},{65,1},{97,33},{2,66}... | collective-permute-start | bytes 196616 | tf_op jit(solution)/shard_map/ppermute | solution.py:19
  94.8 6.1 %collective-permute-start.15 = (bf16[8,4096]{1,0:T(8,128)(2,1)S(1)}, bf16[8,4096]{1,0:T(8,128)(2,1)S(1)}, u32[]{:S(2)}, u32[]{:S(2)}) collective-permute-start(bf16[8,4096]{1,0:T(8,128)(2,1)S(1)} %reduce_sum.22), channel_id=1, source_target_pairs={{0,32},{32,64},{64,96},{96,0},{1,33},{33,65},{65,97},{97,1},{2,34}... | collective-permute-start | bytes 196616 | tf_op jit(solution)/shard_map/ppermute | solution.py:19

commit v4 on v3

v4 whole, which is shorter than its diff:
```python
import math

import jax
import jax.numpy as jnp
from jax import lax
from jax.experimental import pallas as pl
from jax.experimental.pallas import tpu as pltpu
from jax.sharding import Mesh
from jax.sharding import PartitionSpec as P

SHARD = ("shard_0", "shard_1", "shard_2")
PLANE = ("shard_0", "shard_1")
F32 = jnp.float32
BF16 = jnp.bfloat16


def shifted(x, axis, by):
    size = lax.axis_size(axis)
    return lax.ppermute(x, axis, [(i, (i + by) % size) for i in range(size)])


def sum_over_groups(part, ready=()):
    others = tuple(shifted(part, "expert", by) for by in (1, 2, 3))
    (one, two, three), ready = lax.optimization_barrier((others, ready))
    total = (part.astype(F32) + two.astype(F32)) + (one.astype(F32) + three.astype(F32))
    return (total, ready) if ready else total


def attention_kernel(queries, hidden, key_hbm, value_hbm, pieces, keys, values, scores, found, sems):
    tokens, rows, size = keys.shape
    heads = queries.shape[0] // tokens
    kv_local = 2
    parts = sems.shape[1]
    count = tokens // parts

    def copy(n, part):
        source, target = ((key_hbm, keys), (value_hbm, values))[n]
        at = pl.ds(part * count, count)
        return pltpu.make_async_copy(source.at[at], target.at[at], sems.at[n, part])

    for n in range(2):
        for part in range(parts):
            copy(n, part).start()

    def score_part(part, carry):
        copy(0, part).wait()
        for m in range(count):
            t = part * count + m
            at = pl.ds(pl.multiple_of(t * heads, heads), heads)
            scores[at, :] = lax.dot_general(
                queries[at, :], keys[t], (((1,), (1,)), ((), ())), preferred_element_type=F32
            )
        return carry

    lax.fori_loop(0, parts, score_part, 0)
    chips, _, columns = pieces.shape
    block = columns - heads * size
    for chip in range(chips):
        pieces[chip, :, heads * size :] = hidden[:, chip * block : (chip + 1) * block]
    shape = scores.shape
    mine = (lax.broadcasted_iota(jnp.int32, shape, 0) % heads) // (heads // kv_local) == (
        lax.broadcasted_iota(jnp.int32, shape, 1) % kv_local
    )
    logits = jnp.where(mine, scores[...] * (1.0 / math.sqrt(size)), -3.0e38)
    powers = jnp.exp(logits - logits.max(axis=1, keepdims=True))
    scores[...] = powers / powers.sum(axis=1, keepdims=True)

    def wait_part(part, carry):
        copy(1, part).wait()
        return carry

    lax.fori_loop(0, parts, wait_part, 0)
    for t in range(tokens):
        at = pl.ds(t * heads, heads)
        found[at, :] = jnp.dot(
            scores[at, :].astype(BF16), values[t], preferred_element_type=F32
        )
    for h in range(heads):
        attended = found[pl.ds(h, tokens, stride=heads), :].astype(BF16)
        for chip in range(chips):
            pieces[chip, :, h * size : (h + 1) * size] = attended


def attention(queries, keys, values, hidden, chips):
    tokens, heads, size = queries.shape
    rows = keys.shape[1]
    width = heads * size + hidden.shape[1] // chips
    vmem = pl.BlockSpec(memory_space=pltpu.VMEM)
    hbm = pl.BlockSpec(memory_space=pl.ANY)
    return pl.pallas_call(
        attention_kernel,
        out_shape=jax.ShapeDtypeStruct((chips, tokens, width), BF16),
        in_specs=[vmem, vmem, hbm, hbm],
        out_specs=vmem,
        scratch_shapes=[
            pltpu.VMEM((tokens, rows, size), BF16),
            pltpu.VMEM((tokens, rows, size), BF16),
            pltpu.VMEM((tokens * heads, rows), F32),
            pltpu.VMEM((tokens * heads, size), F32),
            pltpu.SemaphoreType.DMA((2, 4)),
        ],
        compiler_params=pltpu.CompilerParams(vmem_limit_bytes=62 * 1024 * 1024),
        cost_estimate=pl.CostEstimate(
            flops=4 * tokens * heads * rows * size,
            bytes_accessed=4 * tokens * rows * size,
            transcendentals=tokens * heads * rows,
        ),
        name="attention",
    )(queries.reshape(tokens * heads, size), hidden, keys, values)


def bring_kernel(_, gains, gate, up, down, held, gain, sems):
    units = gate.shape[0]
    copies = [
        pltpu.make_async_copy(source, held.at[pl.ds(n * units, units)], sems.at[n])
        for n, source in enumerate((gate, up, down))
    ]
    for copy in copies:
        copy.start()
    lanes = gain.shape[1]
    for at in range(0, gain.shape[0], lanes):
        row = gains[:, at : at + lanes].astype(F32)
        gain[at : at + lanes, :] = jnp.broadcast_to(row, (lanes, lanes)).T.astype(BF16)
    for copy in copies:
        copy.wait()


def brought_in(after, gains, *weights):
    size = sum(w.size for w in weights)
    rows, width = weights[0].shape
    hbm = pl.BlockSpec(memory_space=pl.ANY)
    vmem = pl.BlockSpec(memory_space=pltpu.VMEM)
    return pl.pallas_call(
        bring_kernel,
        out_shape=(pltpu.VMEM((3 * rows, width), BF16), jax.ShapeDtypeStruct((width, 128), BF16)),
        in_specs=[hbm, vmem] + [hbm] * len(weights),
        out_specs=(vmem, vmem),
        scratch_shapes=[pltpu.SemaphoreType.DMA((3,))],
        compiler_params=pltpu.CompilerParams(vmem_limit_bytes=36 * 1024 * 1024),
        cost_estimate=pl.CostEstimate(flops=80 * size, bytes_accessed=4 * size, transcendentals=0),
        name="bring",
    )(after, gains, *weights)


def expert_kernel(
    place, ids, gain, router, attn, held, own, partner, send, keep, mixed, hidden_t, act
):
    core, shard, first_expert, adds = (place[n] for n in range(4))
    units, width = held.shape[0] // 3, held.shape[1]
    half_units = units // 2
    chips, block, tokens = own.shape
    half = tokens // 2

    def norm_block(j, squares):
        for mine, part in ((core, own), (1 - core, partner)):
            x = part[j]
            if part is partner:
                x = jnp.concatenate([x[:, half:], x[:, :half]], axis=1)
            rows = pl.ds(pl.multiple_of((2 * j + mine) * block, block), block)
            g = gain[rows, :]
            mixed[rows, :] = x * jnp.concatenate([g, g], axis=1)
            y = x.astype(F32)
            squares = squares + (y * y).reshape(block // 8, 8, tokens).sum(axis=0)
        return squares

    squares = lax.fori_loop(0, chips, norm_block, jnp.zeros((8, tokens), F32), unroll=4)
    scale = lax.rsqrt(squares.sum(axis=0, keepdims=True) / width + 1e-05)
    logits = jnp.dot(router[...], mixed[...], preferred_element_type=F32) * scale
    numbers = lax.broadcasted_iota(jnp.int32, logits.shape, 0)
    named = ids[...]
    named = jnp.where(
        core == 0, named, jnp.concatenate([named[:, half:], named[:, :half]], axis=1)
    )
    first, second = named[0:1, :], named[1:2, :]
    a = jnp.where(numbers == first, logits, 0.0).sum(axis=0, keepdims=True)
    b = jnp.where(numbers == second, logits, 0.0).sum(axis=0, keepdims=True)
    weight_first = 1.0 / (1.0 + jnp.exp(b - a))
    weight_second = 1.0 / (1.0 + jnp.exp(a - b))

    for m in range(2):
        for n in range(2):
            rows = pl.ds((2 * n + m) * half_units, half_units)
            hidden_t[m, n] = jnp.dot(held[rows, :], mixed[...], preferred_element_type=F32)
        expert = first_expert + m
        routed = jnp.where(first == expert, weight_first, 0.0) + jnp.where(
            second == expert, weight_second, 0.0
        )
        gated = hidden_t[m, 0] * scale
        upward = hidden_t[m, 1] * scale
        value = gated / (1.0 + jnp.exp(-gated)) * upward * routed
        act[m] = value.T.astype(BF16)

    step = width // 2

    def down_part(n, carry):
        columns = pl.ds(pl.multiple_of(n * step, step), step)
        total = jnp.dot(
            act[0], held[pl.ds(2 * units, half_units), columns], preferred_element_type=F32
        ) + jnp.dot(
            act[1],
            held[pl.ds(2 * units + half_units, half_units), columns],
            preferred_element_type=F32,
        )
        keep[:, columns] = total[:half].astype(BF16)
        send[:, columns] = total[half:].astype(BF16)
        return carry

    lax.fori_loop(0, width // step, down_part, 0)
    rows = attn[...].astype(F32).T * adds.astype(F32)
    columns = pl.ds(pl.multiple_of(shard * block, block), block)
    keep[:, columns] = (keep[:, columns].astype(F32) + rows[:half]).astype(BF16)
    send[:, columns] = (send[:, columns].astype(F32) + rows[half:]).astype(BF16)


def experts(place, ids, gain, router, attn, held, own, partner):
    units, width = held.shape[0] // 3, held.shape[1]
    tokens = attn.shape[1]
    vmem = pl.BlockSpec(memory_space=pltpu.VMEM)
    half = jax.ShapeDtypeStruct((tokens // 2, width), BF16)
    return pl.pallas_call(
        expert_kernel,
        out_shape=(half, half),
        in_specs=[pl.BlockSpec(memory_space=pltpu.SMEM)] + [vmem] * 7,
        out_specs=(vmem, vmem),
        scratch_shapes=[
            pltpu.VMEM((width, tokens), BF16),
            pltpu.VMEM((2, 2, units // 2, tokens), F32),
            pltpu.VMEM((2, tokens, units // 2), BF16),
        ],
        compiler_params=pltpu.CompilerParams(vmem_limit_bytes=12 * 1024 * 1024),
        cost_estimate=pl.CostEstimate(
            flops=6 * tokens * units * width,
            bytes_accessed=6 * units * width,
            transcendentals=2 * units * tokens,
        ),
        name="experts",
    )(place, ids, gain, router, attn, held, own, partner)


def on_device(
    hidden, queries, key_cache, value_cache, out_weight, norm_gain, router,
    expert_ids, gate_weight, up_weight, down_weight,
):
    count_local, heads_local, head_size = queries.shape
    kv_local = key_cache.shape[2]
    width = hidden.shape[1]
    block = out_weight.shape[1]
    chips, cores = lax.axis_size(PLANE), lax.axis_size("shard_2")
    tokens = chips * cores * count_local
    core = lax.axis_index("shard_2")
    group = lax.axis_index("expert")
    heads = heads_local * head_size
    rows = key_cache.shape[1] * kv_local
    pieces = attention(
        queries,
        key_cache.reshape(count_local, rows, head_size),
        value_cache.reshape(count_local, rows, head_size),
        hidden,
        chips,
    )
    local = gate_weight.shape[0]
    units = local * gate_weight.shape[2]
    place = jnp.stack(
        [
            core,
            lax.axis_index(PLANE) * cores + core,
            group * local,
            (group == 0).astype(jnp.int32),
        ]
    ).astype(jnp.int32)
    ids = expert_ids.reshape(chips, cores, count_local, 2).transpose(3, 1, 0, 2).reshape(2, tokens)
    arrived = lax.all_to_all(pieces, PLANE, 0, 0, tiled=True).reshape(tokens // 2, -1)
    arrived, place, ids = lax.optimization_barrier((arrived, place, ids))
    passed = shifted(arrived, "shard_2", 1)

    def project(rows):
        return lax.dot_general(
            out_weight, rows[:, :heads], (((0,), (1,)), ((), ())), preferred_element_type=F32
        ).astype(BF16)

    def my_columns(rows):
        return jnp.where(core == 0, rows[:, heads : heads + block], rows[:, heads + block :])

    part = jnp.concatenate([project(arrived), project(passed)], axis=1)
    hidden_t = jnp.concatenate([my_columns(arrived), my_columns(passed)], axis=0).T
    held, gain = brought_in(
        part,
        norm_gain[None, :],
        gate_weight.transpose(0, 2, 1).reshape(units, width),
        up_weight.transpose(0, 2, 1).reshape(units, width),
        down_weight.reshape(units, width),
    )
    attn_out, (hidden_t, held, gain) = sum_over_groups(part, (hidden_t, held, gain))
    stream = (attn_out + hidden_t.astype(F32)).astype(BF16)
    own = lax.all_to_all(
        jnp.broadcast_to(stream[None], (chips, block, tokens)), PLANE, 0, 0, tiled=True
    )
    partner = shifted(own, "shard_2", 1)
    send, keep = experts(
        place, ids, gain, router.T, attn_out.astype(BF16), held, own, partner
    )
    pair = (keep.astype(F32) + shifted(send, "shard_2", 1).astype(F32)).astype(BF16)
    parts = lax.all_to_all(pair.reshape(chips, count_local, width), PLANE, 0, 0, tiled=True)
    reduced = parts.astype(F32).sum(axis=0).astype(BF16)
    return (hidden.astype(F32) + sum_over_groups(reduced)).astype(BF16)


def solution(mesh):
    split = Mesh(
        mesh.devices.reshape(mesh.shape["expert"], 4, 4, 2),
        ("expert", "shard_0", "shard_1", "shard_2"),
    )
    in_specs = (
        P(SHARD, None),
        P(SHARD, "expert", None),
        P(SHARD, None, "expert", None),
        P(SHARD, None, "expert", None),
        P("expert", SHARD),
        P(),
        P(),
        P(),
        P("expert", None, SHARD),
        P("expert", None, SHARD),
        P("expert", SHARD, None),
    )
    return jax.shard_map(
        on_device, mesh=split, in_specs=in_specs, out_specs=P(SHARD, None), check_vma=False
    )
```

time: 102 us -> 102 us (level)
  blocking collectives: 20.4 us -> 40.2 us
  waiting for transfers between devices: 34.2 us -> 20.4 us
  Pallas kernels: 16.3 us -> 21.3 us
  starting transfers between devices: 21.5 us -> 16.9 us
  matrix products: 4 us -> 0.55 us
  local copies, waits for them, and re-layouts: 2.75 us -> 1.15 us
    all_to_all x0 -> x1, blocking collectives: none -> 19.6 us  [on_device(): lax.all_to_all(jnp.broadcast_to(stream[None], (chips, block, tokens)), PL...]
    ppermute x18 -> x9, waiting for transfers between devices: 25.1 us -> 12 us  [shifted(): return lax.ppermute(x, axis, [(i, (i + by) % size) for i in range(size)])]
    pallas_call x1 -> x2, Pallas kernels: 7.32 us -> 13.4 us  [the longest x1 8.99 us: brought_in(): pl.pallas_call(bring_kernel, out_shape=(pltpu.VMEM((3 * rows, width), BF1...]
    ppermute x18 -> x9, starting transfers between devices: 13.3 us -> 8.76 us  [shifted(): return lax.ppermute(x, axis, [(i, (i + by) % size) for i in range(size)])]
    dot_general x2 -> x0, matrix products: 3.44 us -> none  [the longest x1 2.09 us: on_device(): jnp.einsum('tkgp,tpkd->tkgd', attn_weights, value_cache, preferred_elemen...]
    unnamed x14, local copies, waits for them, and re-layouts: 1.62 us -> 0.03 us
    pallas_call x1, Pallas kernels: 9.02 us -> 7.94 us  [experts(): pl.pallas_call(expert_kernel, out_shape=(half, half), in_specs=[pl.BlockS...]
  transfers between devices with their start and end apart: 19 -> 10, of which waited for: 18 -> 7; matrix products, arithmetic and copies ran while one was open for 1% -> 1% of each run, Pallas kernels for 7% -> 9%
where the time goes in v4:
time: 102 us
  blocking collectives  40.2 us (39%)
  Pallas kernels  21.3 us (21%)
  waiting for transfers between devices  20.4 us (20%)
  starting transfers between devices  16.9 us (17%)
  other arithmetic  1.24 us (1%)
  local copies, waits for them, and re-layouts  1.15 us (1%)
    all_to_all x1, blocking collectives, on_device(): lax.all_to_all(pair.reshape(chips, count_local, width), PLANE, 0, 0, tile...  20.5 us
    all_to_all x1, blocking collectives, on_device(): lax.all_to_all(jnp.broadcast_to(stream[None], (chips, block, tokens)), PL...  19.6 us
    ppermute x9, waiting for transfers between devices, shifted(): return lax.ppermute(x, axis, [(i, (i + by) % size) for i in range(size)])  12 us
    pallas_call x1, Pallas kernels, brought_in(): pl.pallas_call(bring_kernel, out_shape=(pltpu.VMEM((3 * rows, width), BF1...  8.99 us
    ppermute x9, starting transfers between devices, shifted(): return lax.ppermute(x, axis, [(i, (i + by) % size) for i in range(size)])  8.76 us
    all_to_all x1, waiting for transfers between devices, on_device(): lax.all_to_all(pieces, PLANE, 0, 0, tiled=True).reshape(tokens // 2, -1)  8.45 us
    all_to_all x1, starting transfers between devices, on_device(): lax.all_to_all(pieces, PLANE, 0, 0, tiled=True).reshape(tokens // 2, -1)  8.18 us
    pallas_call x1, Pallas kernels, experts(): pl.pallas_call(expert_kernel, out_shape=(half, half), in_specs=[pl.BlockS...  7.94 us
  transfers between devices with their start and end apart: 10, of which 7 were waited for; matrix products, arithmetic and copies ran while one was open for 1% of the time, Pallas kernels for 9%

profile of v4, /device:TPU:0, one launch (start us, length us, event | category | flops | bytes accessed | tf_op | source)
XLA Modules:
  0.0 102.0 jit_solution(3270243097548734232)
XLA Ops:
  0.0 4.4 %attention.1 = bf16[16,8,1280]{2,1,0:T(8,128)(2,1)} custom-call(bf16[64,128]{1,0:T(8,128)(2,1)} %bitcast.40, bf16[8,4096]{1,0:T(8,128)(2,1)} %hidden.1, bf16[8,1024,128]{2,1,0:T(8,128)(2,1)} %bitcast.37, bf16[8,1024,128]{2,1,0:T(8,128)(2,1)} %bitcast.38), custom_call_target="tpu_custom_call" | custom-call | flops 33554432 | bytes 4194304 | tf_op jit(solution)/shard_map/attention/pallas_call | solution.py:90
  4.4 8.2 %all-to-all-start = ((bf16[16,8,1280]{2,1,0:T(8,128)(2,1)}), bf16[16,8,1280]{2,1,0:T(8,128)(2,1)S(1)}, u32[]{:S(2)}, u32[]{:S(2)}) async-start(bf16[16,8,1280]{2,1,0:T(8,128)(2,1)} %attention.1), calls=%async_computation | async-start | bytes 655360 | tf_op jit(solution)/shard_map/all_to_all | solution.py:272
  12.6 0.6 broadcast_in_dim.4.gains
  13.3 0.1 reshape.35
  13.4 0.1 reshape.36.ids
  13.5 0.1 pad_add_fusion.place
  13.6 8.4 %all-to-all-done = bf16[16,8,1280]{2,1,0:T(8,128)(2,1)S(1)} async-done(((bf16[16,8,1280]{2,1,0:T(8,128)(2,1)}), bf16[16,8,1280]{2,1,0:T(8,128)(2,1)S(1)}, u32[]{:S(2)}, u32[]{:S(2)}) %all-to-all-start) | async-done | bytes 327712 | tf_op jit(solution)/shard_map/all_to_all | solution.py:272
  22.0 0.2 copy.18
  22.2 0.1 collective-permute-start
  22.3 0.3 fusion
  22.6 1.3 %collective-permute-done = bf16[128,1280]{0,1:T(8,128)(2,1)S(1)} collective-permute-done((bf16[128,1280]{0,1:T(8,128)(2,1)S(1)}, bf16[128,1280]{0,1:T(8,128)(2,1)S(1)}, u32[]{:S(2)}, u32[]{:S(2)}) %collective-permute-start) | collective-permute-done | bytes 327712 | tf_op jit(solution)/shard_map/ppermute | solution.py:19
  23.9 0.3 fusion.1
  24.2 2.8 %collective-permute-start.3 = (bf16[128,256]{1,0:T(8,128)(2,1)S(1)}, bf16[128,256]{1,0:T(8,128)(2,1)S(1)}, u32[]{:S(2)}, u32[]{:S(2)}) collective-permute-start(bf16[128,256]{1,0:T(8,128)(2,1)S(1)} %pad_maximum_fusion._), channel_id=1, source_target_pairs={{0,96},{32,0},{64,32},{96,64},{1,97},{33,1},{65,33},{97,65},{2,98}... | collective-permute-start | bytes 196616 | tf_op jit(solution)/shard_map/ppermute | solution.py:19
  27.1 0.8 collective-permute-start.2
  27.9 0.9 collective-permute-start.1
  28.8 9.0 %bring.1 = (bf16[2688,4096]{1,0:T(8,128)(2,1)S(1)}, bf16[4096,128]{1,0:T(8,128)(2,1)}) custom-call(bf16[128,256]{1,0:T(8,128)(2,1)} %copy-done.3, bf16[1,4096]{1,0:T(2,128)(2,1)} %broadcast_in_dim.4.gains, bf16[896,4096]{1,0:T(8,128)(2,1)} %bitcast.32, bf16[896,4096]{1,0:T(8,128)(2,1)} %bitcast.33, bf16[896,4096]{1,0:T(8,128)(2,1)} %bitcast.34), custom_call_target="tpu_custom_call" | custom-call | flops 880803840 | bytes 44040192 | tf_op jit(solution)/shard_map/bring/pallas_call | solution.py:133
  37.8 0.1 add_convert_fusion.2
  37.9 0.1 broadcast_in_dim.10
  38.0 19.6 %all_to_all.15.own = bf16[16,128,256]{2,1,0:T(8,128)(2,1)S(1)} all-to-all(bf16[16,128,256]{2,1,0:T(8,128)(2,1)S(1)} %broadcast_in_dim.10), channel_id=1, replica_groups=mesh['expert'=4,'shard_0'=4,'shard_1'=4,'shard_2'=2] {'shard_0','shard_1'}, dimensions={0} | all-to-all | bytes 2097152 | tf_op jit(solution)/shard_map/all_to_all | solution.py:295
  57.6 2.7 %collective-permute-done.4.partner = bf16[16,128,256]{2,1,0:T(8,128)(2,1)S(1)} collective-permute-done((bf16[16,128,256]{2,1,0:T(8,128)(2,1)S(1)}, bf16[16,128,256]{2,1,0:T(8,128)(2,1)S(1)}, u32[]{:S(2)}, u32[]{:S(2)}) %collective-permute-start.4) | collective-permute-done | bytes 1048608 | tf_op jit(solution)/shard_map/ppermute | solution.py:19
  60.3 7.9 %experts.1 = (bf16[128,4096]{1,0:T(8,128)(2,1)S(1)}, bf16[128,4096]{1,0:T(8,128)(2,1)S(1)}) custom-call(s32[4]{0:T(128)S(1)} %pad_add_fusion.place, s32[2,256]{1,0:T(2,128)S(1)} %reshape.36.ids, bf16[4096,128]{1,0:T(8,128)(2,1)S(1)} %copy-done.1, bf16[8,4096]{1,0:T(8,128)(2,1)S(1)} %bitcast.31, bf16[128,256]{1,0:T(8,128)(2,1)S(1)} %get-tuple-element.38.attn, ...), custom_call_target="tpu_custom_call" | custom-call | flops 5637144576 | bytes 22020096 | tf_op jit(solution)/shard_map/experts/pallas_call | solution.py:220
  68.2 0.2 collective-permute-start.5
  68.4 2.5 %collective-permute-done.5 = bf16[128,4096]{1,0:T(8,128)(2,1)S(1)} collective-permute-done((bf16[128,4096]{1,0:T(8,128)(2,1)S(1)}, bf16[128,4096]{1,0:T(8,128)(2,1)S(1)}, u32[]{:S(2)}, u32[]{:S(2)}) %collective-permute-start.5) | collective-permute-done | bytes 1048608 | tf_op jit(solution)/shard_map/ppermute | solution.py:19
  71.0 0.2 fusion.2
  71.2 20.5 %all_to_all.16 = bf16[16,8,4096]{2,1,0:T(8,128)(2,1)S(1)} all-to-all(bf16[16,8,4096]{2,1,0:T(8,128)(2,1)S(1)} %fusion.2), channel_id=1, replica_groups=mesh['expert'=4,'shard_0'=4,'shard_1'=4,'shard_2'=2] {'shard_0','shard_1'}, dimensions={0} | all-to-all | bytes 2097152 | tf_op jit(solution)/shard_map/all_to_all | solution.py:303
  91.8 0.1 reduce_sum.12
  91.9 2.4 %collective-permute-start.8 = (bf16[8,4096]{1,0:T(8,128)(2,1)S(1)}, bf16[8,4096]{1,0:T(8,128)(2,1)S(1)}, u32[]{:S(2)}, u32[]{:S(2)}) collective-permute-start(bf16[8,4096]{1,0:T(8,128)(2,1)S(1)} %reduce_sum.12), channel_id=1, source_target_pairs={{0,96},{32,0},{64,32},{96,64},{1,97},{33,1},{65,33},{97,65},{2,98}... | collective-permute-start | bytes 196616 | tf_op jit(solution)/shard_map/ppermute | solution.py:19
  94.3 1.5 %collective-permute-start.7 = (bf16[8,4096]{1,0:T(8,128)(2,1)S(1)}, bf16[8,4096]{1,0:T(8,128)(2,1)S(1)}, u32[]{:S(2)}, u32[]{:S(2)}) collective-permute-start(bf16[8,4096]{1,0:T(8,128)(2,1)S(1)} %reduce_sum.12), channel_id=1, source_target_pairs={{0,64},{32,96},{64,0},{96,32},{1,65},{33,97},{65,1},{97,33},{2,66}... | collective-permute-start | bytes 196616 | tf_op jit(solution)/shard_map/ppermute | solution.py:19
  95.9 0.4 collective-permute-done.8
  96.3 3.9 %collective-permute-done.7 = bf16[8,4096]{1,0:T(8,128)(2,1)S(1)} collective-permute-done((bf16[8,4096]{1,0:T(8,128)(2,1)S(1)}, bf16[8,4096]{1,0:T(8,128)(2,1)S(1)}, u32[]{:S(2)}, u32[]{:S(2)}) %collective-permute-start.7) | collective-permute-done | bytes 65568 | tf_op jit(solution)/shard_map/ppermute | solution.py:19
  100.1 1.2 %collective-permute-done.6 = bf16[8,4096]{1,0:T(8,128)(2,1)S(1)} collective-permute-done((bf16[8,4096]{1,0:T(8,128)(2,1)S(1)}, bf16[8,4096]{1,0:T(8,128)(2,1)S(1)}, u32[]{:S(2)}, u32[]{:S(2)}) %collective-permute-start.6) | collective-permute-done | bytes 65568 | tf_op jit(solution)/shard_map/ppermute | solution.py:19
  101.3 0.7 add_convert_fusion.1
  (24 shorter events, 0.1 us)
Async XLA Ops:
  0.0 22.3 %copy-start = (bf16[1024,128]{1,0:T(8,128)(2,1)S(1)}, bf16[1024,128]{1,0:T(8,128)(2,1)}, u32[]{:S(2)}) copy-start(bf16[1024,128]{1,0:T(8,128)(2,1)} %param.15) | copy-start | bytes 786436
  0.0 12.6 %copy-start.5 = (bf16[4096]{0:T(1024)(128)(2,1)S(1)}, bf16[4096]{0:T(1024)(128)(2,1)}, u32[]{:S(2)}) copy-start(bf16[4096]{0:T(1024)(128)(2,1)} %param.16) | copy-start | bytes 24580
  0.0 13.3 %copy-start.6 = (s32[256,2]{0,1:T(2,128)S(1)}, s32[256,2]{0,1:T(2,128)}, u32[]{:S(2)}) copy-start(s32[256,2]{0,1:T(2,128)} %param.18) | copy-start | bytes 6148
  4.4 17.6 %all-to-all-start = ((bf16[16,8,1280]{2,1,0:T(8,128)(2,1)}), bf16[16,8,1280]{2,1,0:T(8,128)(2,1)S(1)}, u32[]{:S(2)}, u32[]{:S(2)}) async-start(bf16[16,8,1280]{2,1,0:T(8,128)(2,1)} %attention.1), calls=%async_computation | async-start | bytes 655360 | tf_op jit(solution)/shard_map/all_to_all | solution.py:272
  22.2 1.7 %collective-permute-start = (bf16[128,1280]{0,1:T(8,128)(2,1)S(1)}, bf16[128,1280]{0,1:T(8,128)(2,1)S(1)}, u32[]{:S(2)}, u32[]{:S(2)}) collective-permute-start(bf16[128,1280]{0,1:T(8,128)(2,1)S(1)} %copy.18), channel_id=1, source_target_pairs={{0,1},{1,0},{2,3},{3,2},{4,5},{5,4},{6,7},{7,6},{8,9},{9,8},{10,11... | collective-permute-start | bytes 983048 | tf_op jit(solution)/shard_map/ppermute | solution.py:19
  24.2 4.6 %copy-start.3 = (bf16[128,256]{1,0:T(8,128)(2,1)}, bf16[128,256]{1,0:T(8,128)(2,1)S(1)}, u32[]{:S(2)}) copy-start(bf16[128,256]{1,0:T(8,128)(2,1)S(1)} %pad_maximum_fusion._) | copy-start | bytes 196612
  24.2 13.6 %collective-permute-start.3 = (bf16[128,256]{1,0:T(8,128)(2,1)S(1)}, bf16[128,256]{1,0:T(8,128)(2,1)S(1)}, u32[]{:S(2)}, u32[]{:S(2)}) collective-permute-start(bf16[128,256]{1,0:T(8,128)(2,1)S(1)} %pad_maximum_fusion._), channel_id=1, source_target_pairs={{0,96},{32,0},{64,32},{96,64},{1,97},{33,1},{65,33},{97,65},{2,98}... | collective-permute-start | bytes 196616 | tf_op jit(solution)/shard_map/ppermute | solution.py:19
  27.1 10.8 %collective-permute-start.2 = (bf16[128,256]{1,0:T(8,128)(2,1)S(1)}, bf16[128,256]{1,0:T(8,128)(2,1)S(1)}, u32[]{:S(2)}, u32[]{:S(2)}) collective-permute-start(bf16[128,256]{1,0:T(8,128)(2,1)S(1)} %pad_maximum_fusion._), channel_id=1, source_target_pairs={{0,64},{32,96},{64,0},{96,32},{1,65},{33,97},{65,1},{97,33},{2,66}... | collective-permute-start | bytes 196616 | tf_op jit(solution)/shard_map/ppermute | solution.py:19
  27.9 10.0 %collective-permute-start.1 = (bf16[128,256]{1,0:T(8,128)(2,1)S(1)}, bf16[128,256]{1,0:T(8,128)(2,1)S(1)}, u32[]{:S(2)}, u32[]{:S(2)}) collective-permute-start(bf16[128,256]{1,0:T(8,128)(2,1)S(1)} %pad_maximum_fusion._), channel_id=1, source_target_pairs={{0,32},{32,64},{64,96},{96,0},{1,33},{33,65},{65,97},{97,1},{2,34}... | collective-permute-start | bytes 196616 | tf_op jit(solution)/shard_map/ppermute | solution.py:19
  37.8 22.5 %copy-start.1 = (bf16[4096,128]{1,0:T(8,128)(2,1)S(1)}, bf16[4096,128]{1,0:T(8,128)(2,1)}, u32[]{:S(2)}) copy-start(bf16[4096,128]{1,0:T(8,128)(2,1)} %get-tuple-element.26.gain) | copy-start | bytes 3145732
  37.8 22.5 %copy-start.2 = (bf16[4096,8]{0,1:T(8,128)(2,1)S(1)}, bf16[4096,8]{0,1:T(8,128)(2,1)}, u32[]{:S(2)}) copy-start(bf16[4096,8]{0,1:T(8,128)(2,1)} %param.17) | copy-start | bytes 196612
  57.6 2.7 %collective-permute-start.4 = (bf16[16,128,256]{2,1,0:T(8,128)(2,1)S(1)}, bf16[16,128,256]{2,1,0:T(8,128)(2,1)S(1)}, u32[]{:S(2)}, u32[]{:S(2)}) collective-permute-start(bf16[16,128,256]{2,1,0:T(8,128)(2,1)S(1)} %all_to_all.15.own), channel_id=1, source_target_pairs={{0,1},{1,0},{2,3},{3,2},{4,5},{5,4},{6,7},{7,6},{8,9},{9,8},{10,11... | collective-permute-start | bytes 3145736 | tf_op jit(solution)/shard_map/ppermute | solution.py:19
  68.2 2.7 %collective-permute-start.5 = (bf16[128,4096]{1,0:T(8,128)(2,1)S(1)}, bf16[128,4096]{1,0:T(8,128)(2,1)S(1)}, u32[]{:S(2)}, u32[]{:S(2)}) collective-permute-start(bf16[128,4096]{1,0:T(8,128)(2,1)S(1)} %get-tuple-element.33), channel_id=1, source_target_pairs={{0,1},{1,0},{2,3},{3,2},{4,5},{5,4},{6,7},{7,6},{8,9},{9,8},{10,11... | collective-permute-start | bytes 3145736 | tf_op jit(solution)/shard_map/ppermute | solution.py:19
  71.2 30.1 %copy-start.4 = (bf16[8,4096]{1,0:T(8,128)(2,1)S(1)}, bf16[8,4096]{1,0:T(8,128)(2,1)}, u32[]{:S(2)}) copy-start(bf16[8,4096]{1,0:T(8,128)(2,1)} %hidden.1) | copy-start | bytes 196612
  91.9 4.3 %collective-permute-start.8 = (bf16[8,4096]{1,0:T(8,128)(2,1)S(1)}, bf16[8,4096]{1,0:T(8,128)(2,1)S(1)}, u32[]{:S(2)}, u32[]{:S(2)}) collective-permute-start(bf16[8,4096]{1,0:T(8,128)(2,1)S(1)} %reduce_sum.12), channel_id=1, source_target_pairs={{0,96},{32,0},{64,32},{96,64},{1,97},{33,1},{65,33},{97,65},{2,98}... | collective-permute-start | bytes 196616 | tf_op jit(solution)/shard_map/ppermute | solution.py:19
  94.3 5.8 %collective-permute-start.7 = (bf16[8,4096]{1,0:T(8,128)(2,1)S(1)}, bf16[8,4096]{1,0:T(8,128)(2,1)S(1)}, u32[]{:S(2)}, u32[]{:S(2)}) collective-permute-start(bf16[8,4096]{1,0:T(8,128)(2,1)S(1)} %reduce_sum.12), channel_id=1, source_target_pairs={{0,64},{32,96},{64,0},{96,32},{1,65},{33,97},{65,1},{97,33},{2,66}... | collective-permute-start | bytes 196616 | tf_op jit(solution)/shard_map/ppermute | solution.py:19
  95.9 5.5 %collective-permute-start.6 = (bf16[8,4096]{1,0:T(8,128)(2,1)S(1)}, bf16[8,4096]{1,0:T(8,128)(2,1)S(1)}, u32[]{:S(2)}, u32[]{:S(2)}) collective-permute-start(bf16[8,4096]{1,0:T(8,128)(2,1)S(1)} %reduce_sum.12), channel_id=1, source_target_pairs={{0,32},{32,64},{64,96},{96,0},{1,33},{33,65},{65,97},{97,1},{2,34}... | collective-permute-start | bytes 196616 | tf_op jit(solution)/shard_map/ppermute | solution.py:19

commit v5 on v4

--- a/solution.py
+++ b/solution.py
@@ -12,6 +12,8 @@
 PLANE = ("shard_0", "shard_1")
 F32 = jnp.float32
 BF16 = jnp.bfloat16
+BRING_GRANT = 40 * 1024 * 1024
+EXPERT_GRANT = 36 * 1024 * 1024
 
 
 def shifted(x, axis, by):
@@ -109,47 +111,76 @@
     )(queries.reshape(tokens * heads, size), hidden, keys, values)
 
 
-def bring_kernel(_, gains, gate, up, down, held, gain, sems):
-    units = gate.shape[0]
-    copies = [
-        pltpu.make_async_copy(source, held.at[pl.ds(n * units, units)], sems.at[n])
-        for n, source in enumerate((gate, up, down))
-    ]
-    for copy in copies:
-        copy.start()
+def spread_kernel(_, gains, gain):
     lanes = gain.shape[1]
     for at in range(0, gain.shape[0], lanes):
         row = gains[:, at : at + lanes].astype(F32)
         gain[at : at + lanes, :] = jnp.broadcast_to(row, (lanes, lanes)).T.astype(BF16)
-    for copy in copies:
-        copy.wait()
-
-
-def brought_in(after, gains, *weights):
-    size = sum(w.size for w in weights)
-    rows, width = weights[0].shape
-    hbm = pl.BlockSpec(memory_space=pl.ANY)
+
+
+def spread(after, gains):
+    size = gains.shape[1]
     vmem = pl.BlockSpec(memory_space=pltpu.VMEM)
     return pl.pallas_call(
+        spread_kernel,
+        out_shape=jax.ShapeDtypeStruct((size, 128), BF16),
+        in_specs=[pl.BlockSpec(memory_space=pl.ANY), vmem],
+        out_specs=vmem,
+        compiler_params=pltpu.CompilerParams(vmem_limit_bytes=4 * 1024 * 1024),
+        cost_estimate=pl.CostEstimate(
+            flops=20000 * size, bytes_accessed=256 * size, transcendentals=0
+        ),
+        name="spread",
+    )(after, gains)
+
+
+def bring_kernel(_, source, target, sem):
+    copy = pltpu.make_async_copy(source, target, sem)
+    copy.start()
+    copy.wait()
+
+
+def brought_in(after, weights):
+    hbm = pl.BlockSpec(memory_space=pl.ANY)
+    return pl.pallas_call(
         bring_kernel,
-        out_shape=(pltpu.VMEM((3 * rows, width), BF16), jax.ShapeDtypeStruct((width, 128), BF16)),
-        in_specs=[hbm, vmem] + [hbm] * len(weights),
-        out_specs=(vmem, vmem),
-        scratch_shapes=[pltpu.SemaphoreType.DMA((3,))],
-        compiler_params=pltpu.CompilerParams(vmem_limit_bytes=36 * 1024 * 1024),
-        cost_estimate=pl.CostEstimate(flops=80 * size, bytes_accessed=4 * size, transcendentals=0),
+        out_shape=pltpu.VMEM(weights.shape, weights.dtype),
+        in_specs=[hbm, hbm],
+        out_specs=pl.BlockSpec(memory_space=pltpu.VMEM),
+        scratch_shapes=[pltpu.SemaphoreType.DMA],
+        compiler_params=pltpu.CompilerParams(vmem_limit_bytes=BRING_GRANT),
+        cost_estimate=pl.CostEstimate(
+            flops=80 * weights.size, bytes_accessed=4 * weights.size, transcendentals=0
+        ),
         name="bring",
-    )(after, gains, *weights)
+    )(after, weights)
 
 
 def expert_kernel(
-    place, ids, gain, router, attn, held, own, partner, send, keep, mixed, hidden_t, act
+    place, ids, gain, router, attn, gate, own, partner, up_hbm, down_hbm,
+    send, keep, mixed, hidden_t, act, up, down, sems,
 ):
     core, shard, first_expert, adds = (place[n] for n in range(4))
-    units, width = held.shape[0] // 3, held.shape[1]
+    units, width = gate.shape
     half_units = units // 2
     chips, block, tokens = own.shape
     half = tokens // 2
+    step = width // 2
+
+    def up_copy(m):
+        rows = pl.ds(pl.multiple_of(m * half_units, half_units), half_units)
+        return pltpu.make_async_copy(up_hbm.at[rows], up.at[rows], sems.at[m])
+
+    def down_copy(n):
+        columns = pl.ds(pl.multiple_of(n * step, step), step)
+        return pltpu.make_async_copy(
+            down_hbm.at[:, columns], down.at[:, columns], sems.at[2 + n]
+        )
+
+    for m in range(2):
+        up_copy(m).start()
+    for n in range(2):
+        down_copy(n).start()
 
     def norm_block(j, squares):
         for mine, part in ((core, own), (1 - core, partner)):
@@ -178,63 +209,72 @@
     weight_second = 1.0 / (1.0 + jnp.exp(a - b))
 
     for m in range(2):
-        for n in range(2):
-            rows = pl.ds((2 * n + m) * half_units, half_units)
-            hidden_t[m, n] = jnp.dot(held[rows, :], mixed[...], preferred_element_type=F32)
+        rows = pl.ds(m * half_units, half_units)
+        hidden_t[0, m] = jnp.dot(gate[rows, :], mixed[...], preferred_element_type=F32)
+
+    def up_part(m, carry):
+        up_copy(m).wait()
+        rows = pl.ds(pl.multiple_of(m * half_units, half_units), half_units)
+        hidden_t[1, m] = jnp.dot(up[rows, :], mixed[...], preferred_element_type=F32)
+        return carry
+
+    lax.fori_loop(0, 2, up_part, 0)
+    for m in range(2):
         expert = first_expert + m
         routed = jnp.where(first == expert, weight_first, 0.0) + jnp.where(
             second == expert, weight_second, 0.0
         )
-        gated = hidden_t[m, 0] * scale
-        upward = hidden_t[m, 1] * scale
+        gated = hidden_t[0, m] * scale
+        upward = hidden_t[1, m] * scale
         value = gated / (1.0 + jnp.exp(-gated)) * upward * routed
         act[m] = value.T.astype(BF16)
 
-    step = width // 2
-
     def down_part(n, carry):
+        down_copy(n).wait()
         columns = pl.ds(pl.multiple_of(n * step, step), step)
         total = jnp.dot(
-            act[0], held[pl.ds(2 * units, half_units), columns], preferred_element_type=F32
+            act[0], down[pl.ds(0, half_units), columns], preferred_element_type=F32
         ) + jnp.dot(
-            act[1],
-            held[pl.ds(2 * units + half_units, half_units), columns],
-            preferred_element_type=F32,
+            act[1], down[pl.ds(half_units, half_units), columns], preferred_element_type=F32
         )
         keep[:, columns] = total[:half].astype(BF16)
         send[:, columns] = total[half:].astype(BF16)
         return carry
 
-    lax.fori_loop(0, width // step, down_part, 0)
+    lax.fori_loop(0, 2, down_part, 0)
     rows = attn[...].astype(F32).T * adds.astype(F32)
     columns = pl.ds(pl.multiple_of(shard * block, block), block)
     keep[:, columns] = (keep[:, columns].astype(F32) + rows[:half]).astype(BF16)
     send[:, columns] = (send[:, columns].astype(F32) + rows[half:]).astype(BF16)
 
 
-def experts(place, ids, gain, router, attn, held, own, partner):
-    units, width = held.shape[0] // 3, held.shape[1]
+def experts(place, ids, gain, router, attn, gate, own, partner, up, down):
+    units, width = gate.shape
     tokens = attn.shape[1]
     vmem = pl.BlockSpec(memory_space=pltpu.VMEM)
+    hbm = pl.BlockSpec(memory_space=pl.ANY)
     half = jax.ShapeDtypeStruct((tokens // 2, width), BF16)
     return pl.pallas_call(
         expert_kernel,
         out_shape=(half, half),
-        in_specs=[pl.BlockSpec(memory_space=pltpu.SMEM)] + [vmem] * 7,
+        in_specs=[pl.BlockSpec(memory_space=pltpu.SMEM)] + [vmem] * 7 + [hbm] * 2,
         out_specs=(vmem, vmem),
         scratch_shapes=[
             pltpu.VMEM((width, tokens), BF16),
             pltpu.VMEM((2, 2, units // 2, tokens), F32),
             pltpu.VMEM((2, tokens, units // 2), BF16),
+            pltpu.VMEM((units, width), BF16),
+            pltpu.VMEM((units, width), BF16),
+            pltpu.SemaphoreType.DMA((4,)),
         ],
-        compiler_params=pltpu.CompilerParams(vmem_limit_bytes=12 * 1024 * 1024),
+        compiler_params=pltpu.CompilerParams(vmem_limit_bytes=EXPERT_GRANT),
         cost_estimate=pl.CostEstimate(
             flops=6 * tokens * units * width,
             bytes_accessed=6 * units * width,
             transcendentals=2 * units * tokens,
         ),
         name="experts",
-    )(place, ids, gain, router, attn, held, own, partner)
+    )(place, ids, gain, router, attn, gate, own, partner, up, down)
 
 
 def on_device(
@@ -283,26 +323,34 @@
 
     part = jnp.concatenate([project(arrived), project(passed)], axis=1)
     hidden_t = jnp.concatenate([my_columns(arrived), my_columns(passed)], axis=0).T
-    held, gain = brought_in(
-        part,
-        norm_gain[None, :],
-        gate_weight.transpose(0, 2, 1).reshape(units, width),
-        up_weight.transpose(0, 2, 1).reshape(units, width),
-        down_weight.reshape(units, width),
-    )
-    attn_out, (hidden_t, held, gain) = sum_over_groups(part, (hidden_t, held, gain))
+    attn_out, (hidden_t,) = sum_over_groups(part, (hidden_t,))
     stream = (attn_out + hidden_t.astype(F32)).astype(BF16)
     own = lax.all_to_all(
         jnp.broadcast_to(stream[None], (chips, block, tokens)), PLANE, 0, 0, tiled=True
     )
+    gain = spread(stream, norm_gain[None, :])
+    own, gain = lax.optimization_barrier((own, gain))
     partner = shifted(own, "shard_2", 1)
+    gate = brought_in(own, gate_weight.transpose(0, 2, 1).reshape(units, width))
+    partner, gate = lax.optimization_barrier((partner, gate))
     send, keep = experts(
-        place, ids, gain, router.T, attn_out.astype(BF16), held, own, partner
+        place,
+        ids,
+        gain,
+        router.T,
+        attn_out.astype(BF16),
+        gate,
+        own,
+        partner,
+        up_weight.transpose(0, 2, 1).reshape(units, width),
+        down_weight.reshape(units, width),
     )
     pair = (keep.astype(F32) + shifted(send, "shard_2", 1).astype(F32)).astype(BF16)
     parts = lax.all_to_all(pair.reshape(chips, count_local, width), PLANE, 0, 0, tiled=True)
+    residual, _ = lax.optimization_barrier((hidden, pair))
+    parts, residual = lax.optimization_barrier((parts, residual.astype(F32)))
     reduced = parts.astype(F32).sum(axis=0).astype(BF16)
-    return (hidden.astype(F32) + sum_over_groups(reduced)).astype(BF16)
+    return (residual + sum_over_groups(reduced)).astype(BF16)
 
 
 def solution(mesh):

time: 102 us -> 104 us (1.020)
  blocking collectives: 40.2 us -> 0 us
  waiting for transfers between devices: 20.4 us -> 55.6 us
  starting transfers between devices: 16.9 us -> 26.5 us
  Pallas kernels: 21.3 us -> 16.5 us
    all_to_all x2 -> x0, blocking collectives: 40.2 us -> none  [the longest x1 20.5 us: on_device(): lax.all_to_all(pair.reshape(chips, count_local, width), PLANE, 0, 0, tile...]
    all_to_all x0 -> x2, waiting for transfers between devices: none -> 35.3 us  [the longest x1 19.1 us: on_device(): lax.all_to_all(pair.reshape(chips, count_local, width), PLANE, 0, 0, tile...]
    all_to_all x0 -> x2, starting transfers between devices: none -> 7.31 us  [the longest x1 3.65 us: on_device(): lax.all_to_all(jnp.broadcast_to(stream[None], (chips, block, tokens)), PL...]
    pallas_call x1 -> x2, Pallas kernels: 8.99 us -> 3.46 us  [the longest x1 3.12 us: brought_in(): pl.pallas_call(bring_kernel, out_shape=pltpu.VMEM(weights.shape, weights....]
    ppermute x9, starting transfers between devices: 8.76 us -> 11 us  [shifted(): return lax.ppermute(x, axis, [(i, (i + by) % size) for i in range(size)])]
    convert_element_type x2 -> x4, other arithmetic: 0.73 us -> 1.96 us  [the longest x1 1.23 us: on_device(): (keep.astype(F32) + shifted(send, 'shard_2', 1).astype(F32)).astype(BF16)]
  transfers between devices with their start and end apart: 10 -> 12, of which waited for: 7 -> 9; matrix products, arithmetic and copies ran while one was open for 1% -> 1% of each run, Pallas kernels for 9% -> 3%
where the time goes in v5:
time: 104 us; the launch traced here: 103 us
  waiting for transfers between devices  55.6 us (53%)
  starting transfers between devices  26.5 us (25%)
  Pallas kernels  16.5 us (16%)
  other arithmetic  2.22 us (2%)
  local copies, waits for them, and re-layouts  1.52 us (1%)
    all_to_all x1, waiting for transfers between devices, on_device(): lax.all_to_all(pair.reshape(chips, count_local, width), PLANE, 0, 0, tile...  19.1 us
    all_to_all x1, waiting for transfers between devices, on_device(): lax.all_to_all(jnp.broadcast_to(stream[None], (chips, block, tokens)), PL...  16.1 us
    ppermute x9, waiting for transfers between devices, shifted(): return lax.ppermute(x, axis, [(i, (i + by) % size) for i in range(size)])  11.3 us
    ppermute x9, starting transfers between devices, shifted(): return lax.ppermute(x, axis, [(i, (i + by) % size) for i in range(size)])  11 us
    all_to_all x1, waiting for transfers between devices, on_device(): lax.all_to_all(pieces, PLANE, 0, 0, tiled=True).reshape(tokens // 2, -1)  9.06 us
    pallas_call x1, Pallas kernels, experts(): pl.pallas_call(expert_kernel, out_shape=(half, half), in_specs=[pl.BlockS...  8.62 us
    all_to_all x1, starting transfers between devices, on_device(): lax.all_to_all(pieces, PLANE, 0, 0, tiled=True).reshape(tokens // 2, -1)  8.17 us
    pallas_call x1, Pallas kernels, attention(): pl.pallas_call(attention_kernel, out_shape=jax.ShapeDtypeStruct((chips, t...  4.43 us
  transfers between devices with their start and end apart: 12, of which 9 were waited for; matrix products, arithmetic and copies ran while one was open for 1% of the time, Pallas kernels for 3%

profile of v5, /device:TPU:0, one launch (start us, length us, event | category | flops | bytes accessed | tf_op | source)
XLA Modules:
  0.0 103.2 jit_solution(14631811185271467913)
XLA Ops:
  0.0 4.4 %attention.1 = bf16[16,8,1280]{2,1,0:T(8,128)(2,1)} custom-call(bf16[64,128]{1,0:T(8,128)(2,1)} %bitcast.39, bf16[8,4096]{1,0:T(8,128)(2,1)} %hidden.1, bf16[8,1024,128]{2,1,0:T(8,128)(2,1)} %bitcast.36, bf16[8,1024,128]{2,1,0:T(8,128)(2,1)} %bitcast.37), custom_call_target="tpu_custom_call" | custom-call | flops 33554432 | bytes 4194304 | tf_op jit(solution)/shard_map/attention/pallas_call | solution.py:92
  4.4 8.2 %all-to-all-start = ((bf16[16,8,1280]{2,1,0:T(8,128)(2,1)}), bf16[16,8,1280]{2,1,0:T(8,128)(2,1)S(1)}, u32[]{:S(2)}, u32[]{:S(2)}) async-start(bf16[16,8,1280]{2,1,0:T(8,128)(2,1)} %attention.1), calls=%async_computation | async-start | bytes 655360 | tf_op jit(solution)/shard_map/all_to_all | solution.py:312
  12.7 0.1 reshape.35
  12.8 0.1 reshape.36.ids
  12.9 9.1 %all-to-all-done = bf16[16,8,1280]{2,1,0:T(8,128)(2,1)S(1)} async-done(((bf16[16,8,1280]{2,1,0:T(8,128)(2,1)}), bf16[16,8,1280]{2,1,0:T(8,128)(2,1)S(1)}, u32[]{:S(2)}, u32[]{:S(2)}) %all-to-all-start) | async-done | bytes 327712 | tf_op jit(solution)/shard_map/all_to_all | solution.py:312
  22.0 0.2 copy.18
  22.3 0.3 fusion
  22.6 1.3 %collective-permute-done = bf16[128,1280]{0,1:T(8,128)(2,1)S(1)} collective-permute-done((bf16[128,1280]{0,1:T(8,128)(2,1)S(1)}, bf16[128,1280]{0,1:T(8,128)(2,1)S(1)}, u32[]{:S(2)}, u32[]{:S(2)}) %collective-permute-start) | collective-permute-done | bytes 327712 | tf_op jit(solution)/shard_map/ppermute | solution.py:21
  23.9 0.3 fusion.1
  24.2 3.1 %collective-permute-start.2 = (bf16[128,256]{1,0:T(8,128)(2,1)S(1)}, bf16[128,256]{1,0:T(8,128)(2,1)S(1)}, u32[]{:S(2)}, u32[]{:S(2)}) collective-permute-start(bf16[128,256]{1,0:T(8,128)(2,1)S(1)} %pad_maximum_fusion), channel_id=1, source_target_pairs={{0,64},{32,96},{64,0},{96,32},{1,65},{33,97},{65,1},{97,33},{2,66}... | collective-permute-start | bytes 196616 | tf_op jit(solution)/shard_map/ppermute | solution.py:21
  27.3 0.6 collective-permute-start.1
  27.9 2.6 %collective-permute-start.3 = (bf16[128,256]{1,0:T(8,128)(2,1)S(1)}, bf16[128,256]{1,0:T(8,128)(2,1)S(1)}, u32[]{:S(2)}, u32[]{:S(2)}) collective-permute-start(bf16[128,256]{1,0:T(8,128)(2,1)S(1)} %pad_maximum_fusion), channel_id=1, source_target_pairs={{0,96},{32,0},{64,32},{96,64},{1,97},{33,1},{65,33},{97,65},{2,98}... | collective-permute-start | bytes 196616 | tf_op jit(solution)/shard_map/ppermute | solution.py:21
  30.6 2.2 %collective-permute-done.1 = bf16[128,256]{1,0:T(8,128)(2,1)S(1)} collective-permute-done((bf16[128,256]{1,0:T(8,128)(2,1)S(1)}, bf16[128,256]{1,0:T(8,128)(2,1)S(1)}, u32[]{:S(2)}, u32[]{:S(2)}) %collective-permute-start.1) | collective-permute-done | bytes 65568 | tf_op jit(solution)/shard_map/ppermute | solution.py:21
  32.9 1.1 %broadcast_in_dim.4 = bf16[16,128,256]{2,1,0:T(8,128)(2,1)} broadcast(bf16[128,256]{1,0:T(8,128)(2,1)S(1)} %get-tuple-element.44._), dimensions={1,2} | broadcast | bytes 1114112 | tf_op jit(solution)/shard_map/broadcast_in_dim | solution.py:329
  34.0 3.7 %all-to-all-start.1 = ((bf16[16,128,256]{2,1,0:T(8,128)(2,1)}), bf16[16,128,256]{2,1,0:T(8,128)(2,1)S(1)}, u32[]{:S(2)}, u32[]{:S(2)}) async-start(bf16[16,128,256]{2,1,0:T(8,128)(2,1)} %broadcast_in_dim.4), calls=%async_computation.1 | async-start | bytes 2097152 | tf_op jit(solution)/shard_map/all_to_all | solution.py:328
  37.6 0.3 spread.1.gain
  38.0 16.1 %all-to-all-done.1._.own = bf16[16,128,256]{2,1,0:T(8,128)(2,1)S(1)} async-done(((bf16[16,128,256]{2,1,0:T(8,128)(2,1)}), bf16[16,128,256]{2,1,0:T(8,128)(2,1)S(1)}, u32[]{:S(2)}, u32[]{:S(2)}) %all-to-all-start.1) | async-done | bytes 1048608 | tf_op jit(solution)/shard_map/all_to_all | solution.py:328
  54.1 3.1 %bring.1.gate = bf16[896,4096]{1,0:T(8,128)(2,1)S(1)} custom-call(bf16[16,128,256]{2,1,0:T(8,128)(2,1)S(1)} %all-to-all-done.1._.own, bf16[896,4096]{1,0:T(8,128)(2,1)} %bitcast.31), custom_call_target="tpu_custom_call" | custom-call | flops 293601280 | bytes 14680064 | tf_op jit(solution)/shard_map/bring/pallas_call | solution.py:145
  57.3 8.6 %experts.1 = (bf16[128,4096]{1,0:T(8,128)(2,1)S(1)}, bf16[128,4096]{1,0:T(8,128)(2,1)S(1)}) custom-call(s32[4]{0:T(128)S(1)} %pad_add_fusion.place, s32[2,256]{1,0:T(2,128)S(1)} %reshape.36.ids, bf16[4096,128]{1,0:T(8,128)(2,1)S(1)} %spread.1.gain, bf16[8,4096]{1,0:T(8,128)(2,1)S(1)} %bitcast.30, bf16[128,256]{1,0:T(8,128)(2,1)S(1)} %get-tuple-element.43.attn, ...), custom_call_target="tpu_custom_call" | custom-call | flops 5637144576 | bytes 22020096 | tf_op jit(solution)/shard_map/experts/pallas_call | solution.py:257
  65.9 0.6 collective-permute-start.5
  66.5 2.3 %collective-permute-done.5 = bf16[128,4096]{1,0:T(8,128)(2,1)S(1)} collective-permute-done((bf16[128,4096]{1,0:T(8,128)(2,1)S(1)}, bf16[128,4096]{1,0:T(8,128)(2,1)S(1)}, u32[]{:S(2)}, u32[]{:S(2)}) %collective-permute-start.5) | collective-permute-done | bytes 1048608 | tf_op jit(solution)/shard_map/ppermute | solution.py:21
  68.8 1.2 %add_convert_fusion = bf16[128,4096]{1,0:T(8,128)(2,1)} fusion(bf16[128,4096]{1,0:T(8,128)(2,1)S(1)} %collective-permute-done.5, bf16[128,4096]{1,0:T(8,128)(2,1)S(1)} %get-tuple-element.35), kind=kLoop, calls=%fused_computation | loop fusion | flops 2097152 | bytes 3145728 | tf_op jit(solution)/shard_map/convert_element_type | solution.py:348
  70.0 3.7 %all-to-all-start.2 = ((bf16[16,8,4096]{2,1,0:T(8,128)(2,1)}), bf16[16,8,4096]{2,1,0:T(8,128)(2,1)S(1)}, u32[]{:S(2)}, u32[]{:S(2)}) async-start(bf16[16,8,4096]{2,1,0:T(8,128)(2,1)} %bitcast.18), calls=%async_computation.2 | async-start | bytes 2097152 | tf_op jit(solution)/shard_map/all_to_all | solution.py:349
  73.7 19.1 %all-to-all-done.2 = bf16[16,8,4096]{2,1,0:T(8,128)(2,1)S(1)} async-done(((bf16[16,8,4096]{2,1,0:T(8,128)(2,1)}), bf16[16,8,4096]{2,1,0:T(8,128)(2,1)S(1)}, u32[]{:S(2)}, u32[]{:S(2)}) %all-to-all-start.2) | async-done | bytes 1048608 | tf_op jit(solution)/shard_map/all_to_all | solution.py:349
  92.8 0.1 reduce_sum.12
  93.0 3.1 %collective-permute-start.8 = (bf16[8,4096]{1,0:T(8,128)(2,1)S(1)}, bf16[8,4096]{1,0:T(8,128)(2,1)S(1)}, u32[]{:S(2)}, u32[]{:S(2)}) collective-permute-start(bf16[8,4096]{1,0:T(8,128)(2,1)S(1)} %reduce_sum.12), channel_id=1, source_target_pairs={{0,96},{32,0},{64,32},{96,64},{1,97},{33,1},{65,33},{97,65},{2,98}... | collective-permute-start | bytes 196616 | tf_op jit(solution)/shard_map/ppermute | solution.py:21
  96.0 0.4 collective-permute-start.7
  96.5 0.5 collective-permute-start.6
  97.0 1.6 %collective-permute-done.8 = bf16[8,4096]{1,0:T(8,128)(2,1)S(1)} collective-permute-done((bf16[8,4096]{1,0:T(8,128)(2,1)S(1)}, bf16[8,4096]{1,0:T(8,128)(2,1)S(1)}, u32[]{:S(2)}, u32[]{:S(2)}) %collective-permute-start.8) | collective-permute-done | bytes 65568 | tf_op jit(solution)/shard_map/ppermute | solution.py:21
  98.5 3.3 %collective-permute-done.7 = bf16[8,4096]{1,0:T(8,128)(2,1)S(1)} collective-permute-done((bf16[8,4096]{1,0:T(8,128)(2,1)S(1)}, bf16[8,4096]{1,0:T(8,128)(2,1)S(1)}, u32[]{:S(2)}, u32[]{:S(2)}) %collective-permute-start.7) | collective-permute-done | bytes 65568 | tf_op jit(solution)/shard_map/ppermute | solution.py:21
  101.8 0.7 collective-permute-done.6
  102.5 0.7 add_convert_fusion.1
  (24 shorter events, 0.3 us)
Async XLA Ops:
  0.0 22.3 %copy-start = (bf16[1024,128]{1,0:T(8,128)(2,1)S(1)}, bf16[1024,128]{1,0:T(8,128)(2,1)}, u32[]{:S(2)}) copy-start(bf16[1024,128]{1,0:T(8,128)(2,1)} %param.15) | copy-start | bytes 786436
  0.0 12.6 %copy-start.4 = (s32[256,2]{0,1:T(2,128)S(1)}, s32[256,2]{0,1:T(2,128)}, u32[]{:S(2)}) copy-start(s32[256,2]{0,1:T(2,128)} %param.18) | copy-start | bytes 6148
  4.4 17.6 %all-to-all-start = ((bf16[16,8,1280]{2,1,0:T(8,128)(2,1)}), bf16[16,8,1280]{2,1,0:T(8,128)(2,1)S(1)}, u32[]{:S(2)}, u32[]{:S(2)}) async-start(bf16[16,8,1280]{2,1,0:T(8,128)(2,1)} %attention.1), calls=%async_computation | async-start | bytes 655360 | tf_op jit(solution)/shard_map/all_to_all | solution.py:312
  22.2 1.7 %collective-permute-start = (bf16[128,1280]{0,1:T(8,128)(2,1)S(1)}, bf16[128,1280]{0,1:T(8,128)(2,1)S(1)}, u32[]{:S(2)}, u32[]{:S(2)}) collective-permute-start(bf16[128,1280]{0,1:T(8,128)(2,1)S(1)} %copy.18), channel_id=1, source_target_pairs={{0,1},{1,0},{2,3},{3,2},{4,5},{5,4},{6,7},{7,6},{8,9},{9,8},{10,11... | collective-permute-start | bytes 983048 | tf_op jit(solution)/shard_map/ppermute | solution.py:21
  24.2 13.4 %copy-start.3 = (bf16[4096]{0:T(1024)(128)(2,1)S(1)}, bf16[4096]{0:T(1024)(128)(2,1)}, u32[]{:S(2)}) copy-start(bf16[4096]{0:T(1024)(128)(2,1)} %param.16) | copy-start | bytes 24580
  24.2 6.4 %collective-permute-start.2 = (bf16[128,256]{1,0:T(8,128)(2,1)S(1)}, bf16[128,256]{1,0:T(8,128)(2,1)S(1)}, u32[]{:S(2)}, u32[]{:S(2)}) collective-permute-start(bf16[128,256]{1,0:T(8,128)(2,1)S(1)} %pad_maximum_fusion), channel_id=1, source_target_pairs={{0,64},{32,96},{64,0},{96,32},{1,65},{33,97},{65,1},{97,33},{2,66}... | collective-permute-start | bytes 196616 | tf_op jit(solution)/shard_map/ppermute | solution.py:21
  27.3 5.5 %collective-permute-start.1 = (bf16[128,256]{1,0:T(8,128)(2,1)S(1)}, bf16[128,256]{1,0:T(8,128)(2,1)S(1)}, u32[]{:S(2)}, u32[]{:S(2)}) collective-permute-start(bf16[128,256]{1,0:T(8,128)(2,1)S(1)} %pad_maximum_fusion), channel_id=1, source_target_pairs={{0,32},{32,64},{64,96},{96,0},{1,33},{33,65},{65,97},{97,1},{2,34}... | collective-permute-start | bytes 196616 | tf_op jit(solution)/shard_map/ppermute | solution.py:21
  27.9 4.9 %collective-permute-start.3 = (bf16[128,256]{1,0:T(8,128)(2,1)S(1)}, bf16[128,256]{1,0:T(8,128)(2,1)S(1)}, u32[]{:S(2)}, u32[]{:S(2)}) collective-permute-start(bf16[128,256]{1,0:T(8,128)(2,1)S(1)} %pad_maximum_fusion), channel_id=1, source_target_pairs={{0,96},{32,0},{64,32},{96,64},{1,97},{33,1},{65,33},{97,65},{2,98}... | collective-permute-start | bytes 196616 | tf_op jit(solution)/shard_map/ppermute | solution.py:21
  34.0 20.2 %all-to-all-start.1 = ((bf16[16,128,256]{2,1,0:T(8,128)(2,1)}), bf16[16,128,256]{2,1,0:T(8,128)(2,1)S(1)}, u32[]{:S(2)}, u32[]{:S(2)}) async-start(bf16[16,128,256]{2,1,0:T(8,128)(2,1)} %broadcast_in_dim.4), calls=%async_computation.1 | async-start | bytes 2097152 | tf_op jit(solution)/shard_map/all_to_all | solution.py:328
  54.1 3.1 %collective-permute-start.4 = (bf16[16,128,256]{2,1,0:T(8,128)(2,1)S(1)}, bf16[16,128,256]{2,1,0:T(8,128)(2,1)S(1)}, u32[]{:S(2)}, u32[]{:S(2)}) collective-permute-start(bf16[16,128,256]{2,1,0:T(8,128)(2,1)S(1)} %all-to-all-done.1._.own), channel_id=1, source_target_pairs={{0,1},{1,0},{2,3},{3,2},{4,5},{5,4},{6,7},{7,6},{8,9},{9,8},{10,11... | collective-permute-start | bytes 3145736 | tf_op jit(solution)/shard_map/ppermute | solution.py:21
  54.1 3.1 %copy-start.1 = (bf16[4096,8]{0,1:T(8,128)(2,1)S(1)}, bf16[4096,8]{0,1:T(8,128)(2,1)}, u32[]{:S(2)}) copy-start(bf16[4096,8]{0,1:T(8,128)(2,1)} %param.17) | copy-start | bytes 196612
  65.9 2.9 %collective-permute-start.5 = (bf16[128,4096]{1,0:T(8,128)(2,1)S(1)}, bf16[128,4096]{1,0:T(8,128)(2,1)S(1)}, u32[]{:S(2)}, u32[]{:S(2)}) collective-permute-start(bf16[128,4096]{1,0:T(8,128)(2,1)S(1)} %get-tuple-element.36), channel_id=1, source_target_pairs={{0,1},{1,0},{2,3},{3,2},{4,5},{5,4},{6,7},{7,6},{8,9},{9,8},{10,11... | collective-permute-start | bytes 3145736 | tf_op jit(solution)/shard_map/ppermute | solution.py:21
  68.8 4.9 %copy-start.2 = (bf16[8,4096]{1,0:T(8,128)(2,1)S(1)}, bf16[8,4096]{1,0:T(8,128)(2,1)}, u32[]{:S(2)}) copy-start(bf16[8,4096]{1,0:T(8,128)(2,1)} %hidden.1) | copy-start | bytes 196612
  70.0 22.8 %all-to-all-start.2 = ((bf16[16,8,4096]{2,1,0:T(8,128)(2,1)}), bf16[16,8,4096]{2,1,0:T(8,128)(2,1)S(1)}, u32[]{:S(2)}, u32[]{:S(2)}) async-start(bf16[16,8,4096]{2,1,0:T(8,128)(2,1)} %bitcast.18), calls=%async_computation.2 | async-start | bytes 2097152 | tf_op jit(solution)/shard_map/all_to_all | solution.py:349
  93.0 5.6 %collective-permute-start.8 = (bf16[8,4096]{1,0:T(8,128)(2,1)S(1)}, bf16[8,4096]{1,0:T(8,128)(2,1)S(1)}, u32[]{:S(2)}, u32[]{:S(2)}) collective-permute-start(bf16[8,4096]{1,0:T(8,128)(2,1)S(1)} %reduce_sum.12), channel_id=1, source_target_pairs={{0,96},{32,0},{64,32},{96,64},{1,97},{33,1},{65,33},{97,65},{2,98}... | collective-permute-start | bytes 196616 | tf_op jit(solution)/shard_map/ppermute | solution.py:21
  96.0 5.8 %collective-permute-start.7 = (bf16[8,4096]{1,0:T(8,128)(2,1)S(1)}, bf16[8,4096]{1,0:T(8,128)(2,1)S(1)}, u32[]{:S(2)}, u32[]{:S(2)}) collective-permute-start(bf16[8,4096]{1,0:T(8,128)(2,1)S(1)} %reduce_sum.12), channel_id=1, source_target_pairs={{0,64},{32,96},{64,0},{96,32},{1,65},{33,97},{65,1},{97,33},{2,66}... | collective-permute-start | bytes 196616 | tf_op jit(solution)/shard_map/ppermute | solution.py:21
  96.5 6.0 %collective-permute-start.6 = (bf16[8,4096]{1,0:T(8,128)(2,1)S(1)}, bf16[8,4096]{1,0:T(8,128)(2,1)S(1)}, u32[]{:S(2)}, u32[]{:S(2)}) collective-permute-start(bf16[8,4096]{1,0:T(8,128)(2,1)S(1)} %reduce_sum.12), channel_id=1, source_target_pairs={{0,32},{32,64},{64,96},{96,0},{1,33},{33,65},{65,97},{97,1},{2,34}... | collective-permute-start | bytes 196616 | tf_op jit(solution)/shard_map/ppermute | solution.py:21

commit v6 on v5

--- a/solution.py
+++ b/solution.py
@@ -323,13 +323,12 @@
 
     part = jnp.concatenate([project(arrived), project(passed)], axis=1)
     hidden_t = jnp.concatenate([my_columns(arrived), my_columns(passed)], axis=0).T
-    attn_out, (hidden_t,) = sum_over_groups(part, (hidden_t,))
+    gain = spread(part, norm_gain[None, :])
+    attn_out, (hidden_t, gain) = sum_over_groups(part, (hidden_t, gain))
     stream = (attn_out + hidden_t.astype(F32)).astype(BF16)
     own = lax.all_to_all(
         jnp.broadcast_to(stream[None], (chips, block, tokens)), PLANE, 0, 0, tiled=True
     )
-    gain = spread(stream, norm_gain[None, :])
-    own, gain = lax.optimization_barrier((own, gain))
     partner = shifted(own, "shard_2", 1)
     gate = brought_in(own, gate_weight.transpose(0, 2, 1).reshape(units, width))
     partner, gate = lax.optimization_barrier((partner, gate))
@@ -347,10 +346,8 @@
     )
     pair = (keep.astype(F32) + shifted(send, "shard_2", 1).astype(F32)).astype(BF16)
     parts = lax.all_to_all(pair.reshape(chips, count_local, width), PLANE, 0, 0, tiled=True)
-    residual, _ = lax.optimization_barrier((hidden, pair))
-    parts, residual = lax.optimization_barrier((parts, residual.astype(F32)))
     reduced = parts.astype(F32).sum(axis=0).astype(BF16)
-    return (residual + sum_over_groups(reduced)).astype(BF16)
+    return (hidden.astype(F32) + sum_over_groups(reduced)).astype(BF16)
 
 
 def solution(mesh):

time: 104 us -> 97.8 us (0.940)
  blocking collectives: 0 us -> 40.5 us
  waiting for transfers between devices: 55.6 us -> 22 us
  starting transfers between devices: 26.5 us -> 15.9 us
    all_to_all x0 -> x2, blocking collectives: none -> 40.5 us  [the longest x1 20.8 us: on_device(): lax.all_to_all(pair.reshape(chips, count_local, width), PLANE, 0, 0, tile...]
    all_to_all x2 -> x0, waiting for transfers between devices: 35.3 us -> none  [the longest x1 19.1 us: on_device(): lax.all_to_all(pair.reshape(chips, count_local, width), PLANE, 0, 0, tile...]
    all_to_all x2 -> x0, starting transfers between devices: 7.31 us -> none  [the longest x1 3.65 us: on_device(): lax.all_to_all(jnp.broadcast_to(stream[None], (chips, block, tokens)), PL...]
    ppermute x9, starting transfers between devices: 11 us -> 7.7 us  [shifted(): return lax.ppermute(x, axis, [(i, (i + by) % size) for i in range(size)])]
    ppermute x9, waiting for transfers between devices: 11.3 us -> 13 us  [shifted(): return lax.ppermute(x, axis, [(i, (i + by) % size) for i in range(size)])]
    convert_element_type x4 -> x2, other arithmetic: 1.96 us -> 0.73 us  [the longest x1 0.67 us: on_device(): return (hidden.astype(F32) + sum_over_groups(reduced)).astype(BF16)]
  transfers between devices with their start and end apart: 12 -> 10, of which waited for: 9 -> 9; matrix products, arithmetic and copies ran while one was open for 1% -> 1% of each run, Pallas kernels for 3% -> 4%
where the time goes in v6:
time: 97.8 us; the launch traced here: 97.5 us
  blocking collectives  40.5 us (41%)
  waiting for transfers between devices  22 us (22%)
  Pallas kernels  16.6 us (17%)
  starting transfers between devices  15.9 us (16%)
  other arithmetic  1.23 us (1%)
    all_to_all x1, blocking collectives, on_device(): lax.all_to_all(pair.reshape(chips, count_local, width), PLANE, 0, 0, tile...  20.8 us
    all_to_all x1, blocking collectives, on_device(): lax.all_to_all(jnp.broadcast_to(stream[None], (chips, block, tokens)), PL...  19.7 us
    ppermute x9, waiting for transfers between devices, shifted(): return lax.ppermute(x, axis, [(i, (i + by) % size) for i in range(size)])  13 us
    all_to_all x1, waiting for transfers between devices, on_device(): lax.all_to_all(pieces, PLANE, 0, 0, tiled=True).reshape(tokens // 2, -1)  9.03 us
    pallas_call x1, Pallas kernels, experts(): pl.pallas_call(expert_kernel, out_shape=(half, half), in_specs=[pl.BlockS...  8.73 us
    all_to_all x1, starting transfers between devices, on_device(): lax.all_to_all(pieces, PLANE, 0, 0, tiled=True).reshape(tokens // 2, -1)  8.18 us
    ppermute x9, starting transfers between devices, shifted(): return lax.ppermute(x, axis, [(i, (i + by) % size) for i in range(size)])  7.7 us
    pallas_call x1, Pallas kernels, attention(): pl.pallas_call(attention_kernel, out_shape=jax.ShapeDtypeStruct((chips, t...  4.41 us
  transfers between devices with their start and end apart: 10, of which 9 were waited for; matrix products, arithmetic and copies ran while one was open for 1% of the time, Pallas kernels for 4%

profile of v6, /device:TPU:0, one launch (start us, length us, event | category | flops | bytes accessed | tf_op | source)
XLA Modules:
  0.0 97.5 jit_solution(13841563195979788574)
XLA Ops:
  0.0 4.4 %attention.1 = bf16[16,8,1280]{2,1,0:T(8,128)(2,1)} custom-call(bf16[64,128]{1,0:T(8,128)(2,1)} %bitcast.40, bf16[8,4096]{1,0:T(8,128)(2,1)} %hidden.1, bf16[8,1024,128]{2,1,0:T(8,128)(2,1)} %bitcast.37, bf16[8,1024,128]{2,1,0:T(8,128)(2,1)} %bitcast.38), custom_call_target="tpu_custom_call" | custom-call | flops 33554432 | bytes 4194304 | tf_op jit(solution)/shard_map/attention/pallas_call | solution.py:92
  4.4 8.2 %all-to-all-start = ((bf16[16,8,1280]{2,1,0:T(8,128)(2,1)}), bf16[16,8,1280]{2,1,0:T(8,128)(2,1)S(1)}, u32[]{:S(2)}, u32[]{:S(2)}) async-start(bf16[16,8,1280]{2,1,0:T(8,128)(2,1)} %attention.1), calls=%async_computation | async-start | bytes 655360 | tf_op jit(solution)/shard_map/all_to_all | solution.py:312
  12.7 0.1 reshape.35
  12.8 0.1 reshape.36.ids
  13.0 9.0 %all-to-all-done = bf16[16,8,1280]{2,1,0:T(8,128)(2,1)S(1)} async-done(((bf16[16,8,1280]{2,1,0:T(8,128)(2,1)}), bf16[16,8,1280]{2,1,0:T(8,128)(2,1)S(1)}, u32[]{:S(2)}, u32[]{:S(2)}) %all-to-all-start) | async-done | bytes 327712 | tf_op jit(solution)/shard_map/all_to_all | solution.py:312
  22.0 0.2 copy.18
  22.3 0.3 fusion
  22.6 1.3 %collective-permute-done = bf16[128,1280]{0,1:T(8,128)(2,1)S(1)} collective-permute-done((bf16[128,1280]{0,1:T(8,128)(2,1)S(1)}, bf16[128,1280]{0,1:T(8,128)(2,1)S(1)}, u32[]{:S(2)}, u32[]{:S(2)}) %collective-permute-start) | collective-permute-done | bytes 327712 | tf_op jit(solution)/shard_map/ppermute | solution.py:21
  23.9 0.3 fusion.1
  24.2 2.8 %collective-permute-start.3 = (bf16[128,256]{1,0:T(8,128)(2,1)S(1)}, bf16[128,256]{1,0:T(8,128)(2,1)S(1)}, u32[]{:S(2)}, u32[]{:S(2)}) collective-permute-start(bf16[128,256]{1,0:T(8,128)(2,1)S(1)} %pad_maximum_fusion._), channel_id=1, source_target_pairs={{0,96},{32,0},{64,32},{96,64},{1,97},{33,1},{65,33},{97,65},{2,98}... | collective-permute-start | bytes 196616 | tf_op jit(solution)/shard_map/ppermute | solution.py:21
  27.0 0.8 collective-permute-start.2
  27.9 0.9 collective-permute-start.1
  28.7 0.3 spread.1.gain
  29.1 1.1 %collective-permute-done.3 = bf16[128,256]{1,0:T(8,128)(2,1)S(1)} collective-permute-done((bf16[128,256]{1,0:T(8,128)(2,1)S(1)}, bf16[128,256]{1,0:T(8,128)(2,1)S(1)}, u32[]{:S(2)}, u32[]{:S(2)}) %collective-permute-start.3) | collective-permute-done | bytes 65568 | tf_op jit(solution)/shard_map/ppermute | solution.py:21
  30.3 2.8 %collective-permute-done.2 = bf16[128,256]{1,0:T(8,128)(2,1)S(1)} collective-permute-done((bf16[128,256]{1,0:T(8,128)(2,1)S(1)}, bf16[128,256]{1,0:T(8,128)(2,1)S(1)}, u32[]{:S(2)}, u32[]{:S(2)}) %collective-permute-start.2) | collective-permute-done | bytes 65568 | tf_op jit(solution)/shard_map/ppermute | solution.py:21
  33.1 0.7 collective-permute-done.1
  33.9 0.1 broadcast_in_dim.10
  34.0 19.7 %all_to_all.15._.own = bf16[16,128,256]{2,1,0:T(8,128)(2,1)S(1)} all-to-all(bf16[16,128,256]{2,1,0:T(8,128)(2,1)S(1)} %broadcast_in_dim.10), channel_id=1, replica_groups=mesh['expert'=4,'shard_0'=4,'shard_1'=4,'shard_2'=2] {'shard_0','shard_1'}, dimensions={0} | all-to-all | bytes 2097152 | tf_op jit(solution)/shard_map/all_to_all | solution.py:329
  53.6 3.1 %bring.1.gate = bf16[896,4096]{1,0:T(8,128)(2,1)S(1)} custom-call(bf16[16,128,256]{2,1,0:T(8,128)(2,1)S(1)} %all_to_all.15._.own, bf16[896,4096]{1,0:T(8,128)(2,1)} %bitcast.32), custom_call_target="tpu_custom_call" | custom-call | flops 293601280 | bytes 14680064 | tf_op jit(solution)/shard_map/bring/pallas_call | solution.py:145
  56.8 8.7 %experts.1 = (bf16[128,4096]{1,0:T(8,128)(2,1)S(1)}, bf16[128,4096]{1,0:T(8,128)(2,1)S(1)}) custom-call(s32[4]{0:T(128)S(1)} %pad_add_fusion.place, s32[2,256]{1,0:T(2,128)S(1)} %reshape.36.ids, bf16[4096,128]{1,0:T(8,128)(2,1)S(1)} %spread.1.gain, bf16[8,4096]{1,0:T(8,128)(2,1)S(1)} %bitcast.31, bf16[128,256]{1,0:T(8,128)(2,1)S(1)} %get-tuple-element.36.attn, ...), custom_call_target="tpu_custom_call" | custom-call | flops 5637144576 | bytes 22020096 | tf_op jit(solution)/shard_map/experts/pallas_call | solution.py:257
  65.5 0.6 collective-permute-start.5
  66.1 2.3 %collective-permute-done.5 = bf16[128,4096]{1,0:T(8,128)(2,1)S(1)} collective-permute-done((bf16[128,4096]{1,0:T(8,128)(2,1)S(1)}, bf16[128,4096]{1,0:T(8,128)(2,1)S(1)}, u32[]{:S(2)}, u32[]{:S(2)}) %collective-permute-start.5) | collective-permute-done | bytes 1048608 | tf_op jit(solution)/shard_map/ppermute | solution.py:21
  68.4 0.2 fusion.2
  68.7 20.8 %all_to_all.16 = bf16[16,8,4096]{2,1,0:T(8,128)(2,1)S(1)} all-to-all(bf16[16,8,4096]{2,1,0:T(8,128)(2,1)S(1)} %fusion.2), channel_id=1, replica_groups=mesh['expert'=4,'shard_0'=4,'shard_1'=4,'shard_2'=2] {'shard_0','shard_1'}, dimensions={0} | all-to-all | bytes 2097152 | tf_op jit(solution)/shard_map/all_to_all | solution.py:348
  89.5 0.1 reduce_sum.12
  89.6 0.2 collective-permute-start.8
  89.8 1.0 %collective-permute-start.7 = (bf16[8,4096]{1,0:T(8,128)(2,1)S(1)}, bf16[8,4096]{1,0:T(8,128)(2,1)S(1)}, u32[]{:S(2)}, u32[]{:S(2)}) collective-permute-start(bf16[8,4096]{1,0:T(8,128)(2,1)S(1)} %reduce_sum.12), channel_id=1, source_target_pairs={{0,64},{32,96},{64,0},{96,32},{1,65},{33,97},{65,1},{97,33},{2,66}... | collective-permute-start | bytes 196616 | tf_op jit(solution)/shard_map/ppermute | solution.py:21
  90.8 1.3 %collective-permute-start.6 = (bf16[8,4096]{1,0:T(8,128)(2,1)S(1)}, bf16[8,4096]{1,0:T(8,128)(2,1)S(1)}, u32[]{:S(2)}, u32[]{:S(2)}) collective-permute-start(bf16[8,4096]{1,0:T(8,128)(2,1)S(1)} %reduce_sum.12), channel_id=1, source_target_pairs={{0,32},{32,64},{64,96},{96,0},{1,33},{33,65},{65,97},{97,1},{2,34}... | collective-permute-start | bytes 196616 | tf_op jit(solution)/shard_map/ppermute | solution.py:21
  92.1 1.8 %collective-permute-done.8 = bf16[8,4096]{1,0:T(8,128)(2,1)S(1)} collective-permute-done((bf16[8,4096]{1,0:T(8,128)(2,1)S(1)}, bf16[8,4096]{1,0:T(8,128)(2,1)S(1)}, u32[]{:S(2)}, u32[]{:S(2)}) %collective-permute-start.8) | collective-permute-done | bytes 65568 | tf_op jit(solution)/shard_map/ppermute | solution.py:21
  94.0 2.4 %collective-permute-done.7 = bf16[8,4096]{1,0:T(8,128)(2,1)S(1)} collective-permute-done((bf16[8,4096]{1,0:T(8,128)(2,1)S(1)}, bf16[8,4096]{1,0:T(8,128)(2,1)S(1)}, u32[]{:S(2)}, u32[]{:S(2)}) %collective-permute-start.7) | collective-permute-done | bytes 65568 | tf_op jit(solution)/shard_map/ppermute | solution.py:21
  96.3 0.5 collective-permute-done.6
  96.8 0.7 add_convert_fusion.1
  (21 shorter events, 0.3 us)
Async XLA Ops:
  0.0 22.3 %copy-start = (bf16[1024,128]{1,0:T(8,128)(2,1)S(1)}, bf16[1024,128]{1,0:T(8,128)(2,1)}, u32[]{:S(2)}) copy-start(bf16[1024,128]{1,0:T(8,128)(2,1)} %param.15) | copy-start | bytes 786436
  0.0 12.6 %copy-start.3 = (bf16[4096]{0:T(1024)(128)(2,1)S(1)}, bf16[4096]{0:T(1024)(128)(2,1)}, u32[]{:S(2)}) copy-start(bf16[4096]{0:T(1024)(128)(2,1)} %param.16) | copy-start | bytes 24580
  0.0 12.7 %copy-start.4 = (s32[256,2]{0,1:T(2,128)S(1)}, s32[256,2]{0,1:T(2,128)}, u32[]{:S(2)}) copy-start(s32[256,2]{0,1:T(2,128)} %param.18) | copy-start | bytes 6148
  4.4 17.6 %all-to-all-start = ((bf16[16,8,1280]{2,1,0:T(8,128)(2,1)}), bf16[16,8,1280]{2,1,0:T(8,128)(2,1)S(1)}, u32[]{:S(2)}, u32[]{:S(2)}) async-start(bf16[16,8,1280]{2,1,0:T(8,128)(2,1)} %attention.1), calls=%async_computation | async-start | bytes 655360 | tf_op jit(solution)/shard_map/all_to_all | solution.py:312
  22.2 1.7 %collective-permute-start = (bf16[128,1280]{0,1:T(8,128)(2,1)S(1)}, bf16[128,1280]{0,1:T(8,128)(2,1)S(1)}, u32[]{:S(2)}, u32[]{:S(2)}) collective-permute-start(bf16[128,1280]{0,1:T(8,128)(2,1)S(1)} %copy.18), channel_id=1, source_target_pairs={{0,1},{1,0},{2,3},{3,2},{4,5},{5,4},{6,7},{7,6},{8,9},{9,8},{10,11... | collective-permute-start | bytes 983048 | tf_op jit(solution)/shard_map/ppermute | solution.py:21
  24.2 6.0 %collective-permute-start.3 = (bf16[128,256]{1,0:T(8,128)(2,1)S(1)}, bf16[128,256]{1,0:T(8,128)(2,1)S(1)}, u32[]{:S(2)}, u32[]{:S(2)}) collective-permute-start(bf16[128,256]{1,0:T(8,128)(2,1)S(1)} %pad_maximum_fusion._), channel_id=1, source_target_pairs={{0,96},{32,0},{64,32},{96,64},{1,97},{33,1},{65,33},{97,65},{2,98}... | collective-permute-start | bytes 196616 | tf_op jit(solution)/shard_map/ppermute | solution.py:21
  27.0 6.1 %collective-permute-start.2 = (bf16[128,256]{1,0:T(8,128)(2,1)S(1)}, bf16[128,256]{1,0:T(8,128)(2,1)S(1)}, u32[]{:S(2)}, u32[]{:S(2)}) collective-permute-start(bf16[128,256]{1,0:T(8,128)(2,1)S(1)} %pad_maximum_fusion._), channel_id=1, source_target_pairs={{0,64},{32,96},{64,0},{96,32},{1,65},{33,97},{65,1},{97,33},{2,66}... | collective-permute-start | bytes 196616 | tf_op jit(solution)/shard_map/ppermute | solution.py:21
  27.9 6.0 %collective-permute-start.1 = (bf16[128,256]{1,0:T(8,128)(2,1)S(1)}, bf16[128,256]{1,0:T(8,128)(2,1)S(1)}, u32[]{:S(2)}, u32[]{:S(2)}) collective-permute-start(bf16[128,256]{1,0:T(8,128)(2,1)S(1)} %pad_maximum_fusion._), channel_id=1, source_target_pairs={{0,32},{32,64},{64,96},{96,0},{1,33},{33,65},{65,97},{97,1},{2,34}... | collective-permute-start | bytes 196616 | tf_op jit(solution)/shard_map/ppermute | solution.py:21
  53.6 3.1 %collective-permute-start.4 = (bf16[16,128,256]{2,1,0:T(8,128)(2,1)S(1)}, bf16[16,128,256]{2,1,0:T(8,128)(2,1)S(1)}, u32[]{:S(2)}, u32[]{:S(2)}) collective-permute-start(bf16[16,128,256]{2,1,0:T(8,128)(2,1)S(1)} %all_to_all.15._.own), channel_id=1, source_target_pairs={{0,1},{1,0},{2,3},{3,2},{4,5},{5,4},{6,7},{7,6},{8,9},{9,8},{10,11... | collective-permute-start | bytes 3145736 | tf_op jit(solution)/shard_map/ppermute | solution.py:21
  53.6 3.1 %copy-start.1 = (bf16[4096,8]{0,1:T(8,128)(2,1)S(1)}, bf16[4096,8]{0,1:T(8,128)(2,1)}, u32[]{:S(2)}) copy-start(bf16[4096,8]{0,1:T(8,128)(2,1)} %param.17) | copy-start | bytes 196612
  65.5 2.9 %collective-permute-start.5 = (bf16[128,4096]{1,0:T(8,128)(2,1)S(1)}, bf16[128,4096]{1,0:T(8,128)(2,1)S(1)}, u32[]{:S(2)}, u32[]{:S(2)}) collective-permute-start(bf16[128,4096]{1,0:T(8,128)(2,1)S(1)} %get-tuple-element.31), channel_id=1, source_target_pairs={{0,1},{1,0},{2,3},{3,2},{4,5},{5,4},{6,7},{7,6},{8,9},{9,8},{10,11... | collective-permute-start | bytes 3145736 | tf_op jit(solution)/shard_map/ppermute | solution.py:21
  68.7 28.2 %copy-start.2 = (bf16[8,4096]{1,0:T(8,128)(2,1)S(1)}, bf16[8,4096]{1,0:T(8,128)(2,1)}, u32[]{:S(2)}) copy-start(bf16[8,4096]{1,0:T(8,128)(2,1)} %hidden.1) | copy-start | bytes 196612
  89.6 4.3 %collective-permute-start.8 = (bf16[8,4096]{1,0:T(8,128)(2,1)S(1)}, bf16[8,4096]{1,0:T(8,128)(2,1)S(1)}, u32[]{:S(2)}, u32[]{:S(2)}) collective-permute-start(bf16[8,4096]{1,0:T(8,128)(2,1)S(1)} %reduce_sum.12), channel_id=1, source_target_pairs={{0,96},{32,0},{64,32},{96,64},{1,97},{33,1},{65,33},{97,65},{2,98}... | collective-permute-start | bytes 196616 | tf_op jit(solution)/shard_map/ppermute | solution.py:21
  89.8 6.5 %collective-permute-start.7 = (bf16[8,4096]{1,0:T(8,128)(2,1)S(1)}, bf16[8,4096]{1,0:T(8,128)(2,1)S(1)}, u32[]{:S(2)}, u32[]{:S(2)}) collective-permute-start(bf16[8,4096]{1,0:T(8,128)(2,1)S(1)} %reduce_sum.12), channel_id=1, source_target_pairs={{0,64},{32,96},{64,0},{96,32},{1,65},{33,97},{65,1},{97,33},{2,66}... | collective-permute-start | bytes 196616 | tf_op jit(solution)/shard_map/ppermute | solution.py:21
  90.8 6.0 %collective-permute-start.6 = (bf16[8,4096]{1,0:T(8,128)(2,1)S(1)}, bf16[8,4096]{1,0:T(8,128)(2,1)S(1)}, u32[]{:S(2)}, u32[]{:S(2)}) collective-permute-start(bf16[8,4096]{1,0:T(8,128)(2,1)S(1)} %reduce_sum.12), channel_id=1, source_target_pairs={{0,32},{32,64},{64,96},{96,0},{1,33},{33,65},{65,97},{97,1},{2,34}... | collective-permute-start | bytes 196616 | tf_op jit(solution)/shard_map/ppermute | solution.py:21

commit v7 on v6

--- a/solution.py
+++ b/solution.py
@@ -324,14 +324,13 @@
     part = jnp.concatenate([project(arrived), project(passed)], axis=1)
     hidden_t = jnp.concatenate([my_columns(arrived), my_columns(passed)], axis=0).T
     gain = spread(part, norm_gain[None, :])
-    attn_out, (hidden_t, gain) = sum_over_groups(part, (hidden_t, gain))
+    gate = brought_in(part, gate_weight.transpose(0, 2, 1).reshape(units, width))
+    attn_out, (hidden_t, gain, gate) = sum_over_groups(part, (hidden_t, gain, gate))
     stream = (attn_out + hidden_t.astype(F32)).astype(BF16)
     own = lax.all_to_all(
         jnp.broadcast_to(stream[None], (chips, block, tokens)), PLANE, 0, 0, tiled=True
     )
     partner = shifted(own, "shard_2", 1)
-    gate = brought_in(own, gate_weight.transpose(0, 2, 1).reshape(units, width))
-    partner, gate = lax.optimization_barrier((partner, gate))
     send, keep = experts(
         place,
         ids,

time: 97.8 us -> 97.4 us (level)
  no operation moved by 1% of the time
where the time goes in v7:
time: 97.4 us; the launch traced here: 97.1 us
  blocking collectives  40.2 us (41%)
  waiting for transfers between devices  22.3 us (23%)
  Pallas kernels  16.6 us (17%)
  starting transfers between devices  15.5 us (16%)
  other arithmetic  1.23 us (1%)
    all_to_all x1, blocking collectives, on_device(): lax.all_to_all(pair.reshape(chips, count_local, width), PLANE, 0, 0, tile...  20.5 us
    all_to_all x1, blocking collectives, on_device(): lax.all_to_all(jnp.broadcast_to(stream[None], (chips, block, tokens)), PL...  19.7 us
    ppermute x9, waiting for transfers between devices, shifted(): return lax.ppermute(x, axis, [(i, (i + by) % size) for i in range(size)])  13.3 us
    all_to_all x1, waiting for transfers between devices, on_device(): lax.all_to_all(pieces, PLANE, 0, 0, tiled=True).reshape(tokens // 2, -1)  9.03 us
    pallas_call x1, Pallas kernels, experts(): pl.pallas_call(expert_kernel, out_shape=(half, half), in_specs=[pl.BlockS...  8.72 us
    all_to_all x1, starting transfers between devices, on_device(): lax.all_to_all(pieces, PLANE, 0, 0, tiled=True).reshape(tokens // 2, -1)  8.18 us
    ppermute x9, starting transfers between devices, shifted(): return lax.ppermute(x, axis, [(i, (i + by) % size) for i in range(size)])  7.34 us
    pallas_call x1, Pallas kernels, attention(): pl.pallas_call(attention_kernel, out_shape=jax.ShapeDtypeStruct((chips, t...  4.41 us
  transfers between devices with their start and end apart: 10, of which 9 were waited for; matrix products, arithmetic and copies ran while one was open for 1% of the time, Pallas kernels for 4%

profile of v7, /device:TPU:0, one launch (start us, length us, event | category | flops | bytes accessed | tf_op | source)
XLA Modules:
  0.0 97.1 jit_solution(4824889244978797023)
XLA Ops:
  0.0 4.4 %attention.1 = bf16[16,8,1280]{2,1,0:T(8,128)(2,1)} custom-call(bf16[64,128]{1,0:T(8,128)(2,1)} %bitcast.40, bf16[8,4096]{1,0:T(8,128)(2,1)} %hidden.1, bf16[8,1024,128]{2,1,0:T(8,128)(2,1)} %bitcast.37, bf16[8,1024,128]{2,1,0:T(8,128)(2,1)} %bitcast.38), custom_call_target="tpu_custom_call" | custom-call | flops 33554432 | bytes 4194304 | tf_op jit(solution)/shard_map/attention/pallas_call | solution.py:92
  4.4 8.2 %all-to-all-start = ((bf16[16,8,1280]{2,1,0:T(8,128)(2,1)}), bf16[16,8,1280]{2,1,0:T(8,128)(2,1)S(1)}, u32[]{:S(2)}, u32[]{:S(2)}) async-start(bf16[16,8,1280]{2,1,0:T(8,128)(2,1)} %attention.1), calls=%async_computation | async-start | bytes 655360 | tf_op jit(solution)/shard_map/all_to_all | solution.py:312
  12.7 0.1 reshape.35
  12.8 0.1 reshape.36.ids
  13.0 9.0 %all-to-all-done = bf16[16,8,1280]{2,1,0:T(8,128)(2,1)S(1)} async-done(((bf16[16,8,1280]{2,1,0:T(8,128)(2,1)}), bf16[16,8,1280]{2,1,0:T(8,128)(2,1)S(1)}, u32[]{:S(2)}, u32[]{:S(2)}) %all-to-all-start) | async-done | bytes 327712 | tf_op jit(solution)/shard_map/all_to_all | solution.py:312
  22.0 0.2 copy.18
  22.3 0.3 fusion
  22.6 1.3 %collective-permute-done = bf16[128,1280]{0,1:T(8,128)(2,1)S(1)} collective-permute-done((bf16[128,1280]{0,1:T(8,128)(2,1)S(1)}, bf16[128,1280]{0,1:T(8,128)(2,1)S(1)}, u32[]{:S(2)}, u32[]{:S(2)}) %collective-permute-start) | collective-permute-done | bytes 327712 | tf_op jit(solution)/shard_map/ppermute | solution.py:21
  23.9 0.3 fusion.1
  24.2 2.8 %collective-permute-start.3 = (bf16[128,256]{1,0:T(8,128)(2,1)S(1)}, bf16[128,256]{1,0:T(8,128)(2,1)S(1)}, u32[]{:S(2)}, u32[]{:S(2)}) collective-permute-start(bf16[128,256]{1,0:T(8,128)(2,1)S(1)} %pad_maximum_fusion._), channel_id=1, source_target_pairs={{0,96},{32,0},{64,32},{96,64},{1,97},{33,1},{65,33},{97,65},{2,98}... | collective-permute-start | bytes 196616 | tf_op jit(solution)/shard_map/ppermute | solution.py:21
  27.0 0.8 collective-permute-start.2
  27.9 0.9 collective-permute-start.1
  28.8 0.3 spread.1.gain
  29.1 3.1 %bring.1.gate = bf16[896,4096]{1,0:T(8,128)(2,1)S(1)} custom-call(bf16[128,256]{1,0:T(8,128)(2,1)S(1)} %pad_maximum_fusion._, bf16[896,4096]{1,0:T(8,128)(2,1)} %bitcast.32), custom_call_target="tpu_custom_call" | custom-call | flops 293601280 | bytes 14680064 | tf_op jit(solution)/shard_map/bring/pallas_call | solution.py:145
  32.2 0.9 collective-permute-done.2
  33.1 0.7 collective-permute-done.1
  33.9 0.1 broadcast_in_dim.10
  34.0 19.7 %all_to_all.15.own = bf16[16,128,256]{2,1,0:T(8,128)(2,1)S(1)} all-to-all(bf16[16,128,256]{2,1,0:T(8,128)(2,1)S(1)} %broadcast_in_dim.10), channel_id=1, replica_groups=mesh['expert'=4,'shard_0'=4,'shard_1'=4,'shard_2'=2] {'shard_0','shard_1'}, dimensions={0} | all-to-all | bytes 2097152 | tf_op jit(solution)/shard_map/all_to_all | solution.py:330
  53.6 2.7 %collective-permute-done.4.partner = bf16[16,128,256]{2,1,0:T(8,128)(2,1)S(1)} collective-permute-done((bf16[16,128,256]{2,1,0:T(8,128)(2,1)S(1)}, bf16[16,128,256]{2,1,0:T(8,128)(2,1)S(1)}, u32[]{:S(2)}, u32[]{:S(2)}) %collective-permute-start.4) | collective-permute-done | bytes 1048608 | tf_op jit(solution)/shard_map/ppermute | solution.py:21
  56.3 8.7 %experts.1 = (bf16[128,4096]{1,0:T(8,128)(2,1)S(1)}, bf16[128,4096]{1,0:T(8,128)(2,1)S(1)}) custom-call(s32[4]{0:T(128)S(1)} %pad_add_fusion.place, s32[2,256]{1,0:T(2,128)S(1)} %reshape.36.ids, bf16[4096,128]{1,0:T(8,128)(2,1)S(1)} %spread.1.gain, bf16[8,4096]{1,0:T(8,128)(2,1)S(1)} %bitcast.31, bf16[128,256]{1,0:T(8,128)(2,1)S(1)} %get-tuple-element.34.attn, ...), custom_call_target="tpu_custom_call" | custom-call | flops 5637144576 | bytes 22020096 | tf_op jit(solution)/shard_map/experts/pallas_call | solution.py:257
  65.0 0.2 collective-permute-start.5
  65.3 2.5 %collective-permute-done.5 = bf16[128,4096]{1,0:T(8,128)(2,1)S(1)} collective-permute-done((bf16[128,4096]{1,0:T(8,128)(2,1)S(1)}, bf16[128,4096]{1,0:T(8,128)(2,1)S(1)}, u32[]{:S(2)}, u32[]{:S(2)}) %collective-permute-start.5) | collective-permute-done | bytes 1048608 | tf_op jit(solution)/shard_map/ppermute | solution.py:21
  67.8 0.2 fusion.2
  68.0 20.5 %all_to_all.16 = bf16[16,8,4096]{2,1,0:T(8,128)(2,1)S(1)} all-to-all(bf16[16,8,4096]{2,1,0:T(8,128)(2,1)S(1)} %fusion.2), channel_id=1, replica_groups=mesh['expert'=4,'shard_0'=4,'shard_1'=4,'shard_2'=2] {'shard_0','shard_1'}, dimensions={0} | all-to-all | bytes 2097152 | tf_op jit(solution)/shard_map/all_to_all | solution.py:347
  88.6 0.1 reduce_sum.12
  88.7 0.7 collective-permute-start.8
  89.4 1.5 %collective-permute-start.7 = (bf16[8,4096]{1,0:T(8,128)(2,1)S(1)}, bf16[8,4096]{1,0:T(8,128)(2,1)S(1)}, u32[]{:S(2)}, u32[]{:S(2)}) collective-permute-start(bf16[8,4096]{1,0:T(8,128)(2,1)S(1)} %reduce_sum.12), channel_id=1, source_target_pairs={{0,64},{32,96},{64,0},{96,32},{1,65},{33,97},{65,1},{97,33},{2,66}... | collective-permute-start | bytes 196616 | tf_op jit(solution)/shard_map/ppermute | solution.py:21
  90.9 0.3 collective-permute-start.6
  91.2 1.8 %collective-permute-done.8 = bf16[8,4096]{1,0:T(8,128)(2,1)S(1)} collective-permute-done((bf16[8,4096]{1,0:T(8,128)(2,1)S(1)}, bf16[8,4096]{1,0:T(8,128)(2,1)S(1)}, u32[]{:S(2)}, u32[]{:S(2)}) %collective-permute-start.8) | collective-permute-done | bytes 65568 | tf_op jit(solution)/shard_map/ppermute | solution.py:21
  93.0 2.1 %collective-permute-done.7 = bf16[8,4096]{1,0:T(8,128)(2,1)S(1)} collective-permute-done((bf16[8,4096]{1,0:T(8,128)(2,1)S(1)}, bf16[8,4096]{1,0:T(8,128)(2,1)S(1)}, u32[]{:S(2)}, u32[]{:S(2)}) %collective-permute-start.7) | collective-permute-done | bytes 65568 | tf_op jit(solution)/shard_map/ppermute | solution.py:21
  95.2 1.2 %collective-permute-done.6 = bf16[8,4096]{1,0:T(8,128)(2,1)S(1)} collective-permute-done((bf16[8,4096]{1,0:T(8,128)(2,1)S(1)}, bf16[8,4096]{1,0:T(8,128)(2,1)S(1)}, u32[]{:S(2)}, u32[]{:S(2)}) %collective-permute-start.6) | collective-permute-done | bytes 65568 | tf_op jit(solution)/shard_map/ppermute | solution.py:21
  96.4 0.7 add_convert_fusion.1
  (21 shorter events, 0.3 us)
Async XLA Ops:
  0.0 22.3 %copy-start = (bf16[1024,128]{1,0:T(8,128)(2,1)S(1)}, bf16[1024,128]{1,0:T(8,128)(2,1)}, u32[]{:S(2)}) copy-start(bf16[1024,128]{1,0:T(8,128)(2,1)} %param.15) | copy-start | bytes 786436
  0.0 12.6 %copy-start.3 = (bf16[4096]{0:T(1024)(128)(2,1)S(1)}, bf16[4096]{0:T(1024)(128)(2,1)}, u32[]{:S(2)}) copy-start(bf16[4096]{0:T(1024)(128)(2,1)} %param.16) | copy-start | bytes 24580
  0.0 12.7 %copy-start.4 = (s32[256,2]{0,1:T(2,128)S(1)}, s32[256,2]{0,1:T(2,128)}, u32[]{:S(2)}) copy-start(s32[256,2]{0,1:T(2,128)} %param.18) | copy-start | bytes 6148
  4.4 17.6 %all-to-all-start = ((bf16[16,8,1280]{2,1,0:T(8,128)(2,1)}), bf16[16,8,1280]{2,1,0:T(8,128)(2,1)S(1)}, u32[]{:S(2)}, u32[]{:S(2)}) async-start(bf16[16,8,1280]{2,1,0:T(8,128)(2,1)} %attention.1), calls=%async_computation | async-start | bytes 655360 | tf_op jit(solution)/shard_map/all_to_all | solution.py:312
  22.2 1.7 %collective-permute-start = (bf16[128,1280]{0,1:T(8,128)(2,1)S(1)}, bf16[128,1280]{0,1:T(8,128)(2,1)S(1)}, u32[]{:S(2)}, u32[]{:S(2)}) collective-permute-start(bf16[128,1280]{0,1:T(8,128)(2,1)S(1)} %copy.18), channel_id=1, source_target_pairs={{0,1},{1,0},{2,3},{3,2},{4,5},{5,4},{6,7},{7,6},{8,9},{9,8},{10,11... | collective-permute-start | bytes 983048 | tf_op jit(solution)/shard_map/ppermute | solution.py:21
  24.2 8.0 %collective-permute-start.3 = (bf16[128,256]{1,0:T(8,128)(2,1)S(1)}, bf16[128,256]{1,0:T(8,128)(2,1)S(1)}, u32[]{:S(2)}, u32[]{:S(2)}) collective-permute-start(bf16[128,256]{1,0:T(8,128)(2,1)S(1)} %pad_maximum_fusion._), channel_id=1, source_target_pairs={{0,96},{32,0},{64,32},{96,64},{1,97},{33,1},{65,33},{97,65},{2,98}... | collective-permute-start | bytes 196616 | tf_op jit(solution)/shard_map/ppermute | solution.py:21
  27.0 6.1 %collective-permute-start.2 = (bf16[128,256]{1,0:T(8,128)(2,1)S(1)}, bf16[128,256]{1,0:T(8,128)(2,1)S(1)}, u32[]{:S(2)}, u32[]{:S(2)}) collective-permute-start(bf16[128,256]{1,0:T(8,128)(2,1)S(1)} %pad_maximum_fusion._), channel_id=1, source_target_pairs={{0,64},{32,96},{64,0},{96,32},{1,65},{33,97},{65,1},{97,33},{2,66}... | collective-permute-start | bytes 196616 | tf_op jit(solution)/shard_map/ppermute | solution.py:21
  27.9 6.0 %collective-permute-start.1 = (bf16[128,256]{1,0:T(8,128)(2,1)S(1)}, bf16[128,256]{1,0:T(8,128)(2,1)S(1)}, u32[]{:S(2)}, u32[]{:S(2)}) collective-permute-start(bf16[128,256]{1,0:T(8,128)(2,1)S(1)} %pad_maximum_fusion._), channel_id=1, source_target_pairs={{0,32},{32,64},{64,96},{96,0},{1,33},{33,65},{65,97},{97,1},{2,34}... | collective-permute-start | bytes 196616 | tf_op jit(solution)/shard_map/ppermute | solution.py:21
  32.2 24.1 %copy-start.1 = (bf16[4096,8]{0,1:T(8,128)(2,1)S(1)}, bf16[4096,8]{0,1:T(8,128)(2,1)}, u32[]{:S(2)}) copy-start(bf16[4096,8]{0,1:T(8,128)(2,1)} %param.17) | copy-start | bytes 196612
  53.6 2.7 %collective-permute-start.4 = (bf16[16,128,256]{2,1,0:T(8,128)(2,1)S(1)}, bf16[16,128,256]{2,1,0:T(8,128)(2,1)S(1)}, u32[]{:S(2)}, u32[]{:S(2)}) collective-permute-start(bf16[16,128,256]{2,1,0:T(8,128)(2,1)S(1)} %all_to_all.15.own), channel_id=1, source_target_pairs={{0,1},{1,0},{2,3},{3,2},{4,5},{5,4},{6,7},{7,6},{8,9},{9,8},{10,11... | collective-permute-start | bytes 3145736 | tf_op jit(solution)/shard_map/ppermute | solution.py:21
  65.0 2.7 %collective-permute-start.5 = (bf16[128,4096]{1,0:T(8,128)(2,1)S(1)}, bf16[128,4096]{1,0:T(8,128)(2,1)S(1)}, u32[]{:S(2)}, u32[]{:S(2)}) collective-permute-start(bf16[128,4096]{1,0:T(8,128)(2,1)S(1)} %get-tuple-element.29), channel_id=1, source_target_pairs={{0,1},{1,0},{2,3},{3,2},{4,5},{5,4},{6,7},{7,6},{8,9},{9,8},{10,11... | collective-permute-start | bytes 3145736 | tf_op jit(solution)/shard_map/ppermute | solution.py:21
  68.0 28.4 %copy-start.2 = (bf16[8,4096]{1,0:T(8,128)(2,1)S(1)}, bf16[8,4096]{1,0:T(8,128)(2,1)}, u32[]{:S(2)}) copy-start(bf16[8,4096]{1,0:T(8,128)(2,1)} %hidden.1) | copy-start | bytes 196612
  88.7 4.3 %collective-permute-start.8 = (bf16[8,4096]{1,0:T(8,128)(2,1)S(1)}, bf16[8,4096]{1,0:T(8,128)(2,1)S(1)}, u32[]{:S(2)}, u32[]{:S(2)}) collective-permute-start(bf16[8,4096]{1,0:T(8,128)(2,1)S(1)} %reduce_sum.12), channel_id=1, source_target_pairs={{0,96},{32,0},{64,32},{96,64},{1,97},{33,1},{65,33},{97,65},{2,98}... | collective-permute-start | bytes 196616 | tf_op jit(solution)/shard_map/ppermute | solution.py:21
  89.4 5.8 %collective-permute-start.7 = (bf16[8,4096]{1,0:T(8,128)(2,1)S(1)}, bf16[8,4096]{1,0:T(8,128)(2,1)S(1)}, u32[]{:S(2)}, u32[]{:S(2)}) collective-permute-start(bf16[8,4096]{1,0:T(8,128)(2,1)S(1)} %reduce_sum.12), channel_id=1, source_target_pairs={{0,64},{32,96},{64,0},{96,32},{1,65},{33,97},{65,1},{97,33},{2,66}... | collective-permute-start | bytes 196616 | tf_op jit(solution)/shard_map/ppermute | solution.py:21
  90.9 5.5 %collective-permute-start.6 = (bf16[8,4096]{1,0:T(8,128)(2,1)S(1)}, bf16[8,4096]{1,0:T(8,128)(2,1)S(1)}, u32[]{:S(2)}, u32[]{:S(2)}) collective-permute-start(bf16[8,4096]{1,0:T(8,128)(2,1)S(1)} %reduce_sum.12), channel_id=1, source_target_pairs={{0,32},{32,64},{64,96},{96,0},{1,33},{33,65},{65,97},{97,1},{2,34}... | collective-permute-start | bytes 196616 | tf_op jit(solution)/shard_map/ppermute | solution.py:21
